TPU v7x, 256 devices: a whole 4x4x8 slice. The times are simulated.
256 devices in a mesh: row: 16 (over z_hi, x), col: 8 (over y, core), depth: 2 (over z_lo).
Axes of the slice: x: 4, y: 4, z: 8 (z_hi: 4, z_lo: 2; z = z_hi * 2 + z_lo), core: 2. Of those that a mesh axis runs over, the one named last changes fastest.
Arguments:
- volume: bfloat16 [32, 128, 16, 256], P('row', 'col', 'depth'), may hold values from -6 to 6
- first_kernel: bfloat16 [27, 256, 256], P(None, 'row'), may hold values from -0.078125 to 0.078125
- down_kernel: bfloat16 [8, 256, 512], replicated, may hold values from -0.125 to 0.125
- mid_kernel: bfloat16 [27, 512, 512], P(None, None, 'col'), may hold values from -0.0546875 to 0.0546875
- up_kernel: bfloat16 [8, 512, 256], replicated, may hold values from -0.25 to 0.25
- last_kernel: bfloat16 [27, 512, 256], P(None, 'row'), may hold values from -0.0546875 to 0.0546875
Outputs:
- decoded: bfloat16 [32, 128, 16, 256], P('row', 'col', 'depth')
All inputs are finite; a program needn't handle non-finite values.
Results may differ from a plain program's by a relative error of at most 0.0055.
Values may be sent and summed in bfloat16 or wider, within the bound.
No kernel may reach another device: no remote copies, remote signals or barrier semaphores. Data moves between devices by JAX's collectives and lax.ppermute only.
A program may use at most 64 MiB of HBM per device.

v0:
```python
import jax
import jax.numpy as jnp
from jax import lax


def conv_same(volume_in, weight):
    kernel = weight.reshape(3, 3, 3, weight.shape[1], weight.shape[2])
    result = lax.conv_general_dilated(
        volume_in[None],
        kernel,
        (1, 1, 1),
        ((1, 1), (1, 1), (1, 1)),
        dimension_numbers=("NDHWC", "DHWIO", "NDHWC"),
        preferred_element_type=jnp.float32,
    )
    return result[0]


def reference(volume, first_kernel, down_kernel, mid_kernel, up_kernel, last_kernel):
    skip = jax.nn.gelu(conv_same(volume, first_kernel)).astype(jnp.bfloat16)
    down_weights = down_kernel.reshape(2, 2, 2, down_kernel.shape[1], down_kernel.shape[2])
    coarse_raw = lax.conv_general_dilated(
        skip[None],
        down_weights,
        (2, 2, 2),
        "VALID",
        dimension_numbers=("NDHWC", "DHWIO", "NDHWC"),
        preferred_element_type=jnp.float32,
    )[0]
    coarse = jax.nn.gelu(coarse_raw).astype(jnp.bfloat16)
    middle = jax.nn.gelu(conv_same(coarse, mid_kernel)).astype(jnp.bfloat16)
    coarse_x, coarse_y, coarse_z, wide_chans = middle.shape
    fine_chans = up_kernel.shape[2]
    up_table = jnp.transpose(up_kernel, (1, 0, 2)).reshape(wide_chans, 8 * fine_chans)
    lifted_flat = jnp.dot(
        middle.reshape(-1, wide_chans), up_table, preferred_element_type=jnp.float32
    ).astype(jnp.bfloat16)
    lifted = lifted_flat.reshape(coarse_x, coarse_y, coarse_z, 2, 2, 2, fine_chans)
    lifted = jnp.transpose(lifted, (0, 3, 1, 4, 2, 5, 6)).reshape(
        2 * coarse_x, 2 * coarse_y, 2 * coarse_z, fine_chans
    )
    joined = jnp.concatenate([lifted, skip], axis=-1)
    return jax.nn.gelu(conv_same(joined, last_kernel)).astype(jnp.bfloat16)


def solution(mesh):
    return reference
```

profile of v0, /device:TPU:79, one launch (start us, length us, event | category | flops | bytes accessed | tf_op | source)
XLA Modules:
  0.0 271.1 jit_solution(14820290653775413811)
XLA Ops:
  6.6 0.7 all-gather.10.cloned.1.call-update
  7.3 1.3 dynamic-slice.21
  9.2 1.0 dynamic-slice_bitcast_fusion
  10.2 0.7 copy.70
  11.0 0.7 all-gather.14.cloned.1.call-update
  11.8 6.0 %collective-permute-start = (bf16[1,1,16,8,256]{4,3,2,1,0:T(8,128)(2,1)S(1)}, bf16[1,1,16,8,256]{4,3,2,1,0:T(8,128)(2,1)S(1)}, u32[]{:S(2)}, u32[]{:S(2)}) collective-permute-start(bf16[1,1,16,8,256]{4,3,2,1,0:T(8,128)(2,1)S(1)} %get-tuple-element.16), channel_id=2, source_target_pairs={{0,16},{1,17},{2,18},{3,19},{4,20},{5,21},{6,22},{7,23},{8,24},{9,... | collective-permute-start | bytes 196616 | tf_op jit(solution)/conv_general_dilated | solution.py:8
  17.8 1.9 collective-permute-start.1
  19.7 0.6 dynamic-slice.33
  21.0 6.7 %collective-permute-done.1 = bf16[1,1,16,8,256]{4,3,2,1,0:T(8,128)(2,1)S(1)} collective-permute-done((bf16[1,1,16,8,256]{4,3,2,1,0:T(8,128)(2,1)S(1)}, bf16[1,1,16,8,256]{4,3,2,1,0:T(8,128)(2,1)S(1)}, u32[]{:S(2)}, u32[]{:S(2)}) %collective-permute-start.1) | collective-permute-done | bytes 65568 | tf_op jit(solution)/conv_general_dilated | solution.py:8
  27.8 5.3 %collective-permute-start.2 = (bf16[1,4,1,8,256]{4,3,2,1,0:T(8,128)(2,1)S(1)}, bf16[1,4,1,8,256]{4,3,2,1,0:T(8,128)(2,1)S(1)}, u32[]{:S(2)}, u32[]{:S(2)}) collective-permute-start(bf16[1,4,1,8,256]{4,3,2,1,0:T(8,128)(2,1)S(1)} %get-tuple-element.14), channel_id=4, source_target_pairs={{0,2},{1,3},{2,4},{3,5},{4,6},{5,7},{6,8},{7,9},{8,10},{9,11},{10,... | collective-permute-start | bytes 49160 | tf_op jit(solution)/conv_general_dilated | solution.py:8
  33.1 1.9 collective-permute-start.3
  35.0 0.6 dynamic-slice.34
  36.3 1.9 collective-permute-done.3
  38.4 2.0 collective-permute-start.4
  40.4 1.3 collective-permute-start.5
  41.7 0.6 dynamic-slice.35
  42.9 2.9 %collective-permute-done.5 = bf16[1,4,18,1,256]{4,3,2,1,0:T(2,128)(2,1)S(1)} collective-permute-done((bf16[1,4,18,1,256]{4,3,2,1,0:T(2,128)(2,1)S(1)}, bf16[1,4,18,1,256]{4,3,2,1,0:T(2,128)(2,1)S(1)}, u32[]{:S(2)}, u32[]{:S(2)}) %collective-permute-start.5) | collective-permute-done | bytes 36896 | tf_op jit(solution)/conv_general_dilated | solution.py:8
  45.8 0.4 fusion.21
  46.3 36.9 %all-gather.10.cloned.1.call-done = bf16[3,3,3,256,256]{4,3,2,1,0:T(8,128)(2,1)} async-done(((bf16[3,3,3,16,256]{4,3,2,1,0:T(8,128)(2,1)}), bf16[3,3,3,256,256]{4,3,2,1,0:T(8,128)(2,1)}) %all-gather.10.cloned.1.call-update) | async-done | bytes 3538960 | tf_op jit(solution)/reshape | solution.py:7
  83.2 6.8 %fusion.28 = f32[1,2,16,8,256]{4,0,3,2,1:T(1,128)S(1)} fusion(bf16[3,3,3,256,256]{4,3,2,1,0:T(8,128)(2,1)} %all-gather.10.cloned.1.call-done, bf16[1,4,18,10,256]{4,3,2,1,0:T(8,128)(2,1)S(1)} %fusion.21), kind=kOutput, calls=%fused_computation.35 | convolution fusion | flops 905969664 | bytes 4169728 | tf_op jit(solution)/conv_general_dilated | solution.py:8
  90.1 0.7 fusion.62
  90.9 16.6 %all-gather.1 = bf16[1,1,64,4,512]{4,3,1,0,2:T(4,128)(2,1)S(1)} all-gather(bf16[1,1,8,4,512]{4,3,1,0,2:T(4,128)(2,1)S(1)} %copy.53), channel_id=8, replica_groups=mesh['axis_0'=16,'axis_1'=8,'axis_2'=2] {'axis_1'}, dimensions={2}, use_global_device_ids=true | all-gather | bytes 294912 | tf_op jit(solution)/convert_element_type | solution.py:30
  107.5 3.6 %collective-permute-start.6 = (bf16[1,1,64,4,512]{4,3,1,0,2:T(4,128)(2,1)S(1)}, bf16[1,1,64,4,512]{4,3,1,0,2:T(4,128)(2,1)S(1)}, u32[]{:S(2)}, u32[]{:S(2)}) collective-permute-start(bf16[1,1,64,4,512]{4,3,1,0,2:T(4,128)(2,1)S(1)} %all-gather.1), channel_id=9, source_target_pairs={{0,16},{1,17},{16,32},{17,33},{32,48},{33,49},{48,64},{49,65},{64,... | collective-permute-start | bytes 786440 | tf_op jit(solution)/convert_element_type | solution.py:30
  111.1 1.9 collective-permute-start.7
  113.0 0.6 dynamic-slice.10
  113.6 1.3 dynamic-slice.11
  114.9 2.6 collective-permute-done.6
  117.6 13.4 %collective-permute-done.7 = bf16[1,1,64,4,512]{4,3,1,0,2:T(4,128)(2,1)S(1)} collective-permute-done((bf16[1,1,64,4,512]{4,3,1,0,2:T(4,128)(2,1)S(1)}, bf16[1,1,64,4,512]{4,3,1,0,2:T(4,128)(2,1)S(1)}, u32[]{:S(2)}, u32[]{:S(2)}) %collective-permute-start.7) | collective-permute-done | bytes 262176 | tf_op jit(solution)/convert_element_type | solution.py:30
  131.0 1.3 fusion.13
  132.3 0.5 fusion.81
  132.9 1.3 collective-permute-start.8
  134.2 1.5 collective-permute-start.9
  135.7 1.2 dynamic-slice.12
  136.9 0.7 dynamic-slice.29
  138.2 17.8 %collective-permute-done.8 = bf16[1,3,64,1,512]{4,3,1,0,2:T(2,128)(2,1)S(1)} collective-permute-done((bf16[1,3,64,1,512]{4,3,1,0,2:T(2,128)(2,1)S(1)}, bf16[1,3,64,1,512]{4,3,1,0,2:T(2,128)(2,1)S(1)}, u32[]{:S(2)}, u32[]{:S(2)}) %collective-permute-start.8) | collective-permute-done | bytes 196640 | tf_op jit(solution)/conv_general_dilated | solution.py:8
  155.9 1.9 collective-permute-done.9
  157.9 1.5 fusion.3
  159.4 7.4 %fusion.6 = f32[1,1,64,4,64]{4,0,3,2,1:T(1,128)S(1)} fusion(bf16[3,3,3,512,64]{3,4,2,1,0:T(8,128)(2,1)S(1)} %bitcast.54, bf16[1,3,64,6,512]{4,3,1,0,2:T(8,128)(2,1)S(1)} %fusion.3), kind=kOutput, calls=%fused_computation.8 | convolution fusion | flops 448266240 | bytes 3014656 | tf_op jit(solution)/conv_general_dilated | solution.py:8
  166.9 7.9 %all-gather.2 = bf16[1,1,64,8,64]{4,2,1,0,3:T(8,128)(2,1)S(1)} all-gather(bf16[1,1,64,4,64]{4,2,1,0,3:T(8,128)(2,1)S(1)} %fusion.80), channel_id=13, replica_groups=[128,2]<=[256], dimensions={3}, use_global_device_ids=true | all-gather | bytes 98304 | tf_op jit(solution)/convert_element_type | solution.py:31
  174.9 0.8 reshape.95
  175.7 14.1 %all-to-all-start = ((bf16[8,2,2048]{2,1,0:T(2,128)(2,1)}), bf16[8,2,2048]{2,1,0:T(2,128)(2,1)S(1)}, u32[]{:S(2)}, u32[]{:S(2)}) async-start(bf16[8,2,2048]{2,1,0:T(2,128)(2,1)} %reshape.95), calls=%async_computation | async-start | bytes 131072 | tf_op jit(solution)/convert_element_type | solution.py:31
  189.9 4.1 %all-to-all-done = bf16[8,2,2048]{2,1,0:T(2,128)(2,1)S(1)} async-done(((bf16[8,2,2048]{2,1,0:T(2,128)(2,1)}), bf16[8,2,2048]{2,1,0:T(2,128)(2,1)S(1)}, u32[]{:S(2)}, u32[]{:S(2)}) %all-to-all-start) | async-done | bytes 65568 | tf_op jit(solution)/convert_element_type | solution.py:31
  194.0 0.1 reshape.96
  194.2 0.1 reshape.56
  194.4 2.1 convolution_convert_fusion
  196.5 0.7 constant_dynamic-slice_fusion
  197.3 0.1 copy.87
  197.5 5.1 %collective-permute-start.10 = (bf16[1,1,16,8,512]{4,3,2,1,0:T(8,128)(2,1)S(1)}, bf16[1,1,16,8,512]{4,3,2,1,0:T(8,128)(2,1)S(1)}, u32[]{:S(2)}, u32[]{:S(2)}) collective-permute-start(bf16[1,1,16,8,512]{4,3,2,1,0:T(8,128)(2,1)S(1)} %get-tuple-element.12), channel_id=18, source_target_pairs={{0,16},{1,17},{2,18},{3,19},{4,20},{5,21},{6,22},{7,23},{8,24},{9,... | collective-permute-start | bytes 393224 | tf_op jit(solution)/conv_general_dilated | solution.py:8
  202.6 1.9 collective-permute-start.11
  204.5 13.8 %collective-permute-done.10 = bf16[1,1,16,8,512]{4,3,2,1,0:T(8,128)(2,1)S(1)} collective-permute-done((bf16[1,1,16,8,512]{4,3,2,1,0:T(8,128)(2,1)S(1)}, bf16[1,1,16,8,512]{4,3,2,1,0:T(8,128)(2,1)S(1)}, u32[]{:S(2)}, u32[]{:S(2)}) %collective-permute-start.10) | collective-permute-done | bytes 131104 | tf_op jit(solution)/conv_general_dilated | solution.py:8
  218.3 2.2 collective-permute-done.11
  220.5 0.1 fusion.27
  220.7 16.6 %collective-permute-start.12 = (bf16[1,4,1,8,512]{4,3,2,1,0:T(8,128)(2,1)S(1)}, bf16[1,4,1,8,512]{4,3,2,1,0:T(8,128)(2,1)S(1)}, u32[]{:S(2)}, u32[]{:S(2)}) collective-permute-start(bf16[1,4,1,8,512]{4,3,2,1,0:T(8,128)(2,1)S(1)} %get-tuple-element.8), channel_id=20, source_target_pairs={{0,2},{1,3},{2,4},{3,5},{4,6},{5,7},{6,8},{7,9},{8,10},{9,11},{10,... | collective-permute-start | bytes 98312 | tf_op jit(solution)/conv_general_dilated | solution.py:8
  237.3 1.9 collective-permute-start.13
  239.2 3.3 %collective-permute-done.13 = bf16[1,4,1,8,512]{4,3,2,1,0:T(8,128)(2,1)S(1)} collective-permute-done((bf16[1,4,1,8,512]{4,3,2,1,0:T(8,128)(2,1)S(1)}, bf16[1,4,1,8,512]{4,3,2,1,0:T(8,128)(2,1)S(1)}, u32[]{:S(2)}, u32[]{:S(2)}) %collective-permute-start.13) | collective-permute-done | bytes 32800 | tf_op jit(solution)/conv_general_dilated | solution.py:8
  242.5 0.2 fusion.23
  242.7 0.2 fusion.82
  242.9 1.3 collective-permute-start.14
  244.2 1.5 collective-permute-start.15
  245.7 0.6 collective-permute-done.14
  246.3 3.8 %collective-permute-done.15 = bf16[1,4,18,1,512]{4,3,2,1,0:T(2,128)(2,1)S(1)} collective-permute-done((bf16[1,4,18,1,512]{4,3,2,1,0:T(2,128)(2,1)S(1)}, bf16[1,4,18,1,512]{4,3,2,1,0:T(2,128)(2,1)S(1)}, u32[]{:S(2)}, u32[]{:S(2)}) %collective-permute-start.15) | collective-permute-done | bytes 73760 | tf_op jit(solution)/conv_general_dilated | solution.py:8
  250.1 0.9 fusion.9
  251.0 12.8 %fusion.14 = f32[1,2,16,8,256]{4,0,3,2,1:T(1,128)S(1)} fusion(bf16[3,3,3,512,256]{4,3,2,1,0:T(8,128)(2,1)} %all-gather.14.cloned.1.call-done, bf16[1,4,18,10,512]{4,3,2,1,0:T(8,128)(2,1)S(1)} %fusion.9), kind=kOutput, calls=%fused_computation.18 | convolution fusion | flops 1811939328 | bytes 8077312 | tf_op jit(solution)/conv_general_dilated | solution.py:8
  263.8 0.7 fusion.61
  (47 shorter events, 1.1 us)
Async XLA Ops:
  6.5 83.6 %copy-start = (bf16[8,256,512]{2,1,0:T(8,128)(2,1)S(1)}, bf16[8,256,512]{2,1,0:T(8,128)(2,1)}, u32[]{:S(2)}) copy-start(bf16[8,256,512]{2,1,0:T(8,128)(2,1)} %param.2) | copy-start | bytes 6291460
  6.5 13.2 %copy-start.7 = (s32[256]{0:T(256)S(1)}, s32[256]{0:T(256)}, u32[]{:S(2)}) copy-start(s32[256]{0:T(256)} %constant.22) | copy-start | bytes 3076
  6.5 28.5 %copy-start.6 = (s32[256]{0:T(256)S(1)}, s32[256]{0:T(256)}, u32[]{:S(2)}) copy-start(s32[256]{0:T(256)} %constant.23) | copy-start | bytes 3076
  6.5 5.2 %copy-start.1 = (bf16[2,16,8,256]{3,2,1,0:T(8,128)(2,1)S(1)}, bf16[2,16,8,256]{3,2,1,0:T(8,128)(2,1)}, u32[]{:S(2)}) copy-start(bf16[2,16,8,256]{3,2,1,0:T(8,128)(2,1)} %param) | copy-start | bytes 393220
  6.5 76.6 %all-gather.10.cloned.1.call-start = ((), (), s32[]{:S(2)}) async-start(), calls=%async_computation.1 | async-start | bytes 3760128 | tf_op jit(solution)/reshape | solution.py:7
  7.3 187.1 %all-gather.12.cloned.1.call-start = ((), (), s32[]{:S(2)}) async-start(), calls=%async_computation.2 | async-start | bytes 2359296 | tf_op jit(solution)/reshape | solution.py:34
  10.2 31.4 %copy-start.5 = (s32[256]{0:T(256)S(1)}, s32[256]{0:T(256)}, u32[]{:S(2)}) copy-start(s32[256]{0:T(256)} %constant.24) | copy-start | bytes 3076
  11.0 240.0 %all-gather.14.cloned.1.call-start = ((), (), s32[]{:S(2)}) async-start(), calls=%async_computation.3 | async-start | bytes 7520256 | tf_op jit(solution)/reshape | solution.py:7
  11.8 9.2 %collective-permute-start = (bf16[1,1,16,8,256]{4,3,2,1,0:T(8,128)(2,1)S(1)}, bf16[1,1,16,8,256]{4,3,2,1,0:T(8,128)(2,1)S(1)}, u32[]{:S(2)}, u32[]{:S(2)}) collective-permute-start(bf16[1,1,16,8,256]{4,3,2,1,0:T(8,128)(2,1)S(1)} %get-tuple-element.16), channel_id=2, source_target_pairs={{0,16},{1,17},{2,18},{3,19},{4,20},{5,21},{6,22},{7,23},{8,24},{9,... | collective-permute-start | bytes 196616 | tf_op jit(solution)/conv_general_dilated | solution.py:8
  17.8 9.9 %collective-permute-start.1 = (bf16[1,1,16,8,256]{4,3,2,1,0:T(8,128)(2,1)S(1)}, bf16[1,1,16,8,256]{4,3,2,1,0:T(8,128)(2,1)S(1)}, u32[]{:S(2)}, u32[]{:S(2)}) collective-permute-start(bf16[1,1,16,8,256]{4,3,2,1,0:T(8,128)(2,1)S(1)} %get-tuple-element.17), channel_id=3, source_target_pairs={{16,0},{17,1},{18,2},{19,3},{20,4},{21,5},{22,6},{23,7},{24,8},{25... | collective-permute-start | bytes 196616 | tf_op jit(solution)/conv_general_dilated | solution.py:8
  27.8 8.5 %collective-permute-start.2 = (bf16[1,4,1,8,256]{4,3,2,1,0:T(8,128)(2,1)S(1)}, bf16[1,4,1,8,256]{4,3,2,1,0:T(8,128)(2,1)S(1)}, u32[]{:S(2)}, u32[]{:S(2)}) collective-permute-start(bf16[1,4,1,8,256]{4,3,2,1,0:T(8,128)(2,1)S(1)} %get-tuple-element.14), channel_id=4, source_target_pairs={{0,2},{1,3},{2,4},{3,5},{4,6},{5,7},{6,8},{7,9},{8,10},{9,11},{10,... | collective-permute-start | bytes 49160 | tf_op jit(solution)/conv_general_dilated | solution.py:8
  33.1 5.1 %collective-permute-start.3 = (bf16[1,4,1,8,256]{4,3,2,1,0:T(8,128)(2,1)S(1)}, bf16[1,4,1,8,256]{4,3,2,1,0:T(8,128)(2,1)S(1)}, u32[]{:S(2)}, u32[]{:S(2)}) collective-permute-start(bf16[1,4,1,8,256]{4,3,2,1,0:T(8,128)(2,1)S(1)} %get-tuple-element.15), channel_id=5, source_target_pairs={{2,0},{3,1},{4,2},{5,3},{6,4},{7,5},{8,6},{9,7},{10,8},{11,9},{12,... | collective-permute-start | bytes 49160 | tf_op jit(solution)/conv_general_dilated | solution.py:8
  38.4 4.6 %collective-permute-start.4 = (bf16[1,4,18,1,256]{4,3,2,1,0:T(2,128)(2,1)S(1)}, bf16[1,4,18,1,256]{4,3,2,1,0:T(2,128)(2,1)S(1)}, u32[]{:S(2)}, u32[]{:S(2)}) collective-permute-start(bf16[1,4,18,1,256]{4,3,2,1,0:T(2,128)(2,1)S(1)} %get-tuple-element.10), channel_id=6, source_target_pairs={{0,1},{2,3},{4,5},{6,7},{8,9},{10,11},{12,13},{14,15},{16,17},{18,... | collective-permute-start | bytes 110600 | tf_op jit(solution)/conv_general_dilated | solution.py:8
  40.4 5.5 %collective-permute-start.5 = (bf16[1,4,18,1,256]{4,3,2,1,0:T(2,128)(2,1)S(1)}, bf16[1,4,18,1,256]{4,3,2,1,0:T(2,128)(2,1)S(1)}, u32[]{:S(2)}, u32[]{:S(2)}) collective-permute-start(bf16[1,4,18,1,256]{4,3,2,1,0:T(2,128)(2,1)S(1)} %get-tuple-element.11), channel_id=7, source_target_pairs={{1,0},{3,2},{5,4},{7,6},{9,8},{11,10},{13,12},{15,14},{17,16},{19,... | collective-permute-start | bytes 110600 | tf_op jit(solution)/conv_general_dilated | solution.py:8
  90.1 22.9 %copy-start.4 = (u32[256]{0:T(256)S(1)}, u32[256]{0:T(256)}, u32[]{:S(2)}) copy-start(u32[256]{0:T(256)} %constant.54) | copy-start | bytes 3076
  90.1 23.5 %copy-start.9 = (s32[32]{0:T(128)S(1)}, s32[32]{0:T(128)}, u32[]{:S(2)}) copy-start(s32[32]{0:T(128)} %constant.57) | copy-start | bytes 388
  107.5 10.1 %collective-permute-start.6 = (bf16[1,1,64,4,512]{4,3,1,0,2:T(4,128)(2,1)S(1)}, bf16[1,1,64,4,512]{4,3,1,0,2:T(4,128)(2,1)S(1)}, u32[]{:S(2)}, u32[]{:S(2)}) collective-permute-start(bf16[1,1,64,4,512]{4,3,1,0,2:T(4,128)(2,1)S(1)} %all-gather.1), channel_id=9, source_target_pairs={{0,16},{1,17},{16,32},{17,33},{32,48},{33,49},{48,64},{49,65},{64,... | collective-permute-start | bytes 786440 | tf_op jit(solution)/convert_element_type | solution.py:30
  111.1 19.9 %collective-permute-start.7 = (bf16[1,1,64,4,512]{4,3,1,0,2:T(4,128)(2,1)S(1)}, bf16[1,1,64,4,512]{4,3,1,0,2:T(4,128)(2,1)S(1)}, u32[]{:S(2)}, u32[]{:S(2)}) collective-permute-start(bf16[1,1,64,4,512]{4,3,1,0,2:T(4,128)(2,1)S(1)} %all-gather.1), channel_id=10, source_target_pairs={{16,0},{17,1},{32,16},{33,17},{48,32},{49,33},{64,48},{65,49},{80,... | collective-permute-start | bytes 786440 | tf_op jit(solution)/convert_element_type | solution.py:30
  131.0 4.7 %copy-start.8 = (s32[32]{0:T(128)S(1)}, s32[32]{0:T(128)}, u32[]{:S(2)}) copy-start(s32[32]{0:T(128)} %constant.59) | copy-start | bytes 388
  131.0 5.9 %copy-start.3 = (s32[256]{0:T(256)S(1)}, s32[256]{0:T(256)}, u32[]{:S(2)}) copy-start(s32[256]{0:T(256)} %constant.104) | copy-start | bytes 3076
  132.9 23.0 %collective-permute-start.8 = (bf16[1,3,64,1,512]{4,3,1,0,2:T(2,128)(2,1)S(1)}, bf16[1,3,64,1,512]{4,3,1,0,2:T(2,128)(2,1)S(1)}, u32[]{:S(2)}, u32[]{:S(2)}) collective-permute-start(bf16[1,3,64,1,512]{4,3,1,0,2:T(2,128)(2,1)S(1)} %get-tuple-element.4), channel_id=11, source_target_pairs={{0,1},{16,17},{32,33},{48,49},{64,65},{80,81},{96,97},{112,113},{1... | collective-permute-start | bytes 589832 | tf_op jit(solution)/conv_general_dilated | solution.py:8
  134.2 23.7 %collective-permute-start.9 = (bf16[1,3,64,1,512]{4,3,1,0,2:T(2,128)(2,1)S(1)}, bf16[1,3,64,1,512]{4,3,1,0,2:T(2,128)(2,1)S(1)}, u32[]{:S(2)}, u32[]{:S(2)}) collective-permute-start(bf16[1,3,64,1,512]{4,3,1,0,2:T(2,128)(2,1)S(1)} %get-tuple-element.5), channel_id=12, source_target_pairs={{1,0},{17,16},{33,32},{49,48},{65,64},{81,80},{97,96},{113,112},{1... | collective-permute-start | bytes 589832 | tf_op jit(solution)/conv_general_dilated | solution.py:8
  157.9 1.5 copy-start.2
  175.7 18.3 %all-to-all-start = ((bf16[8,2,2048]{2,1,0:T(2,128)(2,1)}), bf16[8,2,2048]{2,1,0:T(2,128)(2,1)S(1)}, u32[]{:S(2)}, u32[]{:S(2)}) async-start(bf16[8,2,2048]{2,1,0:T(2,128)(2,1)} %reshape.95), calls=%async_computation | async-start | bytes 131072 | tf_op jit(solution)/convert_element_type | solution.py:31
  197.5 20.8 %collective-permute-start.10 = (bf16[1,1,16,8,512]{4,3,2,1,0:T(8,128)(2,1)S(1)}, bf16[1,1,16,8,512]{4,3,2,1,0:T(8,128)(2,1)S(1)}, u32[]{:S(2)}, u32[]{:S(2)}) collective-permute-start(bf16[1,1,16,8,512]{4,3,2,1,0:T(8,128)(2,1)S(1)} %get-tuple-element.12), channel_id=18, source_target_pairs={{0,16},{1,17},{2,18},{3,19},{4,20},{5,21},{6,22},{7,23},{8,24},{9,... | collective-permute-start | bytes 393224 | tf_op jit(solution)/conv_general_dilated | solution.py:8
  202.6 18.0 %collective-permute-start.11 = (bf16[1,1,16,8,512]{4,3,2,1,0:T(8,128)(2,1)S(1)}, bf16[1,1,16,8,512]{4,3,2,1,0:T(8,128)(2,1)S(1)}, u32[]{:S(2)}, u32[]{:S(2)}) collective-permute-start(bf16[1,1,16,8,512]{4,3,2,1,0:T(8,128)(2,1)S(1)} %get-tuple-element.13), channel_id=19, source_target_pairs={{16,0},{17,1},{18,2},{19,3},{20,4},{21,5},{22,6},{23,7},{24,8},{25... | collective-permute-start | bytes 393224 | tf_op jit(solution)/conv_general_dilated | solution.py:8
  220.7 18.5 %collective-permute-start.12 = (bf16[1,4,1,8,512]{4,3,2,1,0:T(8,128)(2,1)S(1)}, bf16[1,4,1,8,512]{4,3,2,1,0:T(8,128)(2,1)S(1)}, u32[]{:S(2)}, u32[]{:S(2)}) collective-permute-start(bf16[1,4,1,8,512]{4,3,2,1,0:T(8,128)(2,1)S(1)} %get-tuple-element.8), channel_id=20, source_target_pairs={{0,2},{1,3},{2,4},{3,5},{4,6},{5,7},{6,8},{7,9},{8,10},{9,11},{10,... | collective-permute-start | bytes 98312 | tf_op jit(solution)/conv_general_dilated | solution.py:8
  237.3 5.2 %collective-permute-start.13 = (bf16[1,4,1,8,512]{4,3,2,1,0:T(8,128)(2,1)S(1)}, bf16[1,4,1,8,512]{4,3,2,1,0:T(8,128)(2,1)S(1)}, u32[]{:S(2)}, u32[]{:S(2)}) collective-permute-start(bf16[1,4,1,8,512]{4,3,2,1,0:T(8,128)(2,1)S(1)} %get-tuple-element.9), channel_id=21, source_target_pairs={{2,0},{3,1},{4,2},{5,3},{6,4},{7,5},{8,6},{9,7},{10,8},{11,9},{12,... | collective-permute-start | bytes 98312 | tf_op jit(solution)/conv_general_dilated | solution.py:8
  242.9 3.4 %collective-permute-start.14 = (bf16[1,4,18,1,512]{4,3,2,1,0:T(2,128)(2,1)S(1)}, bf16[1,4,18,1,512]{4,3,2,1,0:T(2,128)(2,1)S(1)}, u32[]{:S(2)}, u32[]{:S(2)}) collective-permute-start(bf16[1,4,18,1,512]{4,3,2,1,0:T(2,128)(2,1)S(1)} %get-tuple-element.6), channel_id=22, source_target_pairs={{0,1},{2,3},{4,5},{6,7},{8,9},{10,11},{12,13},{14,15},{16,17},{18,... | collective-permute-start | bytes 221192 | tf_op jit(solution)/conv_general_dilated | solution.py:8
  244.2 5.9 %collective-permute-start.15 = (bf16[1,4,18,1,512]{4,3,2,1,0:T(2,128)(2,1)S(1)}, bf16[1,4,18,1,512]{4,3,2,1,0:T(2,128)(2,1)S(1)}, u32[]{:S(2)}, u32[]{:S(2)}) collective-permute-start(bf16[1,4,18,1,512]{4,3,2,1,0:T(2,128)(2,1)S(1)} %get-tuple-element.7), channel_id=23, source_target_pairs={{1,0},{3,2},{5,4},{7,6},{9,8},{11,10},{13,12},{15,14},{17,16},{19,... | collective-permute-start | bytes 221192 | tf_op jit(solution)/conv_general_dilated | solution.py:8
Sparse Core Ops, SparseCore 0:
  9.8 73.3 all-gather.9
  85.0 31.0 all-gather.11
  118.6 112.9 all-gather.13
where the time goes:
time: 272 us; the launch traced here: 271 us
  waiting for transfers between devices  113 us (42%)
  starting transfers between devices  69.3 us (25%)
  matrix products  29.8 us (11%)
  blocking collectives  24.4 us (9%)
  between operations  16.8 us (6%)
  local copies, waits for them, and re-layouts  11.6 us (4%)
  other arithmetic  5.59 us (2%)
    conv_general_dilated x14, waiting for transfers between devices, conv_same(): lax.conv_general_dilated(volume_in[None], kernel, (1, 1, 1), ((1, 1), (1,...  55 us
    conv_general_dilated x14, starting transfers between devices, conv_same(): lax.conv_general_dilated(volume_in[None], kernel, (1, 1, 1), ((1, 1), (1,...  49.5 us
    reshape x2, waiting for transfers between devices, conv_same(): kernel = weight.reshape(3, 3, 3, weight.shape[1], weight.shape[2])  36.9 us
    conv_general_dilated x3, matrix products, conv_same(): lax.conv_general_dilated(volume_in[None], kernel, (1, 1, 1), ((1, 1), (1,...  27 us
    convert_element_type x1, blocking collectives, reference(): coarse = jax.nn.gelu(coarse_raw).astype(jnp.bfloat16)  16.6 us
    convert_element_type x2, waiting for transfers between devices, reference(): coarse = jax.nn.gelu(coarse_raw).astype(jnp.bfloat16)  16.1 us
    convert_element_type x1, starting transfers between devices, reference(): middle = jax.nn.gelu(conv_same(coarse, mid_kernel)).astype(jnp.bfloat16)  14.1 us
    convert_element_type x1, blocking collectives, reference(): middle = jax.nn.gelu(conv_same(coarse, mid_kernel)).astype(jnp.bfloat16)  7.87 us
  transfers between devices with their start and end apart: 20, of which 14 were waited for; matrix products, arithmetic and copies ran while one was open for 12% of the time, Pallas kernels for 0%

commit v1 on v0

v1 whole, which is shorter than its diff:
```python
import functools

import jax
import jax.numpy as jnp
import numpy as np
from jax import lax
from jax.sharding import PartitionSpec as P

BF = jnp.bfloat16
F32 = jnp.float32
ALL = ("row", "col", "depth")


def shards_of(r, j):
    zhi, x = r // 4, r % 4
    y, c = j // 2, j % 2
    s1 = ((zhi + c) % 4) * 4 + (x + y) % 4
    s2 = ((zhi + c + 2) % 4) * 4 + (x - y) % 4
    return s1, s2


def flat(r, j, d):
    return (r * 8 + j) * 2 + d


def shard_perms():
    p1, p2 = [], []
    for r in range(16):
        for j in range(8):
            for d in range(2):
                s1, s2 = shards_of(r, j)
                p1.append((flat(s1, j, d), flat(r, j, d)))
                p2.append((flat(s2, j, d if j % 2 else 1 - d), flat(r, j, d)))
    return p1, p2


def tables():
    first = np.zeros((16, 256), np.int32)
    skip = np.zeros((16, 256), np.int32)
    for r in range(16):
        for j in range(8):
            s1, s2 = shards_of(r, j)
            sk = (s2 if s1 < 8 else s1) - 8
            for i in range(16):
                first[r, 32 * j + i] = 16 * s1 + i
                first[r, 32 * j + 16 + i] = 16 * s2 + i
            for i in range(32):
                skip[r, 32 * j + i] = 32 * sk + i
    return first, skip


def pick(table_row):
    want = jnp.tile(table_row.reshape(8, 1, 32), (1, 4, 1)).reshape(8, 128)
    want = want + (256 * (jnp.arange(128) // 32))[None, :]
    return (jnp.arange(1024)[:, None, None] == want[None]).astype(BF)


def edge_swap(face_lo, face_hi, d):
    send = jnp.where(d == 0, face_hi, face_lo)
    return lax.ppermute(send, "depth", [(0, 1), (1, 0)])


def row_halo(for_next, for_prev):
    lo = lax.ppermute(for_next, "row", [(i, i + 1) for i in range(15)])
    hi = lax.ppermute(for_prev, "row", [(i + 1, i) for i in range(15)])
    return lo, hi


def fine_halo(t, d):
    recv = edge_swap(t[:, 0], t[:, 7], d)
    t9 = jnp.concatenate([t, recv[:, None]], 1)
    lo, hi = row_halo(t9[1], t9[0])
    return jnp.stack([lo, t9[0], t9[1], hi])


def to_slab(t4, sel, d):
    rows = t4.reshape(4, 144, 256)
    sel = sel.reshape(4, 256, 8, 128)
    mixed = jnp.einsum("prc,pcjk->jrk", rows, sel, preferred_element_type=F32).astype(BF)
    got = lax.all_to_all(mixed, "col", 0, 0, tiled=True)
    planes = got.reshape(8, 9, 16, 128).transpose(1, 0, 2, 3).reshape(9, 128, 128)
    return z_ends(planes, d)


def z_ends(planes, d):
    last = planes[-1:]
    none = jnp.zeros_like(last)
    return jnp.concatenate([jnp.where(d == 0, none, last), planes[:-1], jnp.where(d == 0, last, none)], 0)


def slab_weights(w):
    w = w.reshape(3, 9, 32, 256)
    zero = jnp.zeros((1, 9, 32, 256), w.dtype)
    left = jnp.concatenate([w, zero], 0)
    right = jnp.concatenate([zero, w], 0)
    both = jnp.stack([left, right], 3)
    return both.transpose(1, 0, 2, 3, 4).reshape(9, 128, 512)


def slab_conv(planes, wt):
    pad = jnp.pad(planes, ((0, 0), (1, 1), (0, 0)))
    cols = [pad[c : c + 8, b : b + 128] for b in range(3) for c in range(3)]
    patches = jnp.concatenate(cols, -1).reshape(1024, 1152)
    return jnp.dot(patches, wt.reshape(1152, 512), preferred_element_type=F32)


def reduce_tiles(acc, j):
    y, c = j // 2, j % 2
    t = acc.reshape(8, 4, 2, 16, 512).transpose(2, 1, 0, 3, 4)
    keep = jnp.where(c == 0, t[0], t[1])
    send = jnp.where(c == 0, t[1], t[0])
    pair = keep + lax.ppermute(send, "col", [(i, i ^ 1) for i in range(8)])
    pair = jnp.roll(pair, -y, 0)
    total = pair[0]
    for o in (1, 3, 2):
        perm = [(2 * a + b, 2 * ((a + o) % 4) + b) for a in range(4) for b in range(2)]
        total = total + lax.ppermute(pair[o].astype(BF), "col", perm).astype(F32)
    return total


def body(volume, first_kernel, down_kernel, mid_kernel, up_kernel, last_kernel):
    r, j, d = (lax.axis_index(a) for a in ALL)
    p1, p2 = shard_perms()
    first_table, skip_table = (jnp.asarray(t) for t in tables())
    w1 = jnp.concatenate([lax.ppermute(first_kernel, ALL, p) for p in (p1, p2)], 1)
    la, lb = (lax.ppermute(last_kernel, ALL, p) for p in (p1, p2))
    in_low = (r // 4 + j % 2) % 4 < 2
    w_lift, w_skip = jnp.where(in_low, la, lb), jnp.where(in_low, lb, la)
    base = (jnp.where(in_low, 0, 2) + r // 4 + j % 2) % 4 * 4
    lift_at = base + (r % 4 + jnp.where(in_low, j // 2, -(j // 2))) % 4

    tile = volume.transpose(0, 2, 1, 3)
    planes = to_slab(fine_halo(tile, d), pick(first_table[r]), d)
    part = slab_conv(planes, slab_weights(w1))
    skip = jax.nn.gelu(reduce_tiles(part, j)).astype(BF).reshape(8, 16, 2, 256)

    cells = skip.reshape(4, 2, 8, 2, 2, 256)
    down = down_kernel.reshape(2, 2, 2, 256, 512)
    coarse = jax.nn.gelu(jnp.einsum("kcjbae,abceo->kjo", cells, down, preferred_element_type=F32)).astype(BF)
    recv = edge_swap(coarse[0], coarse[3], d)
    c5 = jnp.concatenate([coarse, recv[None]], 0)
    lo, hi = row_halo(c5, c5)
    c3 = jnp.stack([lo, c5, hi])
    got = lax.all_gather(c3, "col", axis=0)
    slab = got.transpose(1, 2, 0, 3, 4).reshape(3, 5, 64, 512)
    slab = jnp.stack([z_ends(slab[a], d) for a in range(3)])
    wm = mid_kernel.reshape(3, 3, 3, 512, 64).transpose(0, 2, 3, 1, 4).reshape(9, 512, 192)
    g = sum(
        jnp.dot(slab[a, c : c + 4].reshape(256, 512), wm[3 * a + c], preferred_element_type=F32)
        for a in range(3)
        for c in range(3)
    )
    g = jnp.pad(g.reshape(4, 64, 192), ((0, 0), (1, 1), (0, 0)))
    middle = jax.nn.gelu(g[:, 0:64, 0:64] + g[:, 1:65, 64:128] + g[:, 2:66, 128:192]).astype(BF)

    slab_skip = to_slab(fine_halo(skip.transpose(2, 0, 1, 3), d), pick(skip_table[r]), d)
    part = slab_conv(slab_skip, slab_weights(w_skip))

    recv = edge_swap(middle[0], middle[3], d)
    m5 = jnp.concatenate([middle, recv[None]], 0)
    lo, hi = row_halo(m5, m5)
    m3 = jnp.stack([lo, m5, hi])
    packed = jnp.concatenate([m3.reshape(15, 64, 64), jnp.zeros((1, 64, 64), BF)], 0)
    packed = packed.reshape(8, 2, 64, 64).transpose(0, 2, 1, 3).reshape(512, 128)
    got = lax.all_gather(packed, "col", axis=0)
    got = got.reshape(8, 8, 64, 2, 64).transpose(1, 3, 2, 0, 4).reshape(16, 64, 512)[:15].reshape(3, 5, 64, 512)
    up = lax.dynamic_slice(up_kernel, (0, 0, 32 * lift_at), (8, 512, 32)).reshape(2, 2, 2, 512, 32)
    rows = [
        jnp.einsum("kye,bceo->kcybo", got[m], up[a], preferred_element_type=F32).astype(BF)
        for m, a in ((0, 1), (1, 0), (1, 1), (2, 0))
    ]
    lift = jnp.stack(rows, -2).reshape(5, 2, 128, 128)
    own = lift[:4].reshape(8, 128, 128)
    end = jnp.where(d == 0, lift[4, 0], lift[4, 1])[None]
    planes = z_ends(jnp.concatenate([own, end], 0), d)
    part = part + slab_conv(planes, slab_weights(w_lift))
    out = jax.nn.gelu(reduce_tiles(part, j)).astype(BF).reshape(8, 16, 2, 256)
    return out.transpose(2, 1, 0, 3)


def solution(mesh):
    cells = P("row", "col", "depth", None)
    rows = P(None, "row", None)
    return jax.shard_map(
        body,
        mesh=mesh,
        in_specs=(cells, rows, P(), P(None, None, "col"), P(), rows),
        out_specs=cells,
        check_vma=False,
    )
```

time: 272 us -> 229 us (0.84)
  waiting for transfers between devices: 113 us -> 65.4 us
  local copies, waits for them, and re-layouts: 11.6 us -> 38.3 us
  matrix products: 29.8 us -> 14.1 us
  blocking collectives: 24.4 us -> 18 us
  other arithmetic: 5.59 us -> 9.53 us
  starting transfers between devices: 69.3 us -> 65.6 us
    conv_general_dilated x14 -> x0, waiting for transfers between devices: 55 us -> none  [conv_same(): lax.conv_general_dilated(volume_in[None], kernel, (1, 1, 1), ((1, 1), (1,...]
    ppermute x0 -> x24, starting transfers between devices: none -> 53.3 us  [the longest x4 14.8 us: row_halo(): lo = lax.ppermute(for_next, 'row', [(i, i + 1) for i in range(15)])]
    conv_general_dilated x14 -> x0, starting transfers between devices: 49.5 us -> none  [conv_same(): lax.conv_general_dilated(volume_in[None], kernel, (1, 1, 1), ((1, 1), (1,...]
    ppermute x0 -> x24, waiting for transfers between devices: none -> 40.9 us  [the longest x4 13.1 us: row_halo(): hi = lax.ppermute(for_prev, 'row', [(i + 1, i) for i in range(15)])]
    reshape x3 -> x0, waiting for transfers between devices: 37 us -> none  [the longest x2 36.9 us: conv_same(): kernel = weight.reshape(3, 3, 3, weight.shape[1], weight.shape[2])]
    conv_general_dilated x4 -> x0, matrix products: 27.8 us -> none  [the longest x3 27 us: conv_same(): lax.conv_general_dilated(volume_in[None], kernel, (1, 1, 1), ((1, 1), (1,...]
    convert_element_type x2 -> x0, blocking collectives: 24.4 us -> none  [the longest x1 16.6 us: reference(): coarse = jax.nn.gelu(coarse_raw).astype(jnp.bfloat16)]
    all_gather x0 -> x1, waiting for transfers between devices: none -> 21.8 us  [body(): got = lax.all_gather(packed, 'col', axis=0)]
  transfers between devices with their start and end apart: 20 -> 27, of which waited for: 14 -> 16; matrix products, arithmetic and copies ran while one was open for 12% -> 12% of each run, Pallas kernels for 0% -> 0%
where the time goes in v1:
time: 229 us; the launch traced here: 225 us
  starting transfers between devices  65.6 us (29%)
  waiting for transfers between devices  65.4 us (29%)
  local copies, waits for them, and re-layouts  38.3 us (17%)
  blocking collectives  18 us (8%)
  between operations  14.6 us (6%)
  matrix products  14.1 us (6%)
  other arithmetic  9.53 us (4%)
    all_gather x1, waiting for transfers between devices, body(): got = lax.all_gather(packed, 'col', axis=0)  21.8 us
    all_gather x1, blocking collectives, body(): got = lax.all_gather(c3, 'col', axis=0)  18 us
    ppermute x4, starting transfers between devices, row_halo(): lo = lax.ppermute(for_next, 'row', [(i, i + 1) for i in range(15)])  14.8 us
    ppermute x4, waiting for transfers between devices, row_halo(): hi = lax.ppermute(for_prev, 'row', [(i + 1, i) for i in range(15)])  13.1 us
    all_to_all x2, starting transfers between devices, to_slab(): got = lax.all_to_all(mixed, 'col', 0, 0, tiled=True)  12.4 us
    ppermute x2, waiting for transfers between devices, body(): la, lb = (lax.ppermute(last_kernel, ALL, p) for p in (p1, p2))  11.8 us
    ppermute x4, starting transfers between devices, row_halo(): hi = lax.ppermute(for_prev, 'row', [(i + 1, i) for i in range(15)])  10.2 us
    ppermute x6, waiting for transfers between devices, reduce_tiles(): total = total + lax.ppermute(pair[o].astype(BF), 'col', perm).astype(F32)  9.86 us
  transfers between devices with their start and end apart: 27, of which 16 were waited for; matrix products, arithmetic and copies ran while one was open for 12% of the time, Pallas kernels for 0%

profile of v1, /device:TPU:79, one launch (start us, length us, event | category | flops | bytes accessed | tf_op | source)
XLA Modules:
  0.0 225.5 jit_solution(11649972031807875449)
XLA Ops:
  6.5 2.0 collective-permute-start.3
  8.6 5.7 %collective-permute-start.4 = (bf16[27,16,256]{2,1,0:T(8,128)(2,1)}, bf16[27,16,256]{2,1,0:T(8,128)(2,1)S(1)}, u32[]{:S(2)}, u32[]{:S(2)}) collective-permute-start(bf16[27,16,256]{2,1,0:T(8,128)(2,1)} %param.11), channel_id=1, source_target_pairs={{129,0},{128,1},{194,2},{195,3},{181,4},{180,5},{246,6},{247,7},{1... | collective-permute-start | bytes 663560 | tf_op jit(solution)/shard_map/ppermute | solution.py:125
  14.3 0.9 copy.205
  15.3 1.7 collective-permute-start
  17.0 0.7 fusion.106
  18.1 2.1 collective-permute-done
  20.2 2.3 collective-permute-start.1
  22.4 3.0 %collective-permute-start.2 = (bf16[9,16,256]{2,1,0:T(8,128)(2,1)S(1)}, bf16[9,16,256]{2,1,0:T(8,128)(2,1)S(1)}, u32[]{:S(2)}, u32[]{:S(2)}) collective-permute-start(bf16[9,16,256]{2,1,0:T(8,128)(2,1)S(1)} %get-tuple-element.80), channel_id=1, source_target_pairs={{16,0},{32,16},{48,32},{64,48},{80,64},{96,80},{112,96},{128,112},... | collective-permute-start | bytes 221192 | tf_op jit(solution)/shard_map/ppermute | solution.py:65
  25.5 0.8 collective-permute-done.1
  26.4 5.4 %collective-permute-done.2 = bf16[9,16,256]{2,1,0:T(8,128)(2,1)S(1)} collective-permute-done((bf16[9,16,256]{2,1,0:T(8,128)(2,1)S(1)}, bf16[9,16,256]{2,1,0:T(8,128)(2,1)S(1)}, u32[]{:S(2)}, u32[]{:S(2)}) %collective-permute-start.2) | collective-permute-done | bytes 73760 | tf_op jit(solution)/shard_map/ppermute | solution.py:65
  31.8 1.6 fusion.24
  33.4 7.6 %all-to-all-start = ((bf16[8,144,128]{2,1,0:T(8,128)(2,1)}), bf16[8,144,128]{2,1,0:T(8,128)(2,1)}, u32[]{:S(2)}, u32[]{:S(2)}) async-start(bf16[8,144,128]{2,1,0:T(8,128)(2,1)} %fusion.24), calls=%async_computation | async-start | bytes 589824 | tf_op jit(solution)/shard_map/all_to_all | solution.py:80
  41.3 1.2 copy.128
  42.5 1.6 reshape.437
  44.1 2.7 %all-to-all-done = bf16[8,144,128]{2,1,0:T(8,128)(2,1)} async-done(((bf16[8,144,128]{2,1,0:T(8,128)(2,1)}), bf16[8,144,128]{2,1,0:T(8,128)(2,1)}, u32[]{:S(2)}, u32[]{:S(2)}) %all-to-all-start) | async-done | bytes 294944 | tf_op jit(solution)/shard_map/all_to_all | solution.py:80
  46.8 1.0 copy.199
  49.6 1.5 convolution_bitcast_fusion
  51.1 1.7 fusion.117
  52.8 1.1 collective-permute-start.5
  53.9 5.2 %collective-permute-start.13 = (bf16[27,32,256]{2,1,0:T(8,128)(2,1)}, bf16[27,32,256]{2,1,0:T(8,128)(2,1)}, u32[]{:S(2)}, u32[]{:S(2)}) collective-permute-start(bf16[27,32,256]{2,1,0:T(8,128)(2,1)} %param.15), channel_id=1, source_target_pairs={{0,0},{1,1},{66,2},{67,3},{20,4},{21,5},{86,6},{87,7},{40,8},{41,9... | collective-permute-start | bytes 1327112 | tf_op jit(solution)/shard_map/ppermute | solution.py:126
  59.2 2.9 %copy.144 = bf16[3,3,512,3,64]{2,4,3,1,0:T(8,128)(2,1)} copy(bf16[3,3,512,3,64]{2,4,1,3,0:T(8,128)(2,1)} %bitcast.389) | data formatting | bytes 3538944 | tf_op jit(solution)/shard_map/transpose | solution.py:147
  62.1 2.5 %constant_dynamic-slice_fusion = (bf16[4,512,32]{2,1,0:T(8,128)(2,1)}, bf16[4,512,32]{2,1,0:T(8,128)(2,1)}) fusion(bf16[8,512,256]{2,1,0:T(8,128)(2,1)} %param.14, s32[]{:T(128)S(6)} %add.245, s32[]{:T(128)S(6)} %select_n.400), kind=kLoop, calls=%fused_computation.240 | loop fusion | bytes 524296 | tf_op jit(solution)/shard_map/slice | solution.py:169
  64.6 11.8 %collective-permute-done.13 = bf16[27,32,256]{2,1,0:T(8,128)(2,1)} collective-permute-done((bf16[27,32,256]{2,1,0:T(8,128)(2,1)}, bf16[27,32,256]{2,1,0:T(8,128)(2,1)}, u32[]{:S(2)}, u32[]{:S(2)}) %collective-permute-start.13) | collective-permute-done | bytes 442400 | tf_op jit(solution)/shard_map/ppermute | solution.py:126
  76.4 1.2 broadcast_select_fusion
  77.8 1.2 pad_bitcast_fusion.1
  78.9 1.6 copy_add_fusion
  80.8 2.6 %collective-permute-start.6 = (bf16[8,16,512]{2,1,0:T(8,128)(2,1)S(1)}, bf16[8,16,512]{2,1,0:T(8,128)(2,1)S(1)}, u32[]{:S(2)}, u32[]{:S(2)}) collective-permute-start(bf16[8,16,512]{2,1,0:T(8,128)(2,1)S(1)} %get-tuple-element.29), channel_id=1, source_target_pairs={{0,4},{2,6},{4,8},{6,10},{8,12},{10,14},{12,0},{14,2},{1,5},{3,7},... | collective-permute-start | bytes 393224 | tf_op jit(solution)/shard_map/ppermute | solution.py:117
  83.4 1.1 collective-permute-start.7
  84.6 1.7 collective-permute-start.8
  87.2 2.9 %collective-permute-done.8 = bf16[8,16,512]{2,1,0:T(8,128)(2,1)S(1)} collective-permute-done((bf16[8,16,512]{2,1,0:T(8,128)(2,1)S(1)}, bf16[8,16,512]{2,1,0:T(8,128)(2,1)S(1)}, u32[]{:S(2)}, u32[]{:S(2)}) %collective-permute-start.8) | collective-permute-done | bytes 131104 | tf_op jit(solution)/shard_map/ppermute | solution.py:117
  90.9 1.5 collective-permute-start.9
  92.5 0.9 collective-permute-done.14
  93.4 4.5 %collective-permute-start.15 = (bf16[5,8,512]{2,1,0:T(8,128)(2,1)S(1)}, bf16[5,8,512]{2,1,0:T(8,128)(2,1)S(1)}, u32[]{:S(2)}, u32[]{:S(2)}) collective-permute-start(bf16[5,8,512]{2,1,0:T(8,128)(2,1)S(1)} %get-tuple-element.84), channel_id=1, source_target_pairs={{0,16},{16,32},{32,48},{48,64},{64,80},{80,96},{96,112},{112,128},... | collective-permute-start | bytes 122888 | tf_op jit(solution)/shard_map/ppermute | solution.py:64
  97.9 1.9 collective-permute-start.16
  99.9 7.3 %collective-permute-done.16 = bf16[5,8,512]{2,1,0:T(8,128)(2,1)S(1)} collective-permute-done((bf16[5,8,512]{2,1,0:T(8,128)(2,1)S(1)}, bf16[5,8,512]{2,1,0:T(8,128)(2,1)S(1)}, u32[]{:S(2)}, u32[]{:S(2)}) %collective-permute-start.16) | collective-permute-done | bytes 40992 | tf_op jit(solution)/shard_map/ppermute | solution.py:65
  107.2 18.0 %all-gather = bf16[24,5,8,512]{3,2,1,0:T(8,128)(2,1)S(1)} all-gather(bf16[3,5,8,512]{3,2,1,0:T(8,128)(2,1)S(1)} %pad_maximum_fusion.11), channel_id=2, replica_groups=mesh['row'=16,'col'=8,'depth'=2] {'col'}, dimensions={0}, use_global_device_ids=true | all-gather | bytes 1105920 | tf_op jit(solution)/shard_map/all_gather | solution.py:144
  125.8 1.2 copy-done.2
  129.6 1.3 collective-permute-start.17
  130.9 1.9 collective-permute-start.10
  132.8 3.4 %collective-permute-start.11 = (bf16[9,16,256]{2,1,0:T(8,128)(2,1)S(1)}, bf16[9,16,256]{2,1,0:T(8,128)(2,1)S(1)}, u32[]{:S(2)}, u32[]{:S(2)}) collective-permute-start(bf16[9,16,256]{2,1,0:T(8,128)(2,1)S(1)} %get-tuple-element.78), channel_id=1, source_target_pairs={{16,0},{32,16},{48,32},{64,48},{80,64},{96,80},{112,96},{128,112},... | collective-permute-start | bytes 221192 | tf_op jit(solution)/shard_map/ppermute | solution.py:65
  136.2 6.1 %collective-permute-start.18 = (bf16[5,64,64]{2,1,0:T(8,128)(2,1)S(1)}, bf16[5,64,64]{2,1,0:T(8,128)(2,1)S(1)}, u32[]{:S(2)}, u32[]{:S(2)}) collective-permute-start(bf16[5,64,64]{2,1,0:T(8,128)(2,1)S(1)} %get-tuple-element.82), channel_id=1, source_target_pairs={{0,16},{16,32},{32,48},{48,64},{64,80},{80,96},{96,112},{112,128},... | collective-permute-start | bytes 122888 | tf_op jit(solution)/shard_map/ppermute | solution.py:64
  142.4 1.9 collective-permute-start.19
  144.7 1.6 fusion.21
  146.3 4.8 %all-to-all-start.1 = ((bf16[8,144,128]{2,1,0:T(8,128)(2,1)}), bf16[8,144,128]{2,1,0:T(8,128)(2,1)S(1)}, u32[]{:S(2)}, u32[]{:S(2)}) async-start(bf16[8,144,128]{2,1,0:T(8,128)(2,1)} %fusion.21), calls=%async_computation.1 | async-start | bytes 589824 | tf_op jit(solution)/shard_map/all_to_all | solution.py:80
  151.1 1.2 maximum_bitcast_fusion.2
  152.3 1.2 copy.140
  153.8 1.2 copy.156
  155.0 1.3 copy.174
  156.3 0.9 pad_maximum_fusion.8
  157.7 0.8 copy.149
  159.7 2.9 %fusion.125 = f32[1024,512]{1,0:T(8,128)} fusion(bf16[1024,1152]{1,0:T(8,128)(2,1)S(1)} %constant_dynamic-update-slice_fusion.9, bf16[1152,512]{1,0:T(8,128)(2,1)S(1)} %bitcast.401), kind=kOutput, calls=%fused_computation.265 | convolution fusion | flops 1207959552 | bytes 5636096 | tf_op jit(solution)/shard_map/dot_general | solution.py:104
  162.6 21.8 %all-gather.3.cloned.1.call-done = bf16[8,512,128]{2,1,0:T(8,128)(2,1)} async-done(((bf16[1,512,128]{2,1,0:T(8,128)(2,1)}), bf16[8,512,128]{2,1,0:T(8,128)(2,1)}) %all-gather.3.cloned.1.call-update) | async-done | bytes 1048592 | tf_op jit(solution)/shard_map/all_gather | solution.py:165
  184.3 1.5 copy.150
  185.8 1.1 reshape.427
  186.9 2.9 %copy.151 = bf16[8,2,64,8,64]{4,3,2,1,0:T(8,128)(2,1)} copy(bf16[8,2,64,8,64]{2,0,4,1,3:T(8,128)(2,1)S(1)} %bitcast.364) | data formatting | bytes 2097152 | tf_op jit(solution)/shard_map/transpose | solution.py:166
  189.8 3.3 %reshape.428 = bf16[16,64,512]{2,1,0:T(8,128)(2,1)S(1)} reshape(bf16[8,2,64,8,64]{4,3,2,1,0:T(8,128)(2,1)} %copy.151) | data formatting | bytes 2097152 | tf_op jit(solution)/shard_map/reshape | solution.py:166
  195.7 1.6 copy.153
  202.3 1.5 convolution_add_fusion
  204.7 2.4 %collective-permute-done.20 = f32[4,8,16,512]{3,2,1,0:T(8,128)S(1)} collective-permute-done((f32[4,8,16,512]{3,2,1,0:T(8,128)S(1)}, f32[4,8,16,512]{3,2,1,0:T(8,128)S(1)}, u32[]{:S(2)}, u32[]{:S(2)}) %collective-permute-start.20) | collective-permute-done | bytes 1048608 | tf_op jit(solution)/shard_map/ppermute | solution.py:112
  207.8 1.6 collective-permute-start.21
  209.9 1.7 collective-permute-start.23
  211.6 1.8 collective-permute-done.21
  213.9 3.8 %collective-permute-done.23 = bf16[8,16,512]{2,1,0:T(8,128)(2,1)S(1)} collective-permute-done((bf16[8,16,512]{2,1,0:T(8,128)(2,1)S(1)}, bf16[8,16,512]{2,1,0:T(8,128)(2,1)S(1)}, u32[]{:S(2)}, u32[]{:S(2)}) %collective-permute-start.23) | collective-permute-done | bytes 131104 | tf_op jit(solution)/shard_map/ppermute | solution.py:117
  217.9 0.7 copy.204
  (158 shorter events, 20.0 us)
Async XLA Ops:
  6.5 83.8 %copy-start = (bf16[8,256,512]{2,1,0:T(8,128)(2,1)S(1)}, bf16[8,256,512]{2,1,0:T(8,128)(2,1)}, u32[]{:S(2)}) copy-start(bf16[8,256,512]{2,1,0:T(8,128)(2,1)} %param.12) | copy-start | bytes 6291460
  6.5 34.5 %collective-permute-start.3 = (bf16[27,16,256]{2,1,0:T(8,128)(2,1)}, bf16[27,16,256]{2,1,0:T(8,128)(2,1)S(1)}, u32[]{:S(2)}, u32[]{:S(2)}) collective-permute-start(bf16[27,16,256]{2,1,0:T(8,128)(2,1)} %param.11), channel_id=1, source_target_pairs={{0,0},{1,1},{66,2},{67,3},{20,4},{21,5},{86,6},{87,7},{40,8},{41,9... | collective-permute-start | bytes 663560 | tf_op jit(solution)/shard_map/ppermute | solution.py:125
  8.6 32.4 %collective-permute-start.4 = (bf16[27,16,256]{2,1,0:T(8,128)(2,1)}, bf16[27,16,256]{2,1,0:T(8,128)(2,1)S(1)}, u32[]{:S(2)}, u32[]{:S(2)}) collective-permute-start(bf16[27,16,256]{2,1,0:T(8,128)(2,1)} %param.11), channel_id=1, source_target_pairs={{129,0},{128,1},{194,2},{195,3},{181,4},{180,5},{246,6},{247,7},{1... | collective-permute-start | bytes 663560 | tf_op jit(solution)/shard_map/ppermute | solution.py:125
  15.3 4.9 %collective-permute-start = (bf16[2,16,256]{2,1,0:T(8,128)(2,1)S(1)}, bf16[2,16,256]{2,1,0:T(8,128)(2,1)S(1)}, u32[]{:S(2)}, u32[]{:S(2)}) collective-permute-start(bf16[2,16,256]{2,1,0:T(8,128)(2,1)S(1)} %fusion.104), channel_id=1, source_target_pairs={{0,1},{1,0},{2,3},{3,2},{4,5},{5,4},{6,7},{7,6},{8,9},{9,8},{10,11... | collective-permute-start | bytes 49160 | tf_op jit(solution)/shard_map/ppermute | solution.py:60
  20.2 6.2 %collective-permute-start.1 = (bf16[9,16,256]{2,1,0:T(8,128)(2,1)S(1)}, bf16[9,16,256]{2,1,0:T(8,128)(2,1)S(1)}, u32[]{:S(2)}, u32[]{:S(2)}) collective-permute-start(bf16[9,16,256]{2,1,0:T(8,128)(2,1)S(1)} %get-tuple-element.79), channel_id=1, source_target_pairs={{0,16},{16,32},{32,48},{48,64},{64,80},{80,96},{96,112},{112,128},... | collective-permute-start | bytes 221192 | tf_op jit(solution)/shard_map/ppermute | solution.py:64
  22.4 9.4 %collective-permute-start.2 = (bf16[9,16,256]{2,1,0:T(8,128)(2,1)S(1)}, bf16[9,16,256]{2,1,0:T(8,128)(2,1)S(1)}, u32[]{:S(2)}, u32[]{:S(2)}) collective-permute-start(bf16[9,16,256]{2,1,0:T(8,128)(2,1)S(1)} %get-tuple-element.80), channel_id=1, source_target_pairs={{16,0},{32,16},{48,32},{64,48},{80,64},{96,80},{112,96},{128,112},... | collective-permute-start | bytes 221192 | tf_op jit(solution)/shard_map/ppermute | solution.py:65
  33.4 13.4 %all-to-all-start = ((bf16[8,144,128]{2,1,0:T(8,128)(2,1)}), bf16[8,144,128]{2,1,0:T(8,128)(2,1)}, u32[]{:S(2)}, u32[]{:S(2)}) async-start(bf16[8,144,128]{2,1,0:T(8,128)(2,1)} %fusion.24), calls=%async_computation | async-start | bytes 589824 | tf_op jit(solution)/shard_map/all_to_all | solution.py:80
  48.3 1.3 copy-start.8
  52.8 26.1 %collective-permute-start.5 = (f32[4,8,16,512]{3,2,0,1:T(8,128)}, f32[4,8,16,512]{3,2,0,1:T(8,128)}, u32[]{:S(2)}, u32[]{:S(2)}) collective-permute-start(f32[4,8,16,512]{3,2,0,1:T(8,128)} %get-tuple-element.13), channel_id=1, source_target_pairs={{0,2},{2,0},{4,6},{6,4},{8,10},{10,8},{12,14},{14,12},{1,3},{3,1},... | collective-permute-start | bytes 3145736 | tf_op jit(solution)/shard_map/ppermute | solution.py:112
  53.9 10.7 %collective-permute-start.12 = (bf16[27,32,256]{2,1,0:T(8,128)(2,1)}, bf16[27,32,256]{2,1,0:T(8,128)(2,1)}, u32[]{:S(2)}, u32[]{:S(2)}) collective-permute-start(bf16[27,32,256]{2,1,0:T(8,128)(2,1)} %param.15), channel_id=1, source_target_pairs={{129,0},{128,1},{194,2},{195,3},{181,4},{180,5},{246,6},{247,7},{1... | collective-permute-start | bytes 1327112 | tf_op jit(solution)/shard_map/ppermute | solution.py:126
  53.9 22.5 %collective-permute-start.13 = (bf16[27,32,256]{2,1,0:T(8,128)(2,1)}, bf16[27,32,256]{2,1,0:T(8,128)(2,1)}, u32[]{:S(2)}, u32[]{:S(2)}) collective-permute-start(bf16[27,32,256]{2,1,0:T(8,128)(2,1)} %param.15), channel_id=1, source_target_pairs={{0,0},{1,1},{66,2},{67,3},{20,4},{21,5},{86,6},{87,7},{40,8},{41,9... | collective-permute-start | bytes 1327112 | tf_op jit(solution)/shard_map/ppermute | solution.py:126
  64.6 14.3 %copy-start.5 = (f32[1,4,8,16,512]{4,3,0,1,2:T(8,128)S(1)}, f32[1,4,8,16,512]{4,3,0,1,2:T(8,128)}, u32[]{:S(2)}) copy-start(f32[1,4,8,16,512]{4,3,0,1,2:T(8,128)} %get-tuple-element.14) | copy-start | bytes 3145732
  80.8 6.0 %collective-permute-start.6 = (bf16[8,16,512]{2,1,0:T(8,128)(2,1)S(1)}, bf16[8,16,512]{2,1,0:T(8,128)(2,1)S(1)}, u32[]{:S(2)}, u32[]{:S(2)}) collective-permute-start(bf16[8,16,512]{2,1,0:T(8,128)(2,1)S(1)} %get-tuple-element.29), channel_id=1, source_target_pairs={{0,4},{2,6},{4,8},{6,10},{8,12},{10,14},{12,0},{14,2},{1,5},{3,7},... | collective-permute-start | bytes 393224 | tf_op jit(solution)/shard_map/ppermute | solution.py:117
  83.4 3.8 %collective-permute-start.7 = (bf16[8,16,512]{2,1,0:T(8,128)(2,1)S(1)}, bf16[8,16,512]{2,1,0:T(8,128)(2,1)S(1)}, u32[]{:S(2)}, u32[]{:S(2)}) collective-permute-start(bf16[8,16,512]{2,1,0:T(8,128)(2,1)S(1)} %get-tuple-element.31), channel_id=1, source_target_pairs={{0,12},{2,14},{4,0},{6,2},{8,4},{10,6},{12,8},{14,10},{1,13},{3,15... | collective-permute-start | bytes 393224 | tf_op jit(solution)/shard_map/ppermute | solution.py:117
  84.6 5.6 %collective-permute-start.8 = (bf16[8,16,512]{2,1,0:T(8,128)(2,1)S(1)}, bf16[8,16,512]{2,1,0:T(8,128)(2,1)S(1)}, u32[]{:S(2)}, u32[]{:S(2)}) collective-permute-start(bf16[8,16,512]{2,1,0:T(8,128)(2,1)S(1)} %get-tuple-element.30), channel_id=1, source_target_pairs={{0,8},{2,10},{4,12},{6,14},{8,0},{10,2},{12,4},{14,6},{1,9},{3,11}... | collective-permute-start | bytes 393224 | tf_op jit(solution)/shard_map/ppermute | solution.py:117
  90.8 2.6 %collective-permute-start.14 = (bf16[8,512]{1,0:T(8,128)(2,1)S(1)}, bf16[8,512]{1,0:T(8,128)(2,1)S(1)}, u32[]{:S(2)}, u32[]{:S(2)}) collective-permute-start(bf16[8,512]{1,0:T(8,128)(2,1)S(1)} %fusion.105), channel_id=1, source_target_pairs={{0,1},{1,0},{2,3},{3,2},{4,5},{5,4},{6,7},{7,6},{8,9},{9,8},{10,11... | collective-permute-start | bytes 24584 | tf_op jit(solution)/shard_map/ppermute | solution.py:60
  90.9 8.9 %collective-permute-start.9 = (bf16[2,16,256]{2,1,0:T(8,128)(2,1)S(1)}, bf16[2,16,256]{2,1,0:T(8,128)(2,1)S(1)}, u32[]{:S(2)}, u32[]{:S(2)}) collective-permute-start(bf16[2,16,256]{2,1,0:T(8,128)(2,1)S(1)} %fusion.103), channel_id=1, source_target_pairs={{0,1},{1,0},{2,3},{3,2},{4,5},{5,4},{6,7},{7,6},{8,9},{9,8},{10,11... | collective-permute-start | bytes 49160 | tf_op jit(solution)/shard_map/ppermute | solution.py:60
  93.4 6.5 %collective-permute-start.15 = (bf16[5,8,512]{2,1,0:T(8,128)(2,1)S(1)}, bf16[5,8,512]{2,1,0:T(8,128)(2,1)S(1)}, u32[]{:S(2)}, u32[]{:S(2)}) collective-permute-start(bf16[5,8,512]{2,1,0:T(8,128)(2,1)S(1)} %get-tuple-element.84), channel_id=1, source_target_pairs={{0,16},{16,32},{32,48},{48,64},{64,80},{80,96},{96,112},{112,128},... | collective-permute-start | bytes 122888 | tf_op jit(solution)/shard_map/ppermute | solution.py:64
  97.9 9.2 %collective-permute-start.16 = (bf16[5,8,512]{2,1,0:T(8,128)(2,1)S(1)}, bf16[5,8,512]{2,1,0:T(8,128)(2,1)S(1)}, u32[]{:S(2)}, u32[]{:S(2)}) collective-permute-start(bf16[5,8,512]{2,1,0:T(8,128)(2,1)S(1)} %get-tuple-element.84), channel_id=1, source_target_pairs={{16,0},{32,16},{48,32},{64,48},{80,64},{96,80},{112,96},{128,112},... | collective-permute-start | bytes 122888 | tf_op jit(solution)/shard_map/ppermute | solution.py:65
  125.6 1.5 copy-start.2
  129.4 21.6 %copy-start.6 = (bf16[4,9,32,1,256]{4,2,1,0,3:T(8,128)(2,1)S(1)}, bf16[4,9,32,1,256]{4,2,1,0,3:T(8,128)(2,1)}, u32[]{:S(2)}) copy-start(bf16[4,9,32,1,256]{4,2,1,0,3:T(8,128)(2,1)} %get-tuple-element.32) | copy-start | bytes 1769476
  129.6 6.6 %collective-permute-start.17 = (bf16[64,64]{1,0:T(8,128)(2,1)S(1)}, bf16[64,64]{1,0:T(8,128)(2,1)S(1)}, u32[]{:S(2)}, u32[]{:S(2)}) collective-permute-start(bf16[64,64]{1,0:T(8,128)(2,1)S(1)} %fusion.102), channel_id=1, source_target_pairs={{0,1},{1,0},{2,3},{3,2},{4,5},{5,4},{6,7},{7,6},{8,9},{9,8},{10,11... | collective-permute-start | bytes 24584 | tf_op jit(solution)/shard_map/ppermute | solution.py:60
  130.9 13.4 %collective-permute-start.10 = (bf16[9,16,256]{2,1,0:T(8,128)(2,1)S(1)}, bf16[9,16,256]{2,1,0:T(8,128)(2,1)S(1)}, u32[]{:S(2)}, u32[]{:S(2)}) collective-permute-start(bf16[9,16,256]{2,1,0:T(8,128)(2,1)S(1)} %get-tuple-element.77), channel_id=1, source_target_pairs={{0,16},{16,32},{32,48},{48,64},{64,80},{80,96},{96,112},{112,128},... | collective-permute-start | bytes 221192 | tf_op jit(solution)/shard_map/ppermute | solution.py:64
  132.8 11.9 %collective-permute-start.11 = (bf16[9,16,256]{2,1,0:T(8,128)(2,1)S(1)}, bf16[9,16,256]{2,1,0:T(8,128)(2,1)S(1)}, u32[]{:S(2)}, u32[]{:S(2)}) collective-permute-start(bf16[9,16,256]{2,1,0:T(8,128)(2,1)S(1)} %get-tuple-element.78), channel_id=1, source_target_pairs={{16,0},{32,16},{48,32},{64,48},{80,64},{96,80},{112,96},{128,112},... | collective-permute-start | bytes 221192 | tf_op jit(solution)/shard_map/ppermute | solution.py:65
  136.2 20.1 %collective-permute-start.18 = (bf16[5,64,64]{2,1,0:T(8,128)(2,1)S(1)}, bf16[5,64,64]{2,1,0:T(8,128)(2,1)S(1)}, u32[]{:S(2)}, u32[]{:S(2)}) collective-permute-start(bf16[5,64,64]{2,1,0:T(8,128)(2,1)S(1)} %get-tuple-element.82), channel_id=1, source_target_pairs={{0,16},{16,32},{32,48},{48,64},{64,80},{80,96},{96,112},{112,128},... | collective-permute-start | bytes 122888 | tf_op jit(solution)/shard_map/ppermute | solution.py:64
  142.4 13.9 %collective-permute-start.19 = (bf16[5,64,64]{2,1,0:T(8,128)(2,1)S(1)}, bf16[5,64,64]{2,1,0:T(8,128)(2,1)}, u32[]{:S(2)}, u32[]{:S(2)}) collective-permute-start(bf16[5,64,64]{2,1,0:T(8,128)(2,1)S(1)} %get-tuple-element.82), channel_id=1, source_target_pairs={{16,0},{32,16},{48,32},{64,48},{80,64},{96,80},{112,96},{128,112},... | collective-permute-start | bytes 122888 | tf_op jit(solution)/shard_map/ppermute | solution.py:65
  146.3 12.2 %all-to-all-start.1 = ((bf16[8,144,128]{2,1,0:T(8,128)(2,1)}), bf16[8,144,128]{2,1,0:T(8,128)(2,1)S(1)}, u32[]{:S(2)}, u32[]{:S(2)}) async-start(bf16[8,144,128]{2,1,0:T(8,128)(2,1)} %fusion.21), calls=%async_computation.1 | async-start | bytes 589824 | tf_op jit(solution)/shard_map/all_to_all | solution.py:80
  151.1 33.2 %all-gather.3.cloned.1.call-start = ((), (), s32[]{:S(2)}) async-start(), calls=%async_computation.2 | async-start | bytes 1179648 | tf_op jit(solution)/shard_map/all_gather | solution.py:165
  189.8 3.3 %copy-start.4 = (bf16[4,512,32]{2,1,0:T(8,128)(2,1)S(1)}, bf16[4,512,32]{2,1,0:T(8,128)(2,1)}, u32[]{:S(2)}) copy-start(bf16[4,512,32]{2,1,0:T(8,128)(2,1)} %get-tuple-element.10) | copy-start | bytes 393220
  189.8 4.5 %copy-start.3 = (bf16[4,512,32]{2,1,0:T(8,128)(2,1)S(1)}, bf16[4,512,32]{2,1,0:T(8,128)(2,1)}, u32[]{:S(2)}) copy-start(bf16[4,512,32]{2,1,0:T(8,128)(2,1)} %get-tuple-element.11) | copy-start | bytes 393220
  200.3 1.3 copy-start.7
  200.3 2.0 copy-start.9
  204.3 2.7 %collective-permute-start.20 = (f32[4,8,16,512]{3,2,1,0:T(8,128)S(1)}, f32[4,8,16,512]{3,2,1,0:T(8,128)S(1)}, u32[]{:S(2)}, u32[]{:S(2)}) collective-permute-start(f32[4,8,16,512]{3,2,1,0:T(8,128)S(1)} %select_bitcast_fusion), channel_id=1, source_target_pairs={{0,2},{2,0},{4,6},{6,4},{8,10},{10,8},{12,14},{14,12},{1,3},{3,1},... | collective-permute-start | bytes 3145736 | tf_op jit(solution)/shard_map/ppermute | solution.py:112
  207.1 11.6 %copy-start.1 = (bf16[8,256,512]{2,1,0:T(8,128)(2,1)S(1)}, bf16[8,256,512]{2,1,0:T(8,128)(2,1)}, u32[]{:S(2)}) copy-start(bf16[8,256,512]{2,1,0:T(8,128)(2,1)} %param.12) | copy-start | bytes 6291460
  207.8 5.6 %collective-permute-start.21 = (bf16[8,16,512]{2,1,0:T(8,128)(2,1)S(1)}, bf16[8,16,512]{2,1,0:T(8,128)(2,1)S(1)}, u32[]{:S(2)}, u32[]{:S(2)}) collective-permute-start(bf16[8,16,512]{2,1,0:T(8,128)(2,1)S(1)} %get-tuple-element.26), channel_id=1, source_target_pairs={{0,4},{2,6},{4,8},{6,10},{8,12},{10,14},{12,0},{14,2},{1,5},{3,7},... | collective-permute-start | bytes 393224 | tf_op jit(solution)/shard_map/ppermute | solution.py:117
  209.4 4.5 %collective-permute-start.22 = (bf16[8,16,512]{2,1,0:T(8,128)(2,1)S(1)}, bf16[8,16,512]{2,1,0:T(8,128)(2,1)S(1)}, u32[]{:S(2)}, u32[]{:S(2)}) collective-permute-start(bf16[8,16,512]{2,1,0:T(8,128)(2,1)S(1)} %get-tuple-element.28), channel_id=1, source_target_pairs={{0,12},{2,14},{4,0},{6,2},{8,4},{10,6},{12,8},{14,10},{1,13},{3,15... | collective-permute-start | bytes 393224 | tf_op jit(solution)/shard_map/ppermute | solution.py:117
  209.9 7.8 %collective-permute-start.23 = (bf16[8,16,512]{2,1,0:T(8,128)(2,1)S(1)}, bf16[8,16,512]{2,1,0:T(8,128)(2,1)S(1)}, u32[]{:S(2)}, u32[]{:S(2)}) collective-permute-start(bf16[8,16,512]{2,1,0:T(8,128)(2,1)S(1)} %get-tuple-element.27), channel_id=1, source_target_pairs={{0,8},{2,10},{4,12},{6,14},{8,0},{10,2},{12,4},{14,6},{1,9},{3,11}... | collective-permute-start | bytes 393224 | tf_op jit(solution)/shard_map/ppermute | solution.py:117
Sparse Core Ops, SparseCore 0:
  158.6 25.6 all-gather.2

commit v2 on v1

--- a/solution.py
+++ b/solution.py
@@ -1,9 +1,9 @@
-import functools
-
 import jax
 import jax.numpy as jnp
 import numpy as np
 from jax import lax
+from jax.experimental import pallas as pl
+from jax.experimental.pallas import tpu as pltpu
 from jax.sharding import PartitionSpec as P
 
 BF = jnp.bfloat16
@@ -49,6 +49,14 @@
     return first, skip
 
 
+def lift_table():
+    places = np.zeros((16, 8), np.int32)
+    for r in range(16):
+        for j in range(8):
+            places[r, j] = min(shards_of(r, j))
+    return places
+
+
 def pick(table_row):
     want = jnp.tile(table_row.reshape(8, 1, 32), (1, 4, 1)).reshape(8, 128)
     want = want + (256 * (jnp.arange(128) // 32))[None, :]
@@ -102,6 +110,35 @@
     cols = [pad[c : c + 8, b : b + 128] for b in range(3) for c in range(3)]
     patches = jnp.concatenate(cols, -1).reshape(1024, 1152)
     return jnp.dot(patches, wt.reshape(1152, 512), preferred_element_type=F32)
+
+
+def mid_body(slab_ref, w_ref, prev_ref, own_ref, next_ref):
+    y = lax.broadcasted_iota(jnp.int32, (320, 64), 0) % 64
+    near = [slab_ref[c : c + 5].reshape(320, 512) for c in range(3)]
+    for a, out in enumerate((prev_ref, own_ref, next_ref)):
+        total = jnp.zeros((320, 64), F32)
+        for b in range(3):
+            g = jnp.zeros((320, 64), F32)
+            for c in range(3):
+                g = g + jnp.dot(near[c], w_ref[9 * a + 3 * b + c], preferred_element_type=F32)
+            if b == 0:
+                g = jnp.where(y == 0, 0.0, pltpu.roll(g, 1, 0))
+            if b == 2:
+                g = jnp.where(y == 63, 0.0, pltpu.roll(g, 319, 0))
+            total = total + g
+        out[...] = total.reshape(5, 64, 64).astype(out.dtype)
+
+
+def mid_taps(slab, w):
+    whole = pl.BlockSpec(memory_space=pltpu.VMEM)
+    return pl.pallas_call(
+        mid_body,
+        in_specs=[whole] * 2,
+        out_specs=[whole] * 3,
+        out_shape=[jax.ShapeDtypeStruct((5, 64, 64), t) for t in (BF, F32, BF)],
+        compiler_params=pltpu.CompilerParams(vmem_limit_bytes=24 << 20),
+        name="mid_taps",
+    )(slab, w)
 
 
 def reduce_tiles(acc, j):
@@ -123,56 +160,66 @@
     p1, p2 = shard_perms()
     first_table, skip_table = (jnp.asarray(t) for t in tables())
     w1 = jnp.concatenate([lax.ppermute(first_kernel, ALL, p) for p in (p1, p2)], 1)
-    la, lb = (lax.ppermute(last_kernel, ALL, p) for p in (p1, p2))
     in_low = (r // 4 + j % 2) % 4 < 2
-    w_lift, w_skip = jnp.where(in_low, la, lb), jnp.where(in_low, lb, la)
-    base = (jnp.where(in_low, 0, 2) + r // 4 + j % 2) % 4 * 4
-    lift_at = base + (r % 4 + jnp.where(in_low, j // 2, -(j // 2))) % 4
 
     tile = volume.transpose(0, 2, 1, 3)
-    planes = to_slab(fine_halo(tile, d), pick(first_table[r]), d)
+    t4, w1, last_kernel = lax.optimization_barrier((fine_halo(tile, d), w1, last_kernel))
+    la = lax.ppermute(last_kernel, ALL, p1)
+    lb = lax.ppermute(last_kernel, ALL, p2)
+    planes = to_slab(t4, pick(first_table[r]), d)
     part = slab_conv(planes, slab_weights(w1))
     skip = jax.nn.gelu(reduce_tiles(part, j)).astype(BF).reshape(8, 16, 2, 256)
 
     cells = skip.reshape(4, 2, 8, 2, 2, 256)
     down = down_kernel.reshape(2, 2, 2, 256, 512)
     coarse = jax.nn.gelu(jnp.einsum("kcjbae,abceo->kjo", cells, down, preferred_element_type=F32)).astype(BF)
-    recv = edge_swap(coarse[0], coarse[3], d)
-    c5 = jnp.concatenate([coarse, recv[None]], 0)
-    lo, hi = row_halo(c5, c5)
-    c3 = jnp.stack([lo, c5, hi])
-    got = lax.all_gather(c3, "col", axis=0)
-    slab = got.transpose(1, 2, 0, 3, 4).reshape(3, 5, 64, 512)
-    slab = jnp.stack([z_ends(slab[a], d) for a in range(3)])
-    wm = mid_kernel.reshape(3, 3, 3, 512, 64).transpose(0, 2, 3, 1, 4).reshape(9, 512, 192)
-    g = sum(
-        jnp.dot(slab[a, c : c + 4].reshape(256, 512), wm[3 * a + c], preferred_element_type=F32)
-        for a in range(3)
-        for c in range(3)
+    send = jnp.where(d == 0, coarse[2:], coarse[:2])
+    recv = lax.ppermute(send, "depth", [(0, 1), (1, 0)])
+    got = lax.all_gather(jnp.concatenate([coarse, recv], 0), "col", axis=0)
+    got = got.transpose(1, 0, 2, 3).reshape(6, 64, 512)
+    none = jnp.zeros((1, 64, 512), BF)
+    slab = jnp.where(
+        d == 0, jnp.concatenate([none, got], 0), jnp.concatenate([got[4:], got[:4], none], 0)
     )
-    g = jnp.pad(g.reshape(4, 64, 192), ((0, 0), (1, 1), (0, 0)))
-    middle = jax.nn.gelu(g[:, 0:64, 0:64] + g[:, 1:65, 64:128] + g[:, 2:66, 128:192]).astype(BF)
+    h = mid_taps(slab, mid_kernel)
+    lo, hi = row_halo(h[0], h[2])
+    middle = jax.nn.gelu(h[1] + lo.astype(F32) + hi.astype(F32)).astype(BF)
 
     slab_skip = to_slab(fine_halo(skip.transpose(2, 0, 1, 3), d), pick(skip_table[r]), d)
+
+    middle, la, lb, slab_skip = lax.optimization_barrier((middle, la, lb, slab_skip))
+    w_lift, w_skip = jnp.where(in_low, la, lb), jnp.where(in_low, lb, la)
     part = slab_conv(slab_skip, slab_weights(w_skip))
 
-    recv = edge_swap(middle[0], middle[3], d)
-    m5 = jnp.concatenate([middle, recv[None]], 0)
-    lo, hi = row_halo(m5, m5)
-    m3 = jnp.stack([lo, m5, hi])
-    packed = jnp.concatenate([m3.reshape(15, 64, 64), jnp.zeros((1, 64, 64), BF)], 0)
-    packed = packed.reshape(8, 2, 64, 64).transpose(0, 2, 1, 3).reshape(512, 128)
+    packed = jnp.concatenate([middle, jnp.zeros((1, 64, 64), BF)], 0)
+    packed = packed.reshape(3, 2, 64, 64).transpose(0, 2, 1, 3).reshape(3, 64, 128)
     got = lax.all_gather(packed, "col", axis=0)
-    got = got.reshape(8, 8, 64, 2, 64).transpose(1, 3, 2, 0, 4).reshape(16, 64, 512)[:15].reshape(3, 5, 64, 512)
-    up = lax.dynamic_slice(up_kernel, (0, 0, 32 * lift_at), (8, 512, 32)).reshape(2, 2, 2, 512, 32)
-    rows = [
-        jnp.einsum("kye,bceo->kcybo", got[m], up[a], preferred_element_type=F32).astype(BF)
-        for m, a in ((0, 1), (1, 0), (1, 1), (2, 0))
-    ]
-    lift = jnp.stack(rows, -2).reshape(5, 2, 128, 128)
-    own = lift[:4].reshape(8, 128, 128)
-    end = jnp.where(d == 0, lift[4, 0], lift[4, 1])[None]
-    planes = z_ends(jnp.concatenate([own, end], 0), d)
+    got = got.transpose(1, 2, 0, 3).reshape(192, 1024)
+    places = jnp.asarray(lift_table())
+
+    def cut(row):
+        at = places[jnp.clip(row, 0, 15), j]
+        return lax.dynamic_slice(up_kernel, (0, 0, 32 * at), (8, 512, 32)).reshape(2, 2, 2, 8, 64, 32)
+
+    mine = cut(r)
+    up = jnp.stack([cut(r - 1)[0], mine[0], mine[1], cut(r + 1)[1]])
+    up = up.transpose(3, 4, 1, 2, 0, 5).reshape(8, 64, 2, 2, 128)
+    zero = jnp.zeros_like(up)
+    up = jnp.stack([jnp.stack([up, zero], 2), jnp.stack([zero, up], 2)], 1)
+    lift = jnp.dot(got, up.reshape(1024, 1024), preferred_element_type=F32).astype(BF)
+    lift = lift.reshape(3, 64, 2, 2, 2, 128).transpose(0, 2, 4, 1, 3, 5).reshape(12, 128, 128)
+    none = jnp.zeros((1, 128, 128), BF)
+    lift = jnp.where(d == 0, jnp.concatenate([none, lift[:9]], 0), jnp.concatenate([lift[1:10], none], 0))
+
+    def pack(v):
+        v = jnp.concatenate([v, jnp.zeros((2, 128, 32), BF)], 0)
+        return v.reshape(3, 4, 128, 32).transpose(0, 2, 1, 3).reshape(3, 128, 128)
+
+    def unpack(v):
+        return v.reshape(3, 128, 4, 32).transpose(0, 2, 1, 3).reshape(12, 128, 32)[:10]
+
+    lo, hi = row_halo(pack(lift[..., 96:]), pack(lift[..., :32]))
+    planes = jnp.concatenate([unpack(lo), lift[..., 32:96], unpack(hi)], -1)
     part = part + slab_conv(planes, slab_weights(w_lift))
     out = jax.nn.gelu(reduce_tiles(part, j)).astype(BF).reshape(8, 16, 2, 256)
     return out.transpose(2, 1, 0, 3)

time: 229 us -> 223 us (0.974)
  waiting for transfers between devices: 65.4 us -> 45.9 us
  between operations: 14.6 us -> 3 us
  local copies, waits for them, and re-layouts: 38.3 us -> 49.2 us
  blocking collectives: 18 us -> 27.1 us
  other arithmetic: 9.53 us -> 12.8 us
  Pallas kernels: 0 us -> 2.47 us
  matrix products: 14.1 us -> 11.7 us
    all_gather x1 -> x0, waiting for transfers between devices: 21.8 us -> none  [body(): got = lax.all_gather(packed, 'col', axis=0)]
    all_gather x1 -> x2, blocking collectives: 18 us -> 27.1 us  [the longest x1 15 us: body(): got = lax.all_gather(jnp.concatenate([coarse, recv], 0), 'col', axis=0)]
    another operation x1 -> x5, local copies, waits for them, and re-layouts: 1.65 us -> 10.1 us  [the longest x2 9.82 us: body(): up = jnp.stack([jnp.stack([up, zero], 2), jnp.stack([zero, up], 2)], 1)]
    slice x6 -> x12, local copies, waits for them, and re-layouts: 3.5 us -> 11.2 us  [the longest x5 10.6 us: body(): up = jnp.stack([cut(r - 1)[0], mine[0], mine[1], cut(r + 1)[1]])]
    ppermute x4, starting transfers between devices: 14.8 us -> 22.4 us  [row_halo(): lo = lax.ppermute(for_next, 'row', [(i, i + 1) for i in range(15)])]
    ppermute x2 -> x3, waiting for transfers between devices: 11.8 us -> 18.7 us  [the longest x1 13 us: body(): la = lax.ppermute(last_kernel, ALL, p1)]
    transpose x2 -> x1, local copies, waits for them, and re-layouts: 5.78 us -> 0.26 us  [body(): got = got.transpose(1, 2, 0, 3).reshape(192, 1024)]
    another operation x10 -> x6, other arithmetic: 1.9 us -> 7.2 us  [the longest x1 5.15 us: body(): up = jnp.stack([jnp.stack([up, zero], 2), jnp.stack([zero, up], 2)], 1)]
  transfers between devices with their start and end apart: 27 -> 25, of which waited for: 16 -> 13; matrix products, arithmetic and copies ran while one was open for 12% -> 24% of each run, Pallas kernels for 0% -> 1%
where the time goes in v2:
time: 223 us; the launch traced here: 220 us
  starting transfers between devices  67.5 us (30%)
  local copies, waits for them, and re-layouts  49.2 us (22%)
  waiting for transfers between devices  45.9 us (21%)
  blocking collectives  27.1 us (12%)
  other arithmetic  12.8 us (6%)
  matrix products  11.7 us (5%)
  between operations  3 us (1%)
  Pallas kernels  2.47 us (1%)
    ppermute x4, starting transfers between devices, row_halo(): lo = lax.ppermute(for_next, 'row', [(i, i + 1) for i in range(15)])  22.4 us
    all_gather x1, blocking collectives, body(): got = lax.all_gather(jnp.concatenate([coarse, recv], 0), 'col', axis=0)  15 us
    ppermute x1, waiting for transfers between devices, body(): la = lax.ppermute(last_kernel, ALL, p1)  13 us
    all_gather x1, blocking collectives, body(): got = lax.all_gather(packed, 'col', axis=0)  12 us
    unnamed x44, local copies, waits for them, and re-layouts  10.8 us
    ppermute x6, waiting for transfers between devices, reduce_tiles(): total = total + lax.ppermute(pair[o].astype(BF), 'col', perm).astype(F32)  10.7 us
    slice x5, local copies, waits for them, and re-layouts, body(): up = jnp.stack([cut(r - 1)[0], mine[0], mine[1], cut(r + 1)[1]])  10.6 us
    another operation x2, local copies, waits for them, and re-layouts, body(): up = jnp.stack([jnp.stack([up, zero], 2), jnp.stack([zero, up], 2)], 1)  9.82 us
  transfers between devices with their start and end apart: 25, of which 13 were waited for; matrix products, arithmetic and copies ran while one was open for 24% of the time, Pallas kernels for 1%

profile of v2, /device:TPU:79, one launch (start us, length us, event | category | flops | bytes accessed | tf_op | source)
XLA Modules:
  0.0 219.7 jit_solution(7027376379435215691)
XLA Ops:
  0.0 4.1 %collective-permute-start.4 = (bf16[27,16,256]{2,1,0:T(8,128)(2,1)}, bf16[27,16,256]{2,1,0:T(8,128)(2,1)S(1)}, u32[]{:S(2)}, u32[]{:S(2)}) collective-permute-start(bf16[27,16,256]{2,1,0:T(8,128)(2,1)} %param.12), channel_id=1, source_target_pairs={{129,0},{128,1},{194,2},{195,3},{181,4},{180,5},{246,6},{247,7},{1... | collective-permute-start | bytes 663560 | tf_op jit(solution)/shard_map/ppermute | solution.py:162
  4.1 1.9 collective-permute-start.3
  6.0 0.9 copy.186
  7.0 0.9 collective-permute-start
  7.9 0.7 fusion.94
  8.9 3.4 %collective-permute-done = bf16[2,16,256]{2,1,0:T(8,128)(2,1)S(1)} collective-permute-done((bf16[2,16,256]{2,1,0:T(8,128)(2,1)S(1)}, bf16[2,16,256]{2,1,0:T(8,128)(2,1)S(1)}, u32[]{:S(2)}, u32[]{:S(2)}) %collective-permute-start) | collective-permute-done | bytes 16416 | tf_op jit(solution)/shard_map/ppermute | solution.py:68
  12.3 6.5 %collective-permute-start.1 = (bf16[9,16,256]{2,1,0:T(8,128)(2,1)S(1)}, bf16[9,16,256]{2,1,0:T(8,128)(2,1)S(1)}, u32[]{:S(2)}, u32[]{:S(2)}) collective-permute-start(bf16[9,16,256]{2,1,0:T(8,128)(2,1)S(1)} %get-tuple-element.73), channel_id=1, source_target_pairs={{0,16},{16,32},{32,48},{48,64},{64,80},{80,96},{96,112},{112,128},... | collective-permute-start | bytes 221192 | tf_op jit(solution)/shard_map/ppermute | solution.py:72
  18.8 1.9 collective-permute-start.2
  20.9 8.0 %collective-permute-done.2 = bf16[9,16,256]{2,1,0:T(8,128)(2,1)S(1)} collective-permute-done((bf16[9,16,256]{2,1,0:T(8,128)(2,1)S(1)}, bf16[9,16,256]{2,1,0:T(8,128)(2,1)S(1)}, u32[]{:S(2)}, u32[]{:S(2)}) %collective-permute-start.2) | collective-permute-done | bytes 73760 | tf_op jit(solution)/shard_map/ppermute | solution.py:73
  29.1 1.6 fusion.21
  30.7 4.4 %all-to-all-start = ((bf16[8,144,128]{2,1,0:T(8,128)(2,1)}), bf16[8,144,128]{2,1,0:T(8,128)(2,1)}, u32[]{:S(2)}, u32[]{:S(2)}) async-start(bf16[8,144,128]{2,1,0:T(8,128)(2,1)} %fusion.21), calls=%async_computation | async-start | bytes 589824 | tf_op jit(solution)/shard_map/all_to_all | solution.py:88
  35.4 1.2 copy.109
  36.6 1.6 reshape.288
  38.2 2.7 %all-to-all-done = bf16[8,144,128]{2,1,0:T(8,128)(2,1)} async-done(((bf16[8,144,128]{2,1,0:T(8,128)(2,1)}), bf16[8,144,128]{2,1,0:T(8,128)(2,1)}, u32[]{:S(2)}, u32[]{:S(2)}) %all-to-all-start) | async-done | bytes 294944 | tf_op jit(solution)/shard_map/all_to_all | solution.py:88
  40.9 1.0 copy.183
  43.7 1.5 convolution_bitcast_fusion
  45.2 1.7 fusion.102
  47.0 1.1 collective-permute-start.5
  48.0 1.4 fusion.108
  51.5 3.5 %constant_dynamic-slice_fusion.3 = (bf16[4,512,32]{2,1,0:T(8,128)(2,1)}, bf16[4,512,32]{2,1,0:T(8,128)(2,1)}, bf16[4,512,32]{2,1,0:T(8,128)(2,1)}, bf16[4,512,32]{2,1,0:T(8,128)(2,1)}) fusion(bf16[8,512,256]{2,1,0:T(8,128)(2,1)} %param.15, s32[]{:T(128)S(6)} %select_n.248, s32[]{:T(128)S(6)} %select_n.249, s32[]{:T(128)S(6)} %add.218, s32[]{:T(128)S(6)} %select_n.250), kind=kLoop, calls=%fused_computation.189 | loop fusion | bytes 1048592 | tf_op jit(solution)/shard_map/slice | solution.py:205
  55.0 1.3 copy.127
  56.3 1.9 copy.128
  58.2 1.9 copy.130
  60.2 2.0 copy.129
  62.1 4.6 %copy.120.w_ref = bf16[27,512,64]{2,1,0:T(8,128)(2,1)} copy(bf16[27,512,64]{1,2,0:T(8,128)(2,1)} %param.14) | data formatting | bytes 3538944 | tf_op args[3]
  66.8 1.4 pad_maximum_fusion.1
  68.3 1.6 copy_add_fusion
  70.3 3.0 %collective-permute-start.8 = (bf16[8,16,512]{2,1,0:T(8,128)(2,1)S(1)}, bf16[8,16,512]{2,1,0:T(8,128)(2,1)S(1)}, u32[]{:S(2)}, u32[]{:S(2)}) collective-permute-start(bf16[8,16,512]{2,1,0:T(8,128)(2,1)S(1)} %get-tuple-element.45), channel_id=1, source_target_pairs={{0,8},{2,10},{4,12},{6,14},{8,0},{10,2},{12,4},{14,6},{1,9},{3,11}... | collective-permute-start | bytes 393224 | tf_op jit(solution)/shard_map/ppermute | solution.py:154
  73.5 3.0 %pad_bitcast_fusion.1 = (bf16[8,1,64,2,2,2,128]{2,6,5,4,0,3,1:T(8,128)(2,1)}, bf16[8,1,64,2,2,2,128]{2,6,5,4,0,3,1:T(8,128)(2,1)}) fusion(bf16[8,64,1,2,2,128]{1,5,4,3,0,2:T(8,128)(2,1)S(1)} %bitcast.245), kind=kLoop, calls=%fused_computation.11 | loop fusion | bytes 2621440 | tf_op jit(solution)/shard_map/stack | solution.py:208
  77.0 3.1 %collective-permute-done.7 = bf16[8,16,512]{2,1,0:T(8,128)(2,1)S(1)} collective-permute-done((bf16[8,16,512]{2,1,0:T(8,128)(2,1)S(1)}, bf16[8,16,512]{2,1,0:T(8,128)(2,1)S(1)}, u32[]{:S(2)}, u32[]{:S(2)}) %collective-permute-start.7) | collective-permute-done | bytes 131104 | tf_op jit(solution)/shard_map/ppermute | solution.py:154
  80.8 2.2 collective-permute-start.9
  83.1 1.0 collective-permute-done.9
  84.1 15.0 %all-gather = bf16[48,8,512]{2,1,0:T(8,128)(2,1)S(1)} all-gather(bf16[6,8,512]{2,1,0:T(8,128)(2,1)S(1)} %pad_maximum_fusion.12), channel_id=2, replica_groups=mesh['row'=16,'col'=8,'depth'=2] {'col'}, dimensions={0}, use_global_device_ids=true | all-gather | bytes 442368 | tf_op jit(solution)/shard_map/all_gather | solution.py:178
  99.3 1.9 collective-permute-start.15
  101.2 3.4 %collective-permute-start.16 = (bf16[9,16,256]{2,1,0:T(8,128)(2,1)S(1)}, bf16[9,16,256]{2,1,0:T(8,128)(2,1)S(1)}, u32[]{:S(2)}, u32[]{:S(2)}) collective-permute-start(bf16[9,16,256]{2,1,0:T(8,128)(2,1)S(1)} %get-tuple-element.72), channel_id=1, source_target_pairs={{16,0},{32,16},{48,32},{64,48},{80,64},{96,80},{112,96},{128,112},... | collective-permute-start | bytes 221192 | tf_op jit(solution)/shard_map/ppermute | solution.py:73
  104.7 2.5 %mid_taps.1 = (bf16[5,64,64]{2,1,0:T(8,128)(2,1)S(1)}, f32[5,64,64]{2,1,0:T(8,128)S(1)}, bf16[5,64,64]{2,1,0:T(8,128)(2,1)S(1)}) custom-call(bf16[7,64,512]{2,1,0:T(8,128)(2,1)S(1)} %maximum_select_fusion.slab_ref, bf16[27,512,64]{2,1,0:T(8,128)(2,1)S(1)} %copy-done.2), custom_call_target="tpu_custom_call" | custom-call | tf_op jit(solution)/shard_map/mid_taps/pallas_call | solution.py:134
  107.2 6.1 %collective-permute-start.10 = (bf16[5,64,64]{2,1,0:T(8,128)(2,1)S(1)}, bf16[5,64,64]{2,1,0:T(8,128)(2,1)S(1)}, u32[]{:S(2)}, u32[]{:S(2)}) collective-permute-start(bf16[5,64,64]{2,1,0:T(8,128)(2,1)S(1)} %get-tuple-element.19), channel_id=1, source_target_pairs={{0,16},{16,32},{32,48},{48,64},{64,80},{80,96},{96,112},{112,128},... | collective-permute-start | bytes 122888 | tf_op jit(solution)/shard_map/ppermute | solution.py:72
  113.4 1.9 collective-permute-start.11
  115.3 1.6 fusion.24
  116.9 4.8 %all-to-all-start.1 = ((bf16[8,144,128]{2,1,0:T(8,128)(2,1)}), bf16[8,144,128]{2,1,0:T(8,128)(2,1)S(1)}, u32[]{:S(2)}, u32[]{:S(2)}) async-start(bf16[8,144,128]{2,1,0:T(8,128)(2,1)} %fusion.24), calls=%async_computation.1 | async-start | bytes 589824 | tf_op jit(solution)/shard_map/all_to_all | solution.py:88
  121.8 5.2 %pad_maximum_fusion = bf16[8,2,64,2,2,2,128]{2,6,5,4,0,3,1:T(8,128)(2,1)} fusion(bf16[8,1,64,2,2,2,128]{2,6,5,4,0,3,1:T(8,128)(2,1)} %get-tuple-element.38, bf16[8,1,64,2,2,2,128]{2,6,5,4,0,3,1:T(8,128)(2,1)} %get-tuple-element.37), kind=kLoop, calls=%fused_computation | loop fusion | flops 1048576 | bytes 4194304 | tf_op jit(solution)/shard_map/stack | solution.py:208
  126.9 6.8 %copy.131 = bf16[8,2,64,2,2,2,128]{6,5,4,3,2,1,0:T(2,128)(2,1)} copy(bf16[8,2,64,2,2,2,128]{2,6,5,4,0,3,1:T(8,128)(2,1)} %pad_maximum_fusion) | data formatting | bytes 4194304 | tf_op jit(solution)/shard_map/stack | solution.py:208
  133.7 4.5 %reshape.272 = bf16[1024,1024]{1,0:T(8,128)(2,1)} reshape(bf16[8,2,64,2,2,2,128]{6,5,4,3,2,1,0:T(2,128)(2,1)} %copy.131) | data formatting | bytes 4194304 | tf_op jit(solution)/shard_map/reshape | solution.py:209
  138.2 6.0 %collective-permute-start.13 = (bf16[27,32,256]{2,1,0:T(8,128)(2,1)S(1)}, bf16[27,32,256]{2,1,0:T(8,128)(2,1)S(1)}, u32[]{:S(2)}, u32[]{:S(2)}) collective-permute-start(bf16[27,32,256]{2,1,0:T(8,128)(2,1)S(1)} %copy-done.6), channel_id=1, source_target_pairs={{129,0},{128,1},{194,2},{195,3},{181,4},{180,5},{246,6},{247,7},{1... | collective-permute-start | bytes 1327112 | tf_op jit(solution)/shard_map/ppermute | solution.py:168
  144.2 1.9 collective-permute-start.12
  146.3 4.7 %collective-permute-done.13 = bf16[27,32,256]{2,1,0:T(8,128)(2,1)S(1)} collective-permute-done((bf16[27,32,256]{2,1,0:T(8,128)(2,1)S(1)}, bf16[27,32,256]{2,1,0:T(8,128)(2,1)S(1)}, u32[]{:S(2)}, u32[]{:S(2)}) %collective-permute-start.13) | collective-permute-done | bytes 442400 | tf_op jit(solution)/shard_map/ppermute | solution.py:168
  151.1 13.0 %collective-permute-done.12 = bf16[27,32,256]{2,1,0:T(8,128)(2,1)S(1)} collective-permute-done((bf16[27,32,256]{2,1,0:T(8,128)(2,1)S(1)}, bf16[27,32,256]{2,1,0:T(8,128)(2,1)S(1)}, u32[]{:S(2)}, u32[]{:S(2)}) %collective-permute-start.12) | collective-permute-done | bytes 442400 | tf_op jit(solution)/shard_map/ppermute | solution.py:167
  164.3 12.0 %all_gather.11 = bf16[8,3,64,128]{3,2,1,0:T(8,128)(2,1)S(1)} all-gather(bf16[1,3,64,128]{3,2,1,0:T(8,128)(2,1)S(1)} %all_gather_reshape.3), channel_id=1, replica_groups=mesh['row'=16,'col'=8,'depth'=2] {'col'}, dimensions={0}, use_global_device_ids=true | all-gather | bytes 442368 | tf_op jit(solution)/shard_map/all_gather | solution.py:196
  176.6 2.2 convolution_convert_fusion
  180.3 1.9 collective-permute-start.18
  182.2 7.8 %collective-permute-start.17 = (bf16[3,128,128]{1,2,0:T(8,128)(2,1)S(1)}, bf16[3,128,128]{1,2,0:T(8,128)(2,1)S(1)}, u32[]{:S(2)}, u32[]{:S(2)}) collective-permute-start(bf16[3,128,128]{1,2,0:T(8,128)(2,1)S(1)} %bitcast.302), channel_id=1, source_target_pairs={{0,16},{16,32},{32,48},{48,64},{64,80},{80,96},{96,112},{112,128},... | collective-permute-start | bytes 294920 | tf_op jit(solution)/shard_map/ppermute | solution.py:72
  190.3 1.2 copy.124
  192.8 2.9 %fusion.109 = f32[1024,512]{1,0:T(8,128)} fusion(bf16[1024,1152]{1,0:T(8,128)(2,1)S(1)} %bitcast.309, bf16[1152,512]{1,0:T(8,128)(2,1)S(1)} %bitcast.275), kind=kOutput, calls=%fused_computation.211 | convolution fusion | flops 1207959552 | bytes 5636096 | tf_op jit(solution)/shard_map/dot_general | solution.py:112
  195.8 1.2 copy.137
  197.0 1.3 copy.153
  201.2 1.5 convolution_add_fusion
  203.3 0.8 collective-permute-start.19
  204.1 2.3 %collective-permute-done.19 = f32[4,8,16,512]{3,2,1,0:T(8,128)S(1)} collective-permute-done((f32[4,8,16,512]{3,2,1,0:T(8,128)S(1)}, f32[4,8,16,512]{3,2,1,0:T(8,128)S(1)}, u32[]{:S(2)}, u32[]{:S(2)}) %collective-permute-start.19) | collective-permute-done | bytes 1048608 | tf_op jit(solution)/shard_map/ppermute | solution.py:149
  207.2 2.1 collective-permute-start.20
  209.3 2.4 %collective-permute-start.22 = (bf16[8,16,512]{2,1,0:T(8,128)(2,1)S(1)}, bf16[8,16,512]{2,1,0:T(8,128)(2,1)S(1)}, u32[]{:S(2)}, u32[]{:S(2)}) collective-permute-start(bf16[8,16,512]{2,1,0:T(8,128)(2,1)S(1)} %get-tuple-element.42), channel_id=1, source_target_pairs={{0,8},{2,10},{4,12},{6,14},{8,0},{10,2},{12,4},{14,6},{1,9},{3,11}... | collective-permute-start | bytes 393224 | tf_op jit(solution)/shard_map/ppermute | solution.py:154
  211.7 1.7 collective-permute-done.20
  213.4 1.8 collective-permute-done.22
  215.2 3.6 %collective-permute-done.21 = bf16[8,16,512]{2,1,0:T(8,128)(2,1)S(1)} collective-permute-done((bf16[8,16,512]{2,1,0:T(8,128)(2,1)S(1)}, bf16[8,16,512]{2,1,0:T(8,128)(2,1)S(1)}, u32[]{:S(2)}, u32[]{:S(2)}) %collective-permute-start.21) | collective-permute-done | bytes 131104 | tf_op jit(solution)/shard_map/ppermute | solution.py:154
  219.0 0.7 copy.185
  (140 shorter events, 12.7 us)
Async XLA Ops:
  0.0 80.3 %copy-start = (bf16[8,256,512]{2,1,0:T(8,128)(2,1)S(1)}, bf16[8,256,512]{2,1,0:T(8,128)(2,1)}, u32[]{:S(2)}) copy-start(bf16[8,256,512]{2,1,0:T(8,128)(2,1)} %param.13) | copy-start | bytes 6291460
  0.0 29.0 %collective-permute-start.4 = (bf16[27,16,256]{2,1,0:T(8,128)(2,1)}, bf16[27,16,256]{2,1,0:T(8,128)(2,1)S(1)}, u32[]{:S(2)}, u32[]{:S(2)}) collective-permute-start(bf16[27,16,256]{2,1,0:T(8,128)(2,1)} %param.12), channel_id=1, source_target_pairs={{129,0},{128,1},{194,2},{195,3},{181,4},{180,5},{246,6},{247,7},{1... | collective-permute-start | bytes 663560 | tf_op jit(solution)/shard_map/ppermute | solution.py:162
  4.1 24.9 %collective-permute-start.3 = (bf16[27,16,256]{2,1,0:T(8,128)(2,1)}, bf16[27,16,256]{2,1,0:T(8,128)(2,1)S(1)}, u32[]{:S(2)}, u32[]{:S(2)}) collective-permute-start(bf16[27,16,256]{2,1,0:T(8,128)(2,1)} %param.12), channel_id=1, source_target_pairs={{0,0},{1,1},{66,2},{67,3},{20,4},{21,5},{86,6},{87,7},{40,8},{41,9... | collective-permute-start | bytes 663560 | tf_op jit(solution)/shard_map/ppermute | solution.py:162
  7.0 5.3 %collective-permute-start = (bf16[2,16,256]{2,1,0:T(8,128)(2,1)S(1)}, bf16[2,16,256]{2,1,0:T(8,128)(2,1)S(1)}, u32[]{:S(2)}, u32[]{:S(2)}) collective-permute-start(bf16[2,16,256]{2,1,0:T(8,128)(2,1)S(1)} %fusion.93), channel_id=1, source_target_pairs={{0,1},{1,0},{2,3},{3,2},{4,5},{5,4},{6,7},{7,6},{8,9},{9,8},{10,11... | collective-permute-start | bytes 49160 | tf_op jit(solution)/shard_map/ppermute | solution.py:68
  12.3 8.6 %collective-permute-start.1 = (bf16[9,16,256]{2,1,0:T(8,128)(2,1)S(1)}, bf16[9,16,256]{2,1,0:T(8,128)(2,1)S(1)}, u32[]{:S(2)}, u32[]{:S(2)}) collective-permute-start(bf16[9,16,256]{2,1,0:T(8,128)(2,1)S(1)} %get-tuple-element.73), channel_id=1, source_target_pairs={{0,16},{16,32},{32,48},{48,64},{64,80},{80,96},{96,112},{112,128},... | collective-permute-start | bytes 221192 | tf_op jit(solution)/shard_map/ppermute | solution.py:72
  18.8 10.1 %collective-permute-start.2 = (bf16[9,16,256]{2,1,0:T(8,128)(2,1)S(1)}, bf16[9,16,256]{2,1,0:T(8,128)(2,1)S(1)}, u32[]{:S(2)}, u32[]{:S(2)}) collective-permute-start(bf16[9,16,256]{2,1,0:T(8,128)(2,1)S(1)} %get-tuple-element.74), channel_id=1, source_target_pairs={{16,0},{32,16},{48,32},{64,48},{80,64},{96,80},{112,96},{128,112},... | collective-permute-start | bytes 221192 | tf_op jit(solution)/shard_map/ppermute | solution.py:73
  30.7 10.3 %all-to-all-start = ((bf16[8,144,128]{2,1,0:T(8,128)(2,1)}), bf16[8,144,128]{2,1,0:T(8,128)(2,1)}, u32[]{:S(2)}, u32[]{:S(2)}) async-start(bf16[8,144,128]{2,1,0:T(8,128)(2,1)} %fusion.21), calls=%async_computation | async-start | bytes 589824 | tf_op jit(solution)/shard_map/all_to_all | solution.py:88
  42.5 1.3 copy-start.5
  47.0 21.3 %collective-permute-start.5 = (f32[4,8,16,512]{3,2,0,1:T(8,128)}, f32[4,8,16,512]{3,2,0,1:T(8,128)}, u32[]{:S(2)}, u32[]{:S(2)}) collective-permute-start(f32[4,8,16,512]{3,2,0,1:T(8,128)} %get-tuple-element.35), channel_id=1, source_target_pairs={{0,2},{2,0},{4,6},{6,4},{8,10},{10,8},{12,14},{14,12},{1,3},{3,1},... | collective-permute-start | bytes 3145736 | tf_op jit(solution)/shard_map/ppermute | solution.py:149
  66.7 1.5 copy-start.3
  70.2 6.4 %collective-permute-start.6 = (bf16[8,16,512]{2,1,0:T(8,128)(2,1)S(1)}, bf16[8,16,512]{2,1,0:T(8,128)(2,1)S(1)}, u32[]{:S(2)}, u32[]{:S(2)}) collective-permute-start(bf16[8,16,512]{2,1,0:T(8,128)(2,1)S(1)} %get-tuple-element.44), channel_id=1, source_target_pairs={{0,4},{2,6},{4,8},{6,10},{8,12},{10,14},{12,0},{14,2},{1,5},{3,7},... | collective-permute-start | bytes 393224 | tf_op jit(solution)/shard_map/ppermute | solution.py:154
  70.3 6.7 %collective-permute-start.8 = (bf16[8,16,512]{2,1,0:T(8,128)(2,1)S(1)}, bf16[8,16,512]{2,1,0:T(8,128)(2,1)S(1)}, u32[]{:S(2)}, u32[]{:S(2)}) collective-permute-start(bf16[8,16,512]{2,1,0:T(8,128)(2,1)S(1)} %get-tuple-element.45), channel_id=1, source_target_pairs={{0,8},{2,10},{4,12},{6,14},{8,0},{10,2},{12,4},{14,6},{1,9},{3,11}... | collective-permute-start | bytes 393224 | tf_op jit(solution)/shard_map/ppermute | solution.py:154
  73.2 6.9 %collective-permute-start.7 = (bf16[8,16,512]{2,1,0:T(8,128)(2,1)S(1)}, bf16[8,16,512]{2,1,0:T(8,128)(2,1)S(1)}, u32[]{:S(2)}, u32[]{:S(2)}) collective-permute-start(bf16[8,16,512]{2,1,0:T(8,128)(2,1)S(1)} %get-tuple-element.46), channel_id=1, source_target_pairs={{0,12},{2,14},{4,0},{6,2},{8,4},{10,6},{12,8},{14,10},{1,13},{3,15... | collective-permute-start | bytes 393224 | tf_op jit(solution)/shard_map/ppermute | solution.py:154
  80.8 24.0 %copy-start.2 = (bf16[27,512,64]{2,1,0:T(8,128)(2,1)S(1)}, bf16[27,512,64]{2,1,0:T(8,128)(2,1)}, u32[]{:S(2)}) copy-start(bf16[27,512,64]{2,1,0:T(8,128)(2,1)} %copy.120.w_ref) | copy-start | bytes 5308420
  80.8 3.3 %collective-permute-start.9 = (bf16[2,8,512]{2,1,0:T(8,128)(2,1)S(1)}, bf16[2,8,512]{2,1,0:T(8,128)(2,1)S(1)}, u32[]{:S(2)}, u32[]{:S(2)}) collective-permute-start(bf16[2,8,512]{2,1,0:T(8,128)(2,1)S(1)} %slice_select_fusion.1), channel_id=1, source_target_pairs={{0,1},{1,0},{2,3},{3,2},{4,5},{5,4},{6,7},{7,6},{8,9},{9,8},{10,11... | collective-permute-start | bytes 49160 | tf_op jit(solution)/shard_map/ppermute | solution.py:177
  83.0 16.2 %collective-permute-start.14 = (bf16[2,16,256]{2,1,0:T(8,128)(2,1)S(1)}, bf16[2,16,256]{2,1,0:T(8,128)(2,1)S(1)}, u32[]{:S(2)}, u32[]{:S(2)}) collective-permute-start(bf16[2,16,256]{2,1,0:T(8,128)(2,1)S(1)} %fusion.92), channel_id=1, source_target_pairs={{0,1},{1,0},{2,3},{3,2},{4,5},{5,4},{6,7},{7,6},{8,9},{9,8},{10,11... | collective-permute-start | bytes 49160 | tf_op jit(solution)/shard_map/ppermute | solution.py:68
  99.3 16.0 %collective-permute-start.15 = (bf16[9,16,256]{2,1,0:T(8,128)(2,1)S(1)}, bf16[9,16,256]{2,1,0:T(8,128)(2,1)S(1)}, u32[]{:S(2)}, u32[]{:S(2)}) collective-permute-start(bf16[9,16,256]{2,1,0:T(8,128)(2,1)S(1)} %get-tuple-element.71), channel_id=1, source_target_pairs={{0,16},{16,32},{32,48},{48,64},{64,80},{80,96},{96,112},{112,128},... | collective-permute-start | bytes 221192 | tf_op jit(solution)/shard_map/ppermute | solution.py:72
  101.2 14.1 %collective-permute-start.16 = (bf16[9,16,256]{2,1,0:T(8,128)(2,1)S(1)}, bf16[9,16,256]{2,1,0:T(8,128)(2,1)S(1)}, u32[]{:S(2)}, u32[]{:S(2)}) collective-permute-start(bf16[9,16,256]{2,1,0:T(8,128)(2,1)S(1)} %get-tuple-element.72), channel_id=1, source_target_pairs={{16,0},{32,16},{48,32},{64,48},{80,64},{96,80},{112,96},{128,112},... | collective-permute-start | bytes 221192 | tf_op jit(solution)/shard_map/ppermute | solution.py:73
  107.2 38.9 %collective-permute-start.10 = (bf16[5,64,64]{2,1,0:T(8,128)(2,1)S(1)}, bf16[5,64,64]{2,1,0:T(8,128)(2,1)S(1)}, u32[]{:S(2)}, u32[]{:S(2)}) collective-permute-start(bf16[5,64,64]{2,1,0:T(8,128)(2,1)S(1)} %get-tuple-element.19), channel_id=1, source_target_pairs={{0,16},{16,32},{32,48},{48,64},{64,80},{80,96},{96,112},{112,128},... | collective-permute-start | bytes 122888 | tf_op jit(solution)/shard_map/ppermute | solution.py:72
  113.4 32.7 %collective-permute-start.11 = (bf16[5,64,64]{2,1,0:T(8,128)(2,1)S(1)}, bf16[5,64,64]{2,1,0:T(8,128)(2,1)S(1)}, u32[]{:S(2)}, u32[]{:S(2)}) collective-permute-start(bf16[5,64,64]{2,1,0:T(8,128)(2,1)S(1)} %get-tuple-element.20), channel_id=1, source_target_pairs={{16,0},{32,16},{48,32},{64,48},{80,64},{96,80},{112,96},{128,112},... | collective-permute-start | bytes 122888 | tf_op jit(solution)/shard_map/ppermute | solution.py:73
  116.9 29.3 %all-to-all-start.1 = ((bf16[8,144,128]{2,1,0:T(8,128)(2,1)}), bf16[8,144,128]{2,1,0:T(8,128)(2,1)S(1)}, u32[]{:S(2)}, u32[]{:S(2)}) async-start(bf16[8,144,128]{2,1,0:T(8,128)(2,1)} %fusion.24), calls=%async_computation.1 | async-start | bytes 589824 | tf_op jit(solution)/shard_map/all_to_all | solution.py:88
  133.7 4.5 %copy-start.6 = (bf16[27,32,256]{2,1,0:T(8,128)(2,1)S(1)}, bf16[27,32,256]{2,1,0:T(8,128)(2,1)}, u32[]{:S(2)}) copy-start(bf16[27,32,256]{2,1,0:T(8,128)(2,1)} %param.16) | copy-start | bytes 1327108
  138.2 12.9 %collective-permute-start.13 = (bf16[27,32,256]{2,1,0:T(8,128)(2,1)S(1)}, bf16[27,32,256]{2,1,0:T(8,128)(2,1)S(1)}, u32[]{:S(2)}, u32[]{:S(2)}) collective-permute-start(bf16[27,32,256]{2,1,0:T(8,128)(2,1)S(1)} %copy-done.6), channel_id=1, source_target_pairs={{129,0},{128,1},{194,2},{195,3},{181,4},{180,5},{246,6},{247,7},{1... | collective-permute-start | bytes 1327112 | tf_op jit(solution)/shard_map/ppermute | solution.py:168
  144.2 19.9 %collective-permute-start.12 = (bf16[27,32,256]{2,1,0:T(8,128)(2,1)S(1)}, bf16[27,32,256]{2,1,0:T(8,128)(2,1)S(1)}, u32[]{:S(2)}, u32[]{:S(2)}) collective-permute-start(bf16[27,32,256]{2,1,0:T(8,128)(2,1)S(1)} %copy-done.6), channel_id=1, source_target_pairs={{0,0},{1,1},{66,2},{67,3},{20,4},{21,5},{86,6},{87,7},{40,8},{41,9... | collective-permute-start | bytes 1327112 | tf_op jit(solution)/shard_map/ppermute | solution.py:167
  180.3 18.3 %collective-permute-start.18 = (bf16[3,128,128]{1,2,0:T(8,128)(2,1)S(1)}, bf16[3,128,128]{1,2,0:T(8,128)(2,1)S(1)}, u32[]{:S(2)}, u32[]{:S(2)}) collective-permute-start(bf16[3,128,128]{1,2,0:T(8,128)(2,1)S(1)} %bitcast.301), channel_id=1, source_target_pairs={{16,0},{32,16},{48,32},{64,48},{80,64},{96,80},{112,96},{128,112},... | collective-permute-start | bytes 294920 | tf_op jit(solution)/shard_map/ppermute | solution.py:73
  182.2 16.1 %collective-permute-start.17 = (bf16[3,128,128]{1,2,0:T(8,128)(2,1)S(1)}, bf16[3,128,128]{1,2,0:T(8,128)(2,1)S(1)}, u32[]{:S(2)}, u32[]{:S(2)}) collective-permute-start(bf16[3,128,128]{1,2,0:T(8,128)(2,1)S(1)} %bitcast.302), channel_id=1, source_target_pairs={{0,16},{16,32},{32,48},{48,64},{64,80},{80,96},{96,112},{112,128},... | collective-permute-start | bytes 294920 | tf_op jit(solution)/shard_map/ppermute | solution.py:72
  199.3 1.3 copy-start.4
  199.3 2.0 copy-start.7
  203.3 3.1 %collective-permute-start.19 = (f32[4,8,16,512]{3,2,1,0:T(8,128)S(1)}, f32[4,8,16,512]{3,2,1,0:T(8,128)S(1)}, u32[]{:S(2)}, u32[]{:S(2)}) collective-permute-start(f32[4,8,16,512]{3,2,1,0:T(8,128)S(1)} %select_bitcast_fusion), channel_id=1, source_target_pairs={{0,2},{2,0},{4,6},{6,4},{8,10},{10,8},{12,14},{14,12},{1,3},{3,1},... | collective-permute-start | bytes 3145736 | tf_op jit(solution)/shard_map/ppermute | solution.py:149
  206.4 13.3 %copy-start.1 = (bf16[8,256,512]{2,1,0:T(8,128)(2,1)S(1)}, bf16[8,256,512]{2,1,0:T(8,128)(2,1)}, u32[]{:S(2)}) copy-start(bf16[8,256,512]{2,1,0:T(8,128)(2,1)} %param.13) | copy-start | bytes 6291460
  207.2 6.2 %collective-permute-start.20 = (bf16[8,16,512]{2,1,0:T(8,128)(2,1)S(1)}, bf16[8,16,512]{2,1,0:T(8,128)(2,1)S(1)}, u32[]{:S(2)}, u32[]{:S(2)}) collective-permute-start(bf16[8,16,512]{2,1,0:T(8,128)(2,1)S(1)} %get-tuple-element.41), channel_id=1, source_target_pairs={{0,4},{2,6},{4,8},{6,10},{8,12},{10,14},{12,0},{14,2},{1,5},{3,7},... | collective-permute-start | bytes 393224 | tf_op jit(solution)/shard_map/ppermute | solution.py:154
  209.3 5.9 %collective-permute-start.22 = (bf16[8,16,512]{2,1,0:T(8,128)(2,1)S(1)}, bf16[8,16,512]{2,1,0:T(8,128)(2,1)S(1)}, u32[]{:S(2)}, u32[]{:S(2)}) collective-permute-start(bf16[8,16,512]{2,1,0:T(8,128)(2,1)S(1)} %get-tuple-element.42), channel_id=1, source_target_pairs={{0,8},{2,10},{4,12},{6,14},{8,0},{10,2},{12,4},{14,6},{1,9},{3,11}... | collective-permute-start | bytes 393224 | tf_op jit(solution)/shard_map/ppermute | solution.py:154
  211.6 7.1 %collective-permute-start.21 = (bf16[8,16,512]{2,1,0:T(8,128)(2,1)S(1)}, bf16[8,16,512]{2,1,0:T(8,128)(2,1)S(1)}, u32[]{:S(2)}, u32[]{:S(2)}) collective-permute-start(bf16[8,16,512]{2,1,0:T(8,128)(2,1)S(1)} %get-tuple-element.43), channel_id=1, source_target_pairs={{0,12},{2,14},{4,0},{6,2},{8,4},{10,6},{12,8},{14,10},{1,13},{3,15... | collective-permute-start | bytes 393224 | tf_op jit(solution)/shard_map/ppermute | solution.py:154

commit v3 on v2

--- a/solution.py
+++ b/solution.py
@@ -112,10 +112,19 @@
     return jnp.dot(patches, wt.reshape(1152, 512), preferred_element_type=F32)
 
 
-def mid_body(slab_ref, w_ref, prev_ref, own_ref, next_ref):
+WHOLE = pl.BlockSpec(memory_space=pltpu.VMEM)
+
+
+def mid_body(slab_ref, w_hbm, prev_ref, own_ref, next_ref, w_ref, sems):
+    copies = [
+        pltpu.make_async_copy(w_hbm.at[pl.ds(9 * a, 9)], w_ref.at[pl.ds(9 * a, 9)], sems.at[a]) for a in range(3)
+    ]
+    for copy in copies:
+        copy.start()
     y = lax.broadcasted_iota(jnp.int32, (320, 64), 0) % 64
     near = [slab_ref[c : c + 5].reshape(320, 512) for c in range(3)]
     for a, out in enumerate((prev_ref, own_ref, next_ref)):
+        copies[a].wait()
         total = jnp.zeros((320, 64), F32)
         for b in range(3):
             g = jnp.zeros((320, 64), F32)
@@ -130,15 +139,67 @@
 
 
 def mid_taps(slab, w):
-    whole = pl.BlockSpec(memory_space=pltpu.VMEM)
     return pl.pallas_call(
         mid_body,
-        in_specs=[whole] * 2,
-        out_specs=[whole] * 3,
+        in_specs=[WHOLE, pl.BlockSpec(memory_space=pl.ANY)],
+        out_specs=[WHOLE] * 3,
         out_shape=[jax.ShapeDtypeStruct((5, 64, 64), t) for t in (BF, F32, BF)],
+        scratch_shapes=[pltpu.VMEM((27, 512, 64), BF), pltpu.SemaphoreType.DMA((3,))],
         compiler_params=pltpu.CompilerParams(vmem_limit_bytes=24 << 20),
         name="mid_taps",
     )(slab, w)
+
+
+def lift_body(at_ref, got_ref, up_ref, planes_ref, next_ref, prev_ref, w_ref, tmp_ref):
+    w_ref[...] = jnp.zeros((1024, 1024), BF)
+    ch = lax.broadcasted_iota(jnp.int32, (256, 128), 0)
+    lane = lax.broadcasted_iota(jnp.int32, (256, 128), 1)
+    part, within = lane // 32, lane % 32
+    shard = jnp.where(part == 0, at_ref[0], jnp.where(part == 3, at_ref[2], at_ref[1]))
+    hit = ch == 32 * shard + within
+    upper = jnp.where(hit & (part < 2), 1.0, 0.0).astype(BF)
+    lower = jnp.where(hit & (part >= 2), 1.0, 0.0).astype(BF)
+    for tap in range(4):
+        u = jnp.dot(up_ref[tap], upper, preferred_element_type=F32)
+        u = u + jnp.dot(up_ref[4 + tap], lower, preferred_element_type=F32)
+        u = u.astype(BF)
+        for src in range(8):
+            for h in range(2):
+                rows = slice(128 * src + 64 * h, 128 * src + 64 * h + 64)
+                w_ref[rows, 128 * (4 * h + tap) : 128 * (4 * h + tap) + 128] = u[64 * src : 64 * src + 64]
+    got = jnp.concatenate(
+        [jnp.concatenate([got_ref[src, g] for src in range(8)], 1) for g in range(3)], 0
+    )
+    out = jnp.dot(got, w_ref[...], preferred_element_type=F32)
+    for g in range(3):
+        for h in range(2):
+            for b in range(2):
+                for c in range(2):
+                    piece = out[64 * g : 64 * g + 64, 128 * (4 * h + 2 * b + c) : 128 * (4 * h + 2 * b + c) + 128]
+                    tmp_ref[2 * (2 * g + h) + c, pl.ds(b, 64, stride=2), :] = piece
+    group = lax.broadcasted_iota(jnp.int32, (128, 128), 1) // 32
+    for q in range(3):
+        nxt = jnp.zeros((128, 128), F32)
+        prv = jnp.zeros((128, 128), F32)
+        for k in range(4):
+            plane = tmp_ref[4 * q + k]
+            planes_ref[4 * q + k] = plane.astype(BF)
+            nxt = jnp.where(group == k, pltpu.roll(plane, (32 * k - 96) % 128, 1), nxt)
+            prv = jnp.where(group == k, pltpu.roll(plane, 32 * k, 1) if k else plane, prv)
+        next_ref[q] = nxt.astype(BF)
+        prev_ref[q] = prv.astype(BF)
+
+
+def lift_planes(at, got, up):
+    return pl.pallas_call(
+        lift_body,
+        in_specs=[pl.BlockSpec(memory_space=pltpu.SMEM), WHOLE, WHOLE],
+        out_specs=[WHOLE] * 3,
+        out_shape=[jax.ShapeDtypeStruct((n, 128, 128), BF) for n in (12, 3, 3)],
+        scratch_shapes=[pltpu.VMEM((1024, 1024), BF), pltpu.VMEM((12, 128, 128), F32)],
+        compiler_params=pltpu.CompilerParams(vmem_limit_bytes=24 << 20),
+        name="lift_planes",
+    )(at, got, up)
 
 
 def reduce_tiles(acc, j):
@@ -194,32 +255,17 @@
     packed = jnp.concatenate([middle, jnp.zeros((1, 64, 64), BF)], 0)
     packed = packed.reshape(3, 2, 64, 64).transpose(0, 2, 1, 3).reshape(3, 64, 128)
     got = lax.all_gather(packed, "col", axis=0)
-    got = got.transpose(1, 2, 0, 3).reshape(192, 1024)
     places = jnp.asarray(lift_table())
-
-    def cut(row):
-        at = places[jnp.clip(row, 0, 15), j]
-        return lax.dynamic_slice(up_kernel, (0, 0, 32 * at), (8, 512, 32)).reshape(2, 2, 2, 8, 64, 32)
-
-    mine = cut(r)
-    up = jnp.stack([cut(r - 1)[0], mine[0], mine[1], cut(r + 1)[1]])
-    up = up.transpose(3, 4, 1, 2, 0, 5).reshape(8, 64, 2, 2, 128)
-    zero = jnp.zeros_like(up)
-    up = jnp.stack([jnp.stack([up, zero], 2), jnp.stack([zero, up], 2)], 1)
-    lift = jnp.dot(got, up.reshape(1024, 1024), preferred_element_type=F32).astype(BF)
-    lift = lift.reshape(3, 64, 2, 2, 2, 128).transpose(0, 2, 4, 1, 3, 5).reshape(12, 128, 128)
+    at = jnp.stack([places[jnp.clip(r + step, 0, 15), j] for step in (-1, 0, 1)])
+    lift, for_next, for_prev = lift_planes(at, got, up_kernel)
+
+    def unpack(v):
+        return v.reshape(3, 128, 4, 32).transpose(0, 2, 1, 3).reshape(12, 128, 32)
+
+    lo, hi = row_halo(for_next, for_prev)
+    lift = jnp.concatenate([unpack(lo), lift[..., 32:96], unpack(hi)], -1)
     none = jnp.zeros((1, 128, 128), BF)
-    lift = jnp.where(d == 0, jnp.concatenate([none, lift[:9]], 0), jnp.concatenate([lift[1:10], none], 0))
-
-    def pack(v):
-        v = jnp.concatenate([v, jnp.zeros((2, 128, 32), BF)], 0)
-        return v.reshape(3, 4, 128, 32).transpose(0, 2, 1, 3).reshape(3, 128, 128)
-
-    def unpack(v):
-        return v.reshape(3, 128, 4, 32).transpose(0, 2, 1, 3).reshape(12, 128, 32)[:10]
-
-    lo, hi = row_halo(pack(lift[..., 96:]), pack(lift[..., :32]))
-    planes = jnp.concatenate([unpack(lo), lift[..., 32:96], unpack(hi)], -1)
+    planes = jnp.where(d == 0, jnp.concatenate([none, lift[:9]], 0), jnp.concatenate([lift[1:10], none], 0))
     part = part + slab_conv(planes, slab_weights(w_lift))
     out = jax.nn.gelu(reduce_tiles(part, j)).astype(BF).reshape(8, 16, 2, 256)
     return out.transpose(2, 1, 0, 3)

time: 223 us -> 207 us (0.928)
  local copies, waits for them, and re-layouts: 49.2 us -> 28.6 us
  starting transfers between devices: 67.5 us -> 77.8 us
  waiting for transfers between devices: 45.9 us -> 41.3 us
  blocking collectives: 27.1 us -> 31.6 us
  other arithmetic: 12.8 us -> 9.65 us
  Pallas kernels: 2.47 us -> 5.52 us
    slice x9 -> x1, local copies, waits for them, and re-layouts: 11 us -> 0.17 us  [body(): lift = jnp.concatenate([unpack(lo), lift[..., 32:96], unpack(hi)], -1)]
    another operation x5 -> x2, local copies, waits for them, and re-layouts: 10.1 us -> 0.3 us  [the longest x2 9.82 us: body(): up = jnp.stack([jnp.stack([up, zero], 2), jnp.stack([zero, up], 2)], 1)]
    ppermute x4, starting transfers between devices: 22.4 us -> 30.4 us  [row_halo(): lo = lax.ppermute(for_next, 'row', [(i, i + 1) for i in range(15)])]
    ppermute x4, waiting for transfers between devices: 8.05 us -> 2.05 us  [row_halo(): hi = lax.ppermute(for_prev, 'row', [(i + 1, i) for i in range(15)])]
    ppermute x1, waiting for transfers between devices: 13 us -> 18.9 us  [body(): la = lax.ppermute(last_kernel, ALL, p1)]
    reshape x6 -> x0, local copies, waits for them, and re-layouts: 5.43 us -> none  [the longest x1 4.48 us: body(): up.reshape(1024, 1024)]
    all_to_all x2, starting transfers between devices: 9.27 us -> 14 us  [to_slab(): got = lax.all_to_all(mixed, 'col', 0, 0, tiled=True)]
    ppermute x1, waiting for transfers between devices: 4.73 us -> 0.01 us  [body(): lb = lax.ppermute(last_kernel, ALL, p2)]
  transfers between devices with their start and end apart: 25 -> 25, of which waited for: 13 -> 11; matrix products, arithmetic and copies ran while one was open for 24% -> 10% of each run, Pallas kernels for 1% -> 2%
where the time goes in v3:
time: 207 us; the launch traced here: 205 us
  starting transfers between devices  77.8 us (38%)
  waiting for transfers between devices  41.3 us (20%)
  blocking collectives  31.6 us (15%)
  local copies, waits for them, and re-layouts  28.6 us (14%)
  matrix products  9.87 us (5%)
  other arithmetic  9.65 us (5%)
  Pallas kernels  5.52 us (3%)
    ppermute x4, starting transfers between devices, row_halo(): lo = lax.ppermute(for_next, 'row', [(i, i + 1) for i in range(15)])  30.4 us
    ppermute x1, waiting for transfers between devices, body(): la = lax.ppermute(last_kernel, ALL, p1)  18.9 us
    all_gather x1, blocking collectives, body(): got = lax.all_gather(jnp.concatenate([coarse, recv], 0), 'col', axis=0)  16 us
    all_gather x1, blocking collectives, body(): got = lax.all_gather(packed, 'col', axis=0)  15.5 us
    unnamed x42, local copies, waits for them, and re-layouts  15.3 us
    all_to_all x2, starting transfers between devices, to_slab(): got = lax.all_to_all(mixed, 'col', 0, 0, tiled=True)  14 us
    ppermute x4, starting transfers between devices, row_halo(): hi = lax.ppermute(for_prev, 'row', [(i + 1, i) for i in range(15)])  8.74 us
    ppermute x6, waiting for transfers between devices, reduce_tiles(): total = total + lax.ppermute(pair[o].astype(BF), 'col', perm).astype(F32)  7.02 us
  transfers between devices with their start and end apart: 25, of which 11 were waited for; matrix products, arithmetic and copies ran while one was open for 10% of the time, Pallas kernels for 2%

profile of v3, /device:TPU:79, one launch (start us, length us, event | category | flops | bytes accessed | tf_op | source)
XLA Modules:
  0.0 205.1 jit_solution(10000445972485114783)
XLA Ops:
  0.0 4.1 %collective-permute-start.4 = (bf16[27,16,256]{2,1,0:T(8,128)(2,1)}, bf16[27,16,256]{2,1,0:T(8,128)(2,1)S(1)}, u32[]{:S(2)}, u32[]{:S(2)}) collective-permute-start(bf16[27,16,256]{2,1,0:T(8,128)(2,1)} %param.12), channel_id=1, source_target_pairs={{129,0},{128,1},{194,2},{195,3},{181,4},{180,5},{246,6},{247,7},{1... | collective-permute-start | bytes 663560 | tf_op jit(solution)/shard_map/ppermute | solution.py:223
  4.1 1.9 collective-permute-start.3
  6.0 0.9 copy.182
  7.0 0.9 collective-permute-start
  7.9 0.7 fusion.92
  8.9 3.3 %collective-permute-done = bf16[2,16,256]{2,1,0:T(8,128)(2,1)S(1)} collective-permute-done((bf16[2,16,256]{2,1,0:T(8,128)(2,1)S(1)}, bf16[2,16,256]{2,1,0:T(8,128)(2,1)S(1)}, u32[]{:S(2)}, u32[]{:S(2)}) %collective-permute-start) | collective-permute-done | bytes 16416 | tf_op jit(solution)/shard_map/ppermute | solution.py:68
  12.3 2.8 %collective-permute-start.2 = (bf16[9,16,256]{2,1,0:T(8,128)(2,1)S(1)}, bf16[9,16,256]{2,1,0:T(8,128)(2,1)S(1)}, u32[]{:S(2)}, u32[]{:S(2)}) collective-permute-start(bf16[9,16,256]{2,1,0:T(8,128)(2,1)S(1)} %get-tuple-element.72), channel_id=1, source_target_pairs={{16,0},{32,16},{48,32},{64,48},{80,64},{96,80},{112,96},{128,112},... | collective-permute-start | bytes 221192 | tf_op jit(solution)/shard_map/ppermute | solution.py:73
  15.2 6.7 %collective-permute-start.1 = (bf16[9,16,256]{2,1,0:T(8,128)(2,1)S(1)}, bf16[9,16,256]{2,1,0:T(8,128)(2,1)S(1)}, u32[]{:S(2)}, u32[]{:S(2)}) collective-permute-start(bf16[9,16,256]{2,1,0:T(8,128)(2,1)S(1)} %get-tuple-element.71), channel_id=1, source_target_pairs={{0,16},{16,32},{32,48},{48,64},{64,80},{80,96},{96,112},{112,128},... | collective-permute-start | bytes 221192 | tf_op jit(solution)/shard_map/ppermute | solution.py:72
  21.8 1.4 collective-permute-done.1
  23.4 1.6 fusion.21
  25.0 9.0 %all-to-all-start = ((bf16[8,144,128]{2,1,0:T(8,128)(2,1)}), bf16[8,144,128]{2,1,0:T(8,128)(2,1)}, u32[]{:S(2)}, u32[]{:S(2)}) async-start(bf16[8,144,128]{2,1,0:T(8,128)(2,1)} %fusion.21), calls=%async_computation | async-start | bytes 589824 | tf_op jit(solution)/shard_map/all_to_all | solution.py:88
  34.2 1.2 copy.122
  35.5 1.6 reshape.243
  37.1 2.7 %all-to-all-done = bf16[8,144,128]{2,1,0:T(8,128)(2,1)} async-done(((bf16[8,144,128]{2,1,0:T(8,128)(2,1)}), bf16[8,144,128]{2,1,0:T(8,128)(2,1)}, u32[]{:S(2)}, u32[]{:S(2)}) %all-to-all-start) | async-done | bytes 294944 | tf_op jit(solution)/shard_map/all_to_all | solution.py:88
  39.8 1.0 copy.179
  42.6 1.5 convolution_bitcast_fusion
  44.1 1.7 fusion.100
  45.8 1.1 collective-permute-start.5
  46.9 2.6 %collective-permute-done.5 = f32[4,8,16,512]{3,2,0,1:T(8,128)} collective-permute-done((f32[4,8,16,512]{3,2,0,1:T(8,128)}, f32[4,8,16,512]{3,2,0,1:T(8,128)}, u32[]{:S(2)}, u32[]{:S(2)}) %collective-permute-start.5) | collective-permute-done | bytes 1048608 | tf_op jit(solution)/shard_map/ppermute | solution.py:210
  49.5 1.9 copy_add_fusion
  52.5 1.2 collective-permute-start.8
  53.7 1.4 collective-permute-start.6
  55.1 4.6 %copy.133.w_hbm = bf16[27,512,64]{2,1,0:T(8,128)(2,1)} copy(bf16[27,512,64]{1,2,0:T(8,128)(2,1)} %param.14) | data formatting | bytes 3538944 | tf_op args[3]
  59.8 1.4 fusion.105
  61.8 1.1 fusion.47
  63.8 1.2 collective-permute-start.14
  65.0 1.0 collective-permute-done.9
  66.0 16.0 %all-gather = bf16[48,8,512]{2,1,0:T(8,128)(2,1)S(1)} all-gather(bf16[6,8,512]{2,1,0:T(8,128)(2,1)S(1)} %pad_maximum_fusion.10), channel_id=2, replica_groups=mesh['row'=16,'col'=8,'depth'=2] {'col'}, dimensions={0}, use_global_device_ids=true | all-gather | bytes 442368 | tf_op jit(solution)/shard_map/all_gather | solution.py:239
  82.3 3.6 %mid_taps.1 = (bf16[5,64,64]{2,1,0:T(8,128)(2,1)S(1)}, f32[5,64,64]{2,1,0:T(8,128)S(1)}, bf16[5,64,64]{2,1,0:T(8,128)(2,1)S(1)}) custom-call(bf16[7,64,512]{2,1,0:T(8,128)(2,1)S(1)} %maximum_select_fusion.slab_ref, bf16[27,512,64]{2,1,0:T(8,128)(2,1)S(1)} %copy-done.2), custom_call_target="tpu_custom_call" | custom-call | tf_op jit(solution)/shard_map/mid_taps/pallas_call | solution.py:142
  85.9 2.1 %collective-permute-start.11 = (bf16[5,64,64]{2,1,0:T(8,128)(2,1)S(1)}, bf16[5,64,64]{2,1,0:T(8,128)(2,1)S(1)}, u32[]{:S(2)}, u32[]{:S(2)}) collective-permute-start(bf16[5,64,64]{2,1,0:T(8,128)(2,1)S(1)} %get-tuple-element.23), channel_id=1, source_target_pairs={{16,0},{32,16},{48,32},{64,48},{80,64},{96,80},{112,96},{128,112},... | collective-permute-start | bytes 122888 | tf_op jit(solution)/shard_map/ppermute | solution.py:73
  87.9 8.3 %collective-permute-start.10 = (bf16[5,64,64]{2,1,0:T(8,128)(2,1)S(1)}, bf16[5,64,64]{2,1,0:T(8,128)(2,1)S(1)}, u32[]{:S(2)}, u32[]{:S(2)}) collective-permute-start(bf16[5,64,64]{2,1,0:T(8,128)(2,1)S(1)} %get-tuple-element.22), channel_id=1, source_target_pairs={{0,16},{16,32},{32,48},{48,64},{64,80},{80,96},{96,112},{112,128},... | collective-permute-start | bytes 122888 | tf_op jit(solution)/shard_map/ppermute | solution.py:72
  96.3 1.9 collective-permute-start.16
  98.2 7.6 %collective-permute-start.15 = (bf16[9,16,256]{2,1,0:T(8,128)(2,1)S(1)}, bf16[9,16,256]{2,1,0:T(8,128)(2,1)S(1)}, u32[]{:S(2)}, u32[]{:S(2)}) collective-permute-start(bf16[9,16,256]{2,1,0:T(8,128)(2,1)S(1)} %get-tuple-element.69), channel_id=1, source_target_pairs={{0,16},{16,32},{32,48},{48,64},{64,80},{80,96},{96,112},{112,128},... | collective-permute-start | bytes 221192 | tf_op jit(solution)/shard_map/ppermute | solution.py:72
  105.9 2.0 collective-permute-done.16
  107.9 1.6 fusion.24
  109.5 5.0 %all-to-all-start.1 = ((bf16[8,144,128]{2,1,0:T(8,128)(2,1)}), bf16[8,144,128]{2,1,0:T(8,128)(2,1)S(1)}, u32[]{:S(2)}, u32[]{:S(2)}) async-start(bf16[8,144,128]{2,1,0:T(8,128)(2,1)} %fusion.24), calls=%async_computation.1 | async-start | bytes 589824 | tf_op jit(solution)/shard_map/all_to_all | solution.py:88
  114.5 2.0 pad_add_fusion.at_ref
  116.5 1.9 collective-permute-start.12
  118.4 6.4 %collective-permute-start.13 = (bf16[27,32,256]{2,1,0:T(8,128)(2,1)S(1)}, bf16[27,32,256]{2,1,0:T(8,128)(2,1)S(1)}, u32[]{:S(2)}, u32[]{:S(2)}) collective-permute-start(bf16[27,32,256]{2,1,0:T(8,128)(2,1)S(1)} %copy-done.6), channel_id=1, source_target_pairs={{129,0},{128,1},{194,2},{195,3},{181,4},{180,5},{246,6},{247,7},{1... | collective-permute-start | bytes 1327112 | tf_op jit(solution)/shard_map/ppermute | solution.py:229
  125.1 18.9 %collective-permute-done.12 = bf16[27,32,256]{2,1,0:T(8,128)(2,1)S(1)} collective-permute-done((bf16[27,32,256]{2,1,0:T(8,128)(2,1)S(1)}, bf16[27,32,256]{2,1,0:T(8,128)(2,1)S(1)}, u32[]{:S(2)}, u32[]{:S(2)}) %collective-permute-start.12) | collective-permute-done | bytes 442400 | tf_op jit(solution)/shard_map/ppermute | solution.py:228
  144.0 0.8 slice_dynamic-update-slice_fusion.17
  144.7 0.8 slice_dynamic-update-slice_fusion.16
  145.6 0.8 slice_dynamic-update-slice_fusion.15
  147.1 0.7 slice_dynamic-update-slice_fusion.13
  147.8 0.8 slice_dynamic-update-slice_fusion.12
  148.6 0.8 slice_dynamic-update-slice_fusion.11
  149.4 0.8 slice_dynamic-update-slice_fusion.10
  150.2 0.8 slice_dynamic-update-slice_fusion.9
  151.4 1.2 copy.137
  152.6 1.3 copy.153
  154.2 15.5 %all_gather.11.got_ref = bf16[8,3,64,128]{3,2,1,0:T(8,128)(2,1)S(1)} all-gather(bf16[1,3,64,128]{3,2,1,0:T(8,128)(2,1)S(1)} %all_gather_reshape.3), channel_id=1, replica_groups=mesh['row'=16,'col'=8,'depth'=2] {'col'}, dimensions={0}, use_global_device_ids=true | all-gather | bytes 442368 | tf_op jit(solution)/shard_map/all_gather | solution.py:257
  169.7 1.9 lift_planes.1
  171.7 1.9 collective-permute-start.18
  173.8 7.8 %collective-permute-start.17 = (bf16[3,128,128]{2,1,0:T(8,128)(2,1)S(1)}, bf16[3,128,128]{2,1,0:T(8,128)(2,1)S(1)}, u32[]{:S(2)}, u32[]{:S(2)}) collective-permute-start(bf16[3,128,128]{2,1,0:T(8,128)(2,1)S(1)} %get-tuple-element.29), channel_id=1, source_target_pairs={{0,16},{16,32},{32,48},{48,64},{64,80},{80,96},{96,112},{112,128},... | collective-permute-start | bytes 294920 | tf_op jit(solution)/shard_map/ppermute | solution.py:72
  181.7 3.2 %fusion.106 = f32[1024,512]{1,0:T(8,128)S(1)} fusion(bf16[1024,1152]{1,0:T(8,128)(2,1)} %bitcast.65, bf16[1152,512]{1,0:T(8,128)(2,1)S(1)} %bitcast.235), kind=kOutput, calls=%fused_computation.199 | convolution fusion | flops 1207959552 | bytes 5636096 | tf_op jit(solution)/shard_map/dot_general | solution.py:112
  185.0 1.2 copy.139
  188.4 1.5 convolution_add_fusion
  190.5 0.8 collective-permute-start.19
  191.3 2.3 %collective-permute-done.19 = f32[4,8,16,512]{3,2,1,0:T(8,128)S(1)} collective-permute-done((f32[4,8,16,512]{3,2,1,0:T(8,128)S(1)}, f32[4,8,16,512]{3,2,1,0:T(8,128)S(1)}, u32[]{:S(2)}, u32[]{:S(2)}) %collective-permute-start.19) | collective-permute-done | bytes 1048608 | tf_op jit(solution)/shard_map/ppermute | solution.py:210
  194.4 1.9 collective-permute-start.22
  196.3 1.5 collective-permute-start.20
  197.7 2.9 %collective-permute-done.22 = bf16[8,16,512]{2,1,0:T(8,128)(2,1)S(1)} collective-permute-done((bf16[8,16,512]{2,1,0:T(8,128)(2,1)S(1)}, bf16[8,16,512]{2,1,0:T(8,128)(2,1)S(1)}, u32[]{:S(2)}, u32[]{:S(2)}) %collective-permute-start.22) | collective-permute-done | bytes 131104 | tf_op jit(solution)/shard_map/ppermute | solution.py:215
  200.7 3.5 %collective-permute-done.21 = bf16[8,16,512]{2,1,0:T(8,128)(2,1)S(1)} collective-permute-done((bf16[8,16,512]{2,1,0:T(8,128)(2,1)S(1)}, bf16[8,16,512]{2,1,0:T(8,128)(2,1)S(1)}, u32[]{:S(2)}, u32[]{:S(2)}) %collective-permute-start.21) | collective-permute-done | bytes 131104 | tf_op jit(solution)/shard_map/ppermute | solution.py:215
  204.4 0.7 copy.181
  (117 shorter events, 10.8 us)
Async XLA Ops:
  0.0 62.8 %copy-start = (bf16[8,256,512]{2,1,0:T(8,128)(2,1)S(1)}, bf16[8,256,512]{2,1,0:T(8,128)(2,1)}, u32[]{:S(2)}) copy-start(bf16[8,256,512]{2,1,0:T(8,128)(2,1)} %param.13) | copy-start | bytes 6291460
  0.0 23.2 %collective-permute-start.4 = (bf16[27,16,256]{2,1,0:T(8,128)(2,1)}, bf16[27,16,256]{2,1,0:T(8,128)(2,1)S(1)}, u32[]{:S(2)}, u32[]{:S(2)}) collective-permute-start(bf16[27,16,256]{2,1,0:T(8,128)(2,1)} %param.12), channel_id=1, source_target_pairs={{129,0},{128,1},{194,2},{195,3},{181,4},{180,5},{246,6},{247,7},{1... | collective-permute-start | bytes 663560 | tf_op jit(solution)/shard_map/ppermute | solution.py:223
  4.1 19.1 %collective-permute-start.3 = (bf16[27,16,256]{2,1,0:T(8,128)(2,1)}, bf16[27,16,256]{2,1,0:T(8,128)(2,1)S(1)}, u32[]{:S(2)}, u32[]{:S(2)}) collective-permute-start(bf16[27,16,256]{2,1,0:T(8,128)(2,1)} %param.12), channel_id=1, source_target_pairs={{0,0},{1,1},{66,2},{67,3},{20,4},{21,5},{86,6},{87,7},{40,8},{41,9... | collective-permute-start | bytes 663560 | tf_op jit(solution)/shard_map/ppermute | solution.py:223
  7.0 5.3 %collective-permute-start = (bf16[2,16,256]{2,1,0:T(8,128)(2,1)S(1)}, bf16[2,16,256]{2,1,0:T(8,128)(2,1)S(1)}, u32[]{:S(2)}, u32[]{:S(2)}) collective-permute-start(bf16[2,16,256]{2,1,0:T(8,128)(2,1)S(1)} %fusion.91), channel_id=1, source_target_pairs={{0,1},{1,0},{2,3},{3,2},{4,5},{5,4},{6,7},{7,6},{8,9},{9,8},{10,11... | collective-permute-start | bytes 49160 | tf_op jit(solution)/shard_map/ppermute | solution.py:68
  12.3 9.5 %collective-permute-start.2 = (bf16[9,16,256]{2,1,0:T(8,128)(2,1)S(1)}, bf16[9,16,256]{2,1,0:T(8,128)(2,1)S(1)}, u32[]{:S(2)}, u32[]{:S(2)}) collective-permute-start(bf16[9,16,256]{2,1,0:T(8,128)(2,1)S(1)} %get-tuple-element.72), channel_id=1, source_target_pairs={{16,0},{32,16},{48,32},{64,48},{80,64},{96,80},{112,96},{128,112},... | collective-permute-start | bytes 221192 | tf_op jit(solution)/shard_map/ppermute | solution.py:73
  15.2 8.1 %collective-permute-start.1 = (bf16[9,16,256]{2,1,0:T(8,128)(2,1)S(1)}, bf16[9,16,256]{2,1,0:T(8,128)(2,1)S(1)}, u32[]{:S(2)}, u32[]{:S(2)}) collective-permute-start(bf16[9,16,256]{2,1,0:T(8,128)(2,1)S(1)} %get-tuple-element.71), channel_id=1, source_target_pairs={{0,16},{16,32},{32,48},{48,64},{64,80},{80,96},{96,112},{112,128},... | collective-permute-start | bytes 221192 | tf_op jit(solution)/shard_map/ppermute | solution.py:72
  25.0 14.8 %all-to-all-start = ((bf16[8,144,128]{2,1,0:T(8,128)(2,1)}), bf16[8,144,128]{2,1,0:T(8,128)(2,1)}, u32[]{:S(2)}, u32[]{:S(2)}) async-start(bf16[8,144,128]{2,1,0:T(8,128)(2,1)} %fusion.21), calls=%async_computation | async-start | bytes 589824 | tf_op jit(solution)/shard_map/all_to_all | solution.py:88
  41.3 1.3 copy-start.4
  45.8 3.7 %collective-permute-start.5 = (f32[4,8,16,512]{3,2,0,1:T(8,128)}, f32[4,8,16,512]{3,2,0,1:T(8,128)}, u32[]{:S(2)}, u32[]{:S(2)}) collective-permute-start(f32[4,8,16,512]{3,2,0,1:T(8,128)} %get-tuple-element.37), channel_id=1, source_target_pairs={{0,2},{2,0},{4,6},{6,4},{8,10},{10,8},{12,14},{14,12},{1,3},{3,1},... | collective-permute-start | bytes 3145736 | tf_op jit(solution)/shard_map/ppermute | solution.py:210
  52.5 8.8 %collective-permute-start.8 = (bf16[8,16,512]{2,1,0:T(8,128)(2,1)}, bf16[8,16,512]{2,1,0:T(8,128)(2,1)S(1)}, u32[]{:S(2)}, u32[]{:S(2)}) collective-permute-start(bf16[8,16,512]{2,1,0:T(8,128)(2,1)} %get-tuple-element.45), channel_id=1, source_target_pairs={{0,8},{2,10},{4,12},{6,14},{8,0},{10,2},{12,4},{14,6},{1,9},{3,11}... | collective-permute-start | bytes 393224 | tf_op jit(solution)/shard_map/ppermute | solution.py:215
  53.6 8.1 %collective-permute-start.7 = (bf16[8,16,512]{2,1,0:T(8,128)(2,1)}, bf16[8,16,512]{2,1,0:T(8,128)(2,1)S(1)}, u32[]{:S(2)}, u32[]{:S(2)}) collective-permute-start(bf16[8,16,512]{2,1,0:T(8,128)(2,1)} %get-tuple-element.46), channel_id=1, source_target_pairs={{0,12},{2,14},{4,0},{6,2},{8,4},{10,6},{12,8},{14,10},{1,13},{3,15... | collective-permute-start | bytes 393224 | tf_op jit(solution)/shard_map/ppermute | solution.py:215
  53.7 8.0 %collective-permute-start.6 = (bf16[8,16,512]{2,1,0:T(8,128)(2,1)S(1)}, bf16[8,16,512]{2,1,0:T(8,128)(2,1)}, u32[]{:S(2)}, u32[]{:S(2)}) collective-permute-start(bf16[8,16,512]{2,1,0:T(8,128)(2,1)S(1)} %get-tuple-element.44), channel_id=1, source_target_pairs={{0,4},{2,6},{4,8},{6,10},{8,12},{10,14},{12,0},{14,2},{1,5},{3,7},... | collective-permute-start | bytes 393224 | tf_op jit(solution)/shard_map/ppermute | solution.py:215
  63.3 18.9 %copy-start.2 = (bf16[27,512,64]{2,1,0:T(8,128)(2,1)S(1)}, bf16[27,512,64]{2,1,0:T(8,128)(2,1)}, u32[]{:S(2)}) copy-start(bf16[27,512,64]{2,1,0:T(8,128)(2,1)} %copy.133.w_hbm) | copy-start | bytes 5308420
  63.4 2.7 %collective-permute-start.9 = (bf16[2,8,512]{2,1,0:T(8,128)(2,1)S(1)}, bf16[2,8,512]{2,1,0:T(8,128)(2,1)S(1)}, u32[]{:S(2)}, u32[]{:S(2)}) collective-permute-start(bf16[2,8,512]{2,1,0:T(8,128)(2,1)S(1)} %slice_select_fusion.1), channel_id=1, source_target_pairs={{0,1},{1,0},{2,3},{3,2},{4,5},{5,4},{6,7},{7,6},{8,9},{9,8},{10,11... | collective-permute-start | bytes 49160 | tf_op jit(solution)/shard_map/ppermute | solution.py:238
  63.8 32.4 %collective-permute-start.14 = (bf16[2,16,256]{2,1,0:T(8,128)(2,1)S(1)}, bf16[2,16,256]{2,1,0:T(8,128)(2,1)S(1)}, u32[]{:S(2)}, u32[]{:S(2)}) collective-permute-start(bf16[2,16,256]{2,1,0:T(8,128)(2,1)S(1)} %fusion.90), channel_id=1, source_target_pairs={{0,1},{1,0},{2,3},{3,2},{4,5},{5,4},{6,7},{7,6},{8,9},{9,8},{10,11... | collective-permute-start | bytes 49160 | tf_op jit(solution)/shard_map/ppermute | solution.py:68
  85.9 30.7 %copy-start.6 = (bf16[27,32,256]{2,1,0:T(8,128)(2,1)S(1)}, bf16[27,32,256]{2,1,0:T(8,128)(2,1)}, u32[]{:S(2)}) copy-start(bf16[27,32,256]{2,1,0:T(8,128)(2,1)} %param.16) | copy-start | bytes 1327108
  85.9 39.0 %collective-permute-start.11 = (bf16[5,64,64]{2,1,0:T(8,128)(2,1)S(1)}, bf16[5,64,64]{2,1,0:T(8,128)(2,1)S(1)}, u32[]{:S(2)}, u32[]{:S(2)}) collective-permute-start(bf16[5,64,64]{2,1,0:T(8,128)(2,1)S(1)} %get-tuple-element.23), channel_id=1, source_target_pairs={{16,0},{32,16},{48,32},{64,48},{80,64},{96,80},{112,96},{128,112},... | collective-permute-start | bytes 122888 | tf_op jit(solution)/shard_map/ppermute | solution.py:73
  87.9 36.9 %collective-permute-start.10 = (bf16[5,64,64]{2,1,0:T(8,128)(2,1)S(1)}, bf16[5,64,64]{2,1,0:T(8,128)(2,1)S(1)}, u32[]{:S(2)}, u32[]{:S(2)}) collective-permute-start(bf16[5,64,64]{2,1,0:T(8,128)(2,1)S(1)} %get-tuple-element.22), channel_id=1, source_target_pairs={{0,16},{16,32},{32,48},{48,64},{64,80},{80,96},{96,112},{112,128},... | collective-permute-start | bytes 122888 | tf_op jit(solution)/shard_map/ppermute | solution.py:72
  96.3 11.6 %collective-permute-start.16 = (bf16[9,16,256]{2,1,0:T(8,128)(2,1)S(1)}, bf16[9,16,256]{2,1,0:T(8,128)(2,1)S(1)}, u32[]{:S(2)}, u32[]{:S(2)}) collective-permute-start(bf16[9,16,256]{2,1,0:T(8,128)(2,1)S(1)} %get-tuple-element.70), channel_id=1, source_target_pairs={{16,0},{32,16},{48,32},{64,48},{80,64},{96,80},{112,96},{128,112},... | collective-permute-start | bytes 221192 | tf_op jit(solution)/shard_map/ppermute | solution.py:73
  98.2 9.7 %collective-permute-start.15 = (bf16[9,16,256]{2,1,0:T(8,128)(2,1)S(1)}, bf16[9,16,256]{2,1,0:T(8,128)(2,1)S(1)}, u32[]{:S(2)}, u32[]{:S(2)}) collective-permute-start(bf16[9,16,256]{2,1,0:T(8,128)(2,1)S(1)} %get-tuple-element.69), channel_id=1, source_target_pairs={{0,16},{16,32},{32,48},{48,64},{64,80},{80,96},{96,112},{112,128},... | collective-permute-start | bytes 221192 | tf_op jit(solution)/shard_map/ppermute | solution.py:72
  109.5 15.4 %all-to-all-start.1 = ((bf16[8,144,128]{2,1,0:T(8,128)(2,1)}), bf16[8,144,128]{2,1,0:T(8,128)(2,1)S(1)}, u32[]{:S(2)}, u32[]{:S(2)}) async-start(bf16[8,144,128]{2,1,0:T(8,128)(2,1)} %fusion.24), calls=%async_computation.1 | async-start | bytes 589824 | tf_op jit(solution)/shard_map/all_to_all | solution.py:88
  116.5 27.4 %collective-permute-start.12 = (bf16[27,32,256]{2,1,0:T(8,128)(2,1)S(1)}, bf16[27,32,256]{2,1,0:T(8,128)(2,1)S(1)}, u32[]{:S(2)}, u32[]{:S(2)}) collective-permute-start(bf16[27,32,256]{2,1,0:T(8,128)(2,1)S(1)} %copy-done.6), channel_id=1, source_target_pairs={{0,0},{1,1},{66,2},{67,3},{20,4},{21,5},{86,6},{87,7},{40,8},{41,9... | collective-permute-start | bytes 1327112 | tf_op jit(solution)/shard_map/ppermute | solution.py:228
  118.4 25.5 %collective-permute-start.13 = (bf16[27,32,256]{2,1,0:T(8,128)(2,1)S(1)}, bf16[27,32,256]{2,1,0:T(8,128)(2,1)S(1)}, u32[]{:S(2)}, u32[]{:S(2)}) collective-permute-start(bf16[27,32,256]{2,1,0:T(8,128)(2,1)S(1)} %copy-done.6), channel_id=1, source_target_pairs={{129,0},{128,1},{194,2},{195,3},{181,4},{180,5},{246,6},{247,7},{1... | collective-permute-start | bytes 1327112 | tf_op jit(solution)/shard_map/ppermute | solution.py:229
  151.4 18.3 %copy-start.3 = (bf16[8,512,256]{2,1,0:T(8,128)(2,1)S(1)}, bf16[8,512,256]{2,1,0:T(8,128)(2,1)}, u32[]{:S(2)}) copy-start(bf16[8,512,256]{2,1,0:T(8,128)(2,1)} %up_ref.1) | copy-start | bytes 6291460
  169.7 11.9 %copy-start.5 = (bf16[144,8,2,256]{3,1,2,0:T(8,128)(2,1)S(1)}, bf16[144,8,2,256]{3,1,2,0:T(8,128)(2,1)}, u32[]{:S(2)}) copy-start(bf16[144,8,2,256]{3,1,2,0:T(8,128)(2,1)} %copy.153) | copy-start | bytes 3538948
  171.7 14.8 %collective-permute-start.18 = (bf16[3,128,128]{2,1,0:T(8,128)(2,1)S(1)}, bf16[3,128,128]{2,1,0:T(8,128)(2,1)S(1)}, u32[]{:S(2)}, u32[]{:S(2)}) collective-permute-start(bf16[3,128,128]{2,1,0:T(8,128)(2,1)S(1)} %get-tuple-element.31), channel_id=1, source_target_pairs={{16,0},{32,16},{48,32},{64,48},{80,64},{96,80},{112,96},{128,112},... | collective-permute-start | bytes 294920 | tf_op jit(solution)/shard_map/ppermute | solution.py:73
  173.8 13.0 %collective-permute-start.17 = (bf16[3,128,128]{2,1,0:T(8,128)(2,1)S(1)}, bf16[3,128,128]{2,1,0:T(8,128)(2,1)S(1)}, u32[]{:S(2)}, u32[]{:S(2)}) collective-permute-start(bf16[3,128,128]{2,1,0:T(8,128)(2,1)S(1)} %get-tuple-element.29), channel_id=1, source_target_pairs={{0,16},{16,32},{32,48},{48,64},{64,80},{80,96},{96,112},{112,128},... | collective-permute-start | bytes 294920 | tf_op jit(solution)/shard_map/ppermute | solution.py:72
  190.5 3.1 %collective-permute-start.19 = (f32[4,8,16,512]{3,2,1,0:T(8,128)S(1)}, f32[4,8,16,512]{3,2,1,0:T(8,128)S(1)}, u32[]{:S(2)}, u32[]{:S(2)}) collective-permute-start(f32[4,8,16,512]{3,2,1,0:T(8,128)S(1)} %select_bitcast_fusion), channel_id=1, source_target_pairs={{0,2},{2,0},{4,6},{6,4},{8,10},{10,8},{12,14},{14,12},{1,3},{3,1},... | collective-permute-start | bytes 3145736 | tf_op jit(solution)/shard_map/ppermute | solution.py:210
  193.6 11.5 %copy-start.1 = (bf16[8,256,512]{2,1,0:T(8,128)(2,1)S(1)}, bf16[8,256,512]{2,1,0:T(8,128)(2,1)}, u32[]{:S(2)}) copy-start(bf16[8,256,512]{2,1,0:T(8,128)(2,1)} %param.13) | copy-start | bytes 6291460
  194.4 6.3 %collective-permute-start.22 = (bf16[8,16,512]{2,1,0:T(8,128)(2,1)S(1)}, bf16[8,16,512]{2,1,0:T(8,128)(2,1)S(1)}, u32[]{:S(2)}, u32[]{:S(2)}) collective-permute-start(bf16[8,16,512]{2,1,0:T(8,128)(2,1)S(1)} %get-tuple-element.42), channel_id=1, source_target_pairs={{0,8},{2,10},{4,12},{6,14},{8,0},{10,2},{12,4},{14,6},{1,9},{3,11}... | collective-permute-start | bytes 393224 | tf_op jit(solution)/shard_map/ppermute | solution.py:215
  196.3 7.9 %collective-permute-start.21 = (bf16[8,16,512]{2,1,0:T(8,128)(2,1)S(1)}, bf16[8,16,512]{2,1,0:T(8,128)(2,1)S(1)}, u32[]{:S(2)}, u32[]{:S(2)}) collective-permute-start(bf16[8,16,512]{2,1,0:T(8,128)(2,1)S(1)} %get-tuple-element.43), channel_id=1, source_target_pairs={{0,12},{2,14},{4,0},{6,2},{8,4},{10,6},{12,8},{14,10},{1,13},{3,15... | collective-permute-start | bytes 393224 | tf_op jit(solution)/shard_map/ppermute | solution.py:215
  196.3 7.9 %collective-permute-start.20 = (bf16[8,16,512]{2,1,0:T(8,128)(2,1)S(1)}, bf16[8,16,512]{2,1,0:T(8,128)(2,1)S(1)}, u32[]{:S(2)}, u32[]{:S(2)}) collective-permute-start(bf16[8,16,512]{2,1,0:T(8,128)(2,1)S(1)} %get-tuple-element.41), channel_id=1, source_target_pairs={{0,4},{2,6},{4,8},{6,10},{8,12},{10,14},{12,0},{14,2},{1,5},{3,7},... | collective-permute-start | bytes 393224 | tf_op jit(solution)/shard_map/ppermute | solution.py:215

commit v4 on v3

--- a/solution.py
+++ b/solution.py
@@ -81,38 +81,108 @@
     return jnp.stack([lo, t9[0], t9[1], hi])
 
 
-def to_slab(t4, sel, d):
+def to_slab(t4, sel):
     rows = t4.reshape(4, 144, 256)
     sel = sel.reshape(4, 256, 8, 128)
     mixed = jnp.einsum("prc,pcjk->jrk", rows, sel, preferred_element_type=F32).astype(BF)
     got = lax.all_to_all(mixed, "col", 0, 0, tiled=True)
-    planes = got.reshape(8, 9, 16, 128).transpose(1, 0, 2, 3).reshape(9, 128, 128)
-    return z_ends(planes, d)
-
-
-def z_ends(planes, d):
-    last = planes[-1:]
-    none = jnp.zeros_like(last)
-    return jnp.concatenate([jnp.where(d == 0, none, last), planes[:-1], jnp.where(d == 0, last, none)], 0)
-
-
-def slab_weights(w):
-    w = w.reshape(3, 9, 32, 256)
-    zero = jnp.zeros((1, 9, 32, 256), w.dtype)
-    left = jnp.concatenate([w, zero], 0)
-    right = jnp.concatenate([zero, w], 0)
-    both = jnp.stack([left, right], 3)
-    return both.transpose(1, 0, 2, 3, 4).reshape(9, 128, 512)
-
-
-def slab_conv(planes, wt):
-    pad = jnp.pad(planes, ((0, 0), (1, 1), (0, 0)))
-    cols = [pad[c : c + 8, b : b + 128] for b in range(3) for c in range(3)]
-    patches = jnp.concatenate(cols, -1).reshape(1024, 1152)
-    return jnp.dot(patches, wt.reshape(1152, 512), preferred_element_type=F32)
+    return got
 
 
 WHOLE = pl.BlockSpec(memory_space=pltpu.VMEM)
+SCALARS = pl.BlockSpec(memory_space=pltpu.SMEM)
+
+
+def fill_weights(tap, wt_ref):
+    none = jnp.zeros((32, 256), BF)
+    for blk in range(9):
+        for p in range(4):
+            for xo in range(2):
+                rows = slice(128 * blk + 32 * p, 128 * blk + 32 * p + 32)
+                value = tap(9 * (p - xo) + blk) if 0 <= p - xo <= 2 else none
+                wt_ref[rows, 256 * xo : 256 * xo + 256] = value
+
+
+def fill_plane(q, plane, patch_ref):
+    y = lax.broadcasted_iota(jnp.int32, (128, 128), 0)
+    shifted = (
+        jnp.where(y == 0, 0.0, pltpu.roll(plane, 1, 0)),
+        plane,
+        jnp.where(y == 127, 0.0, pltpu.roll(plane, 127, 0)),
+    )
+    for b in range(3):
+        value = shifted[b].astype(BF)
+        for c in range(3):
+            if 0 <= q - c < 8:
+                rows = slice(128 * (q - c), 128 * (q - c) + 128)
+                patch_ref[rows, 128 * (3 * b + c) : 128 * (3 * b + c) + 128] = value
+
+
+def fill_from_exchange(d, got_ref, patch_ref):
+    for z in range(9):
+        plane = jnp.concatenate([got_ref[src, 16 * z : 16 * z + 16].astype(F32) for src in range(8)], 0)
+        if z < 8:
+            fill_plane(z + 1, plane, patch_ref)
+        else:
+            fill_plane(0, jnp.where(d == 1, plane, 0.0), patch_ref)
+            fill_plane(9, jnp.where(d == 0, plane, 0.0), patch_ref)
+
+
+def split_tiles(core, acc, keep_ref, send_ref):
+    acc = acc.reshape(8, 128, 512)
+    for y in range(4):
+        first, second = acc[:, 32 * y : 32 * y + 16], acc[:, 32 * y + 16 : 32 * y + 32]
+        keep_ref[y] = jnp.where(core == 0, first, second)
+        send_ref[y] = jnp.where(core == 0, second, first)
+
+
+def first_body(at_ref, got_ref, wa_ref, wb_ref, keep_ref, send_ref, wt_ref, patch_ref):
+    fill_weights(lambda n: jnp.concatenate([wa_ref[n], wb_ref[n]], 0), wt_ref)
+    fill_from_exchange(at_ref[0], got_ref, patch_ref)
+    acc = jnp.dot(patch_ref[...], wt_ref[...], preferred_element_type=F32)
+    split_tiles(at_ref[1], acc, keep_ref, send_ref)
+
+
+def skip_body(at_ref, got_ref, wa_ref, wb_ref, acc_ref, wt_ref, patch_ref):
+    low = at_ref[2] == 1
+    fill_weights(lambda n: jnp.where(low, wb_ref[n], wa_ref[n]), wt_ref)
+    fill_from_exchange(at_ref[0], got_ref, patch_ref)
+    acc_ref[...] = jnp.dot(patch_ref[...], wt_ref[...], preferred_element_type=F32)
+
+
+def last_body(
+    at_ref, lift_ref, lo_ref, hi_ref, wa_ref, wb_ref, part_ref, keep_ref, send_ref, wt_ref, patch_ref, full_ref
+):
+    low = at_ref[2] == 1
+    d = at_ref[0]
+    fill_weights(lambda n: jnp.where(low, wa_ref[n], wb_ref[n]), wt_ref)
+    group = lax.broadcasted_iota(jnp.int32, (128, 128), 1) // 32
+    for g in range(3):
+        lo, hi = lo_ref[g].astype(F32), hi_ref[g].astype(F32)
+        for k in range(4):
+            plane = lift_ref[4 * g + k].astype(F32)
+            left = pltpu.roll(lo, 128 - 32 * k, 1) if k else lo
+            right = pltpu.roll(hi, 96 - 32 * k, 1) if k < 3 else hi
+            full_ref[4 * g + k] = jnp.where(group == 0, left, jnp.where(group == 3, right, plane))
+    for q in range(1, 9):
+        fill_plane(q, full_ref[q - 1 + 2 * d], patch_ref)
+    fill_plane(0, jnp.where(d == 1, full_ref[1], 0.0), patch_ref)
+    fill_plane(9, jnp.where(d == 0, full_ref[8], 0.0), patch_ref)
+    acc = part_ref[...] + jnp.dot(patch_ref[...], wt_ref[...], preferred_element_type=F32)
+    split_tiles(at_ref[1], acc, keep_ref, send_ref)
+
+
+def slab_call(kernel, at, *arrays, split=True, full=False):
+    tiles = jax.ShapeDtypeStruct((4, 8, 16, 512), F32)
+    return pl.pallas_call(
+        kernel,
+        in_specs=[SCALARS] + [WHOLE] * len(arrays),
+        out_specs=[WHOLE] * 2 if split else WHOLE,
+        out_shape=[tiles] * 2 if split else jax.ShapeDtypeStruct((1024, 512), F32),
+        scratch_shapes=[pltpu.VMEM((1152, 512), BF), pltpu.VMEM((1024, 1152), BF)]
+        + [pltpu.VMEM((12, 128, 128), F32)] * full,
+        compiler_params=pltpu.CompilerParams(vmem_limit_bytes=32 << 20),
+    )(at, *arrays)
 
 
 def mid_body(slab_ref, w_hbm, prev_ref, own_ref, next_ref, w_ref, sems):
@@ -193,7 +263,7 @@
 def lift_planes(at, got, up):
     return pl.pallas_call(
         lift_body,
-        in_specs=[pl.BlockSpec(memory_space=pltpu.SMEM), WHOLE, WHOLE],
+        in_specs=[SCALARS, WHOLE, WHOLE],
         out_specs=[WHOLE] * 3,
         out_shape=[jax.ShapeDtypeStruct((n, 128, 128), BF) for n in (12, 3, 3)],
         scratch_shapes=[pltpu.VMEM((1024, 1024), BF), pltpu.VMEM((12, 128, 128), F32)],
@@ -202,11 +272,8 @@
     )(at, got, up)
 
 
-def reduce_tiles(acc, j):
-    y, c = j // 2, j % 2
-    t = acc.reshape(8, 4, 2, 16, 512).transpose(2, 1, 0, 3, 4)
-    keep = jnp.where(c == 0, t[0], t[1])
-    send = jnp.where(c == 0, t[1], t[0])
+def reduce_tiles(keep, send, j):
+    y = j // 2
     pair = keep + lax.ppermute(send, "col", [(i, i ^ 1) for i in range(8)])
     pair = jnp.roll(pair, -y, 0)
     total = pair[0]
@@ -220,16 +287,17 @@
     r, j, d = (lax.axis_index(a) for a in ALL)
     p1, p2 = shard_perms()
     first_table, skip_table = (jnp.asarray(t) for t in tables())
-    w1 = jnp.concatenate([lax.ppermute(first_kernel, ALL, p) for p in (p1, p2)], 1)
+    wa, wb = (lax.ppermute(first_kernel, ALL, p) for p in (p1, p2))
     in_low = (r // 4 + j % 2) % 4 < 2
 
     tile = volume.transpose(0, 2, 1, 3)
-    t4, w1, last_kernel = lax.optimization_barrier((fine_halo(tile, d), w1, last_kernel))
+    t4, wa, wb, last_kernel = lax.optimization_barrier((fine_halo(tile, d), wa, wb, last_kernel))
     la = lax.ppermute(last_kernel, ALL, p1)
     lb = lax.ppermute(last_kernel, ALL, p2)
-    planes = to_slab(t4, pick(first_table[r]), d)
-    part = slab_conv(planes, slab_weights(w1))
-    skip = jax.nn.gelu(reduce_tiles(part, j)).astype(BF).reshape(8, 16, 2, 256)
+    at = jnp.stack([d, j % 2, in_low.astype(jnp.int32)])
+    got = to_slab(t4, pick(first_table[r]))
+    keep, send = slab_call(first_body, at, got, wa, wb)
+    skip = jax.nn.gelu(reduce_tiles(keep, send, j)).astype(BF).reshape(8, 16, 2, 256)
 
     cells = skip.reshape(4, 2, 8, 2, 2, 256)
     down = down_kernel.reshape(2, 2, 2, 256, 512)
@@ -246,28 +314,21 @@
     lo, hi = row_halo(h[0], h[2])
     middle = jax.nn.gelu(h[1] + lo.astype(F32) + hi.astype(F32)).astype(BF)
 
-    slab_skip = to_slab(fine_halo(skip.transpose(2, 0, 1, 3), d), pick(skip_table[r]), d)
+    slab_skip = to_slab(fine_halo(skip.transpose(2, 0, 1, 3), d), pick(skip_table[r]))
 
     middle, la, lb, slab_skip = lax.optimization_barrier((middle, la, lb, slab_skip))
-    w_lift, w_skip = jnp.where(in_low, la, lb), jnp.where(in_low, lb, la)
-    part = slab_conv(slab_skip, slab_weights(w_skip))
+    part = slab_call(skip_body, at, slab_skip, la, lb, split=False)
 
     packed = jnp.concatenate([middle, jnp.zeros((1, 64, 64), BF)], 0)
     packed = packed.reshape(3, 2, 64, 64).transpose(0, 2, 1, 3).reshape(3, 64, 128)
     got = lax.all_gather(packed, "col", axis=0)
     places = jnp.asarray(lift_table())
-    at = jnp.stack([places[jnp.clip(r + step, 0, 15), j] for step in (-1, 0, 1)])
-    lift, for_next, for_prev = lift_planes(at, got, up_kernel)
-
-    def unpack(v):
-        return v.reshape(3, 128, 4, 32).transpose(0, 2, 1, 3).reshape(12, 128, 32)
+    rows = jnp.stack([places[jnp.clip(r + step, 0, 15), j] for step in (-1, 0, 1)])
+    lift, for_next, for_prev = lift_planes(rows, got, up_kernel)
 
     lo, hi = row_halo(for_next, for_prev)
-    lift = jnp.concatenate([unpack(lo), lift[..., 32:96], unpack(hi)], -1)
-    none = jnp.zeros((1, 128, 128), BF)
-    planes = jnp.where(d == 0, jnp.concatenate([none, lift[:9]], 0), jnp.concatenate([lift[1:10], none], 0))
-    part = part + slab_conv(planes, slab_weights(w_lift))
-    out = jax.nn.gelu(reduce_tiles(part, j)).astype(BF).reshape(8, 16, 2, 256)
+    keep, send = slab_call(last_body, at, lift, lo, hi, la, lb, part, full=True)
+    out = jax.nn.gelu(reduce_tiles(keep, send, j)).astype(BF).reshape(8, 16, 2, 256)
     return out.transpose(2, 1, 0, 3)
 
 

time: 207 us -> 182 us (0.88)
  local copies, waits for them, and re-layouts: 28.6 us -> 13.3 us
  Pallas kernels: 5.52 us -> 13.1 us
  starting transfers between devices: 77.8 us -> 70.6 us
  matrix products: 9.87 us -> 3.68 us
  blocking collectives: 31.6 us -> 26.1 us
  waiting for transfers between devices: 41.3 us -> 45.4 us
    ppermute x1, waiting for transfers between devices: 18.9 us -> 0.01 us  [body(): la = lax.ppermute(last_kernel, ALL, p1)]
    ppermute x4, waiting for transfers between devices: 2.05 us -> 14.5 us  [row_halo(): hi = lax.ppermute(for_prev, 'row', [(i + 1, i) for i in range(15)])]
    pallas_call x1 -> x4, Pallas kernels: 1.93 us -> 9.53 us  [the longest x3 7.61 us: slab_call(): pl.pallas_call(kernel, in_specs=[SCALARS] + [WHOLE] * len(arrays), out_sp...]
    ppermute x1, starting transfers between devices: 6.39 us -> 0.01 us  [body(): lb = lax.ppermute(last_kernel, ALL, p2)]
    unnamed x42 -> x16, local copies, waits for them, and re-layouts: 15.3 us -> 8.94 us
    dot_general x3 -> x0, matrix products: 6.19 us -> none  [slab_conv(): return jnp.dot(patches, wt.reshape(1152, 512), preferred_element_type=F32)]
    ppermute x1, waiting for transfers between devices: 1.01 us -> 7.14 us  [body(): recv = lax.ppermute(send, 'depth', [(0, 1), (1, 0)])]
    all_to_all x2, waiting for transfers between devices: 2.72 us -> 8.37 us  [to_slab(): got = lax.all_to_all(mixed, 'col', 0, 0, tiled=True)]
  transfers between devices with their start and end apart: 25 -> 25, of which waited for: 11 -> 12; matrix products, arithmetic and copies ran while one was open for 10% -> 8% of each run, Pallas kernels for 2% -> 3%
where the time goes in v4:
time: 182 us; the launch traced here: 180 us
  starting transfers between devices  70.6 us (39%)
  waiting for transfers between devices  45.4 us (25%)
  blocking collectives  26.1 us (14%)
  local copies, waits for them, and re-layouts  13.3 us (7%)
  Pallas kernels  13.1 us (7%)
  other arithmetic  7.74 us (4%)
  matrix products  3.68 us (2%)
    ppermute x4, starting transfers between devices, row_halo(): lo = lax.ppermute(for_next, 'row', [(i, i + 1) for i in range(15)])  27.3 us
    ppermute x4, waiting for transfers between devices, row_halo(): hi = lax.ppermute(for_prev, 'row', [(i + 1, i) for i in range(15)])  14.5 us
    all_gather x1, blocking collectives, body(): got = lax.all_gather(packed, 'col', axis=0)  13.3 us
    all_gather x1, blocking collectives, body(): got = lax.all_gather(jnp.concatenate([coarse, recv], 0), 'col', axis=0)  12.8 us
    all_to_all x2, starting transfers between devices, to_slab(): got = lax.all_to_all(mixed, 'col', 0, 0, tiled=True)  11.6 us
    unnamed x16, local copies, waits for them, and re-layouts  8.94 us
    all_to_all x2, waiting for transfers between devices, to_slab(): got = lax.all_to_all(mixed, 'col', 0, 0, tiled=True)  8.37 us
    ppermute x4, starting transfers between devices, row_halo(): hi = lax.ppermute(for_prev, 'row', [(i + 1, i) for i in range(15)])  7.86 us
  transfers between devices with their start and end apart: 25, of which 12 were waited for; matrix products, arithmetic and copies ran while one was open for 8% of the time, Pallas kernels for 3%

profile of v4, /device:TPU:79, one launch (start us, length us, event | category | flops | bytes accessed | tf_op | source)
XLA Modules:
  0.0 180.3 jit_solution(1523991843138645043)
XLA Ops:
  0.0 4.1 %collective-permute-start.4 = (bf16[27,16,256]{2,1,0:T(8,128)(2,1)}, bf16[27,16,256]{2,1,0:T(8,128)(2,1)S(1)}, u32[]{:S(2)}, u32[]{:S(2)}) collective-permute-start(bf16[27,16,256]{2,1,0:T(8,128)(2,1)} %param.12), channel_id=1, source_target_pairs={{129,0},{128,1},{194,2},{195,3},{181,4},{180,5},{246,6},{247,7},{1... | collective-permute-start | bytes 663560 | tf_op jit(solution)/shard_map/ppermute | solution.py:290
  4.1 1.9 %collective-permute-start.3 = (bf16[27,16,256]{2,1,0:T(8,128)(2,1)}, bf16[27,16,256]{2,1,0:T(8,128)(2,1)S(1)}, u32[]{:S(2)}, u32[]{:S(2)}) collective-permute-start(bf16[27,16,256]{2,1,0:T(8,128)(2,1)} %param.12), channel_id=1, source_target_pairs={{0,0},{1,1},{66,2},{67,3},{20,4},{21,5},{86,6},{87,7},{40,8},{41,9... | collective-permute-start | bytes 663560 | tf_op jit(solution)/shard_map/ppermute | solution.py:290
  6.0 0.9 copy.61
  7.0 0.9 collective-permute-start
  7.9 0.7 fusion.84
  8.9 3.4 %collective-permute-done = bf16[2,16,256]{2,1,0:T(8,128)(2,1)S(1)} collective-permute-done((bf16[2,16,256]{2,1,0:T(8,128)(2,1)S(1)}, bf16[2,16,256]{2,1,0:T(8,128)(2,1)S(1)}, u32[]{:S(2)}, u32[]{:S(2)}) %collective-permute-start) | collective-permute-done | bytes 16416 | tf_op jit(solution)/shard_map/ppermute | solution.py:68
  12.3 6.5 %collective-permute-start.1 = (bf16[9,16,256]{2,1,0:T(8,128)(2,1)S(1)}, bf16[9,16,256]{2,1,0:T(8,128)(2,1)S(1)}, u32[]{:S(2)}, u32[]{:S(2)}) collective-permute-start(bf16[9,16,256]{2,1,0:T(8,128)(2,1)S(1)} %get-tuple-element.56), channel_id=1, source_target_pairs={{0,16},{16,32},{32,48},{48,64},{64,80},{80,96},{96,112},{112,128},... | collective-permute-start | bytes 221192 | tf_op jit(solution)/shard_map/ppermute | solution.py:72
  18.8 1.9 %collective-permute-start.2 = (bf16[9,16,256]{2,1,0:T(8,128)(2,1)S(1)}, bf16[9,16,256]{2,1,0:T(8,128)(2,1)S(1)}, u32[]{:S(2)}, u32[]{:S(2)}) collective-permute-start(bf16[9,16,256]{2,1,0:T(8,128)(2,1)S(1)} %get-tuple-element.57), channel_id=1, source_target_pairs={{16,0},{32,16},{48,32},{64,48},{80,64},{96,80},{112,96},{128,112},... | collective-permute-start | bytes 221192 | tf_op jit(solution)/shard_map/ppermute | solution.py:73
  20.8 0.1 collective-permute-done.1
  20.9 8.0 %collective-permute-done.2 = bf16[9,16,256]{2,1,0:T(8,128)(2,1)S(1)} collective-permute-done((bf16[9,16,256]{2,1,0:T(8,128)(2,1)S(1)}, bf16[9,16,256]{2,1,0:T(8,128)(2,1)S(1)}, u32[]{:S(2)}, u32[]{:S(2)}) %collective-permute-start.2) | collective-permute-done | bytes 73760 | tf_op jit(solution)/shard_map/ppermute | solution.py:73
  29.1 1.6 fusion.20
  30.7 4.4 %all-to-all-start = ((bf16[8,144,128]{2,1,0:T(8,128)(2,1)}), bf16[8,144,128]{2,1,0:T(8,128)(2,1)S(1)}, u32[]{:S(2)}, u32[]{:S(2)}) async-start(bf16[8,144,128]{2,1,0:T(8,128)(2,1)} %fusion.20), calls=%async_computation | async-start | bytes 589824 | tf_op jit(solution)/shard_map/all_to_all | solution.py:88
  35.2 5.6 %all-to-all-done.got_ref = bf16[8,144,128]{2,1,0:T(8,128)(2,1)S(1)} async-done(((bf16[8,144,128]{2,1,0:T(8,128)(2,1)}), bf16[8,144,128]{2,1,0:T(8,128)(2,1)S(1)}, u32[]{:S(2)}, u32[]{:S(2)}) %all-to-all-start) | async-done | bytes 294944 | tf_op jit(solution)/shard_map/all_to_all | solution.py:88
  40.8 0.9 copy-done.4
  41.7 0.9 copy-done.6
  42.7 3.1 %shard_map.91 = (f32[4,8,16,512]{3,2,1,0:T(8,128)S(1)}, f32[4,8,16,512]{3,2,1,0:T(8,128)}) custom-call(s32[3]{0:T(128)S(1)} %pad_add_fusion.at_ref, bf16[8,144,128]{2,1,0:T(8,128)(2,1)S(1)} %all-to-all-done.got_ref, bf16[27,16,256]{2,1,0:T(8,128)(2,1)S(1)} %copy-done.6, bf16[27,16,256]{2,1,0:T(8,128)(2,1)S(1)} %copy-done.4), custom_call_target="tpu_custom_call" | custom-call | tf_op jit(solution)/shard_map/pallas_call | solution.py:177
  45.8 1.1 collective-permute-start.5
  46.8 2.6 %collective-permute-done.5 = f32[4,8,16,512]{3,2,1,0:T(8,128)} collective-permute-done((f32[4,8,16,512]{3,2,1,0:T(8,128)}, f32[4,8,16,512]{3,2,1,0:T(8,128)}, u32[]{:S(2)}, u32[]{:S(2)}) %collective-permute-start.5) | collective-permute-done | bytes 1048608 | tf_op jit(solution)/shard_map/ppermute | solution.py:277
  49.5 1.4 add.143
  50.9 1.2 fusion.90
  52.1 0.7 slice_bitcast_fusion.9
  52.8 3.0 %collective-permute-start.8 = (bf16[8,16,512]{2,1,0:T(8,128)(2,1)S(1)}, bf16[8,16,512]{2,1,0:T(8,128)(2,1)S(1)}, u32[]{:S(2)}, u32[]{:S(2)}) collective-permute-start(bf16[8,16,512]{2,1,0:T(8,128)(2,1)S(1)} %get-tuple-element.50), channel_id=1, source_target_pairs={{0,8},{2,10},{4,12},{6,14},{8,0},{10,2},{12,4},{14,6},{1,9},{3,11}... | collective-permute-start | bytes 393224 | tf_op jit(solution)/shard_map/ppermute | solution.py:282
  55.8 0.3 collective-permute-start.7
  56.1 4.5 %copy.36.w_hbm = bf16[27,512,64]{2,1,0:T(8,128)(2,1)} copy(bf16[27,512,64]{1,2,0:T(8,128)(2,1)} %param.14) | data formatting | bytes 3538944 | tf_op args[3]
  60.7 1.4 fusion.92
  62.1 5.2 %collective-permute-start.12 = (bf16[27,32,256]{2,1,0:T(8,128)(2,1)}, bf16[27,32,256]{2,1,0:T(8,128)(2,1)S(1)}, u32[]{:S(2)}, u32[]{:S(2)}) collective-permute-start(bf16[27,32,256]{2,1,0:T(8,128)(2,1)} %param.16), channel_id=1, source_target_pairs={{0,0},{1,1},{66,2},{67,3},{20,4},{21,5},{86,6},{87,7},{40,8},{41,9... | collective-permute-start | bytes 1327112 | tf_op jit(solution)/shard_map/ppermute | solution.py:295
  67.3 1.1 fusion.39
  68.5 0.5 fusion.79
  69.0 2.2 %collective-permute-start.9 = (bf16[2,8,512]{2,1,0:T(8,128)(2,1)S(1)}, bf16[2,8,512]{2,1,0:T(8,128)(2,1)S(1)}, u32[]{:S(2)}, u32[]{:S(2)}) collective-permute-start(bf16[2,8,512]{2,1,0:T(8,128)(2,1)S(1)} %slice_select_fusion.1), channel_id=1, source_target_pairs={{0,1},{1,0},{2,3},{3,2},{4,5},{5,4},{6,7},{7,6},{8,9},{9,8},{10,11... | collective-permute-start | bytes 49160 | tf_op jit(solution)/shard_map/ppermute | solution.py:306
  71.2 0.1 collective-permute-start.14
  71.3 7.1 %collective-permute-done.9 = bf16[2,8,512]{2,1,0:T(8,128)(2,1)S(1)} collective-permute-done((bf16[2,8,512]{2,1,0:T(8,128)(2,1)S(1)}, bf16[2,8,512]{2,1,0:T(8,128)(2,1)S(1)}, u32[]{:S(2)}, u32[]{:S(2)}) %collective-permute-start.9) | collective-permute-done | bytes 16416 | tf_op jit(solution)/shard_map/ppermute | solution.py:306
  78.5 12.8 %all-gather = bf16[48,8,512]{2,1,0:T(8,128)(2,1)S(1)} all-gather(bf16[6,8,512]{2,1,0:T(8,128)(2,1)S(1)} %pad_maximum_fusion.3), channel_id=2, replica_groups=mesh['row'=16,'col'=8,'depth'=2] {'col'}, dimensions={0}, use_global_device_ids=true | all-gather | bytes 442368 | tf_op jit(solution)/shard_map/all_gather | solution.py:307
  91.4 5.4 %collective-permute-start.15 = (bf16[9,16,256]{2,1,0:T(8,128)(2,1)S(1)}, bf16[9,16,256]{2,1,0:T(8,128)(2,1)S(1)}, u32[]{:S(2)}, u32[]{:S(2)}) collective-permute-start(bf16[9,16,256]{2,1,0:T(8,128)(2,1)S(1)} %get-tuple-element.54), channel_id=1, source_target_pairs={{0,16},{16,32},{32,48},{48,64},{64,80},{80,96},{96,112},{112,128},... | collective-permute-start | bytes 221192 | tf_op jit(solution)/shard_map/ppermute | solution.py:72
  96.8 2.1 %collective-permute-start.16 = (bf16[9,16,256]{2,1,0:T(8,128)(2,1)S(1)}, bf16[9,16,256]{2,1,0:T(8,128)(2,1)S(1)}, u32[]{:S(2)}, u32[]{:S(2)}) collective-permute-start(bf16[9,16,256]{2,1,0:T(8,128)(2,1)S(1)} %get-tuple-element.55), channel_id=1, source_target_pairs={{16,0},{32,16},{48,32},{64,48},{80,64},{96,80},{112,96},{128,112},... | collective-permute-start | bytes 221192 | tf_op jit(solution)/shard_map/ppermute | solution.py:73
  98.9 0.1 maximum_select_fusion.slab_ref
  99.0 3.6 %mid_taps.1 = (bf16[5,64,64]{2,1,0:T(8,128)(2,1)}, f32[5,64,64]{2,1,0:T(8,128)S(1)}, bf16[5,64,64]{2,1,0:T(8,128)(2,1)S(1)}) custom-call(bf16[7,64,512]{2,1,0:T(8,128)(2,1)S(1)} %maximum_select_fusion.slab_ref, bf16[27,512,64]{2,1,0:T(8,128)(2,1)S(1)} %copy-done.1), custom_call_target="tpu_custom_call" | custom-call | tf_op jit(solution)/shard_map/mid_taps/pallas_call | solution.py:212
  102.6 7.6 %collective-permute-start.10 = (bf16[5,64,64]{2,1,0:T(8,128)(2,1)}, bf16[5,64,64]{2,1,0:T(8,128)(2,1)}, u32[]{:S(2)}, u32[]{:S(2)}) collective-permute-start(bf16[5,64,64]{2,1,0:T(8,128)(2,1)} %get-tuple-element.30), channel_id=1, source_target_pairs={{0,16},{16,32},{32,48},{48,64},{64,80},{80,96},{96,112},{112,128},... | collective-permute-start | bytes 122888 | tf_op jit(solution)/shard_map/ppermute | solution.py:72
  110.2 1.9 %collective-permute-start.11 = (bf16[5,64,64]{2,1,0:T(8,128)(2,1)S(1)}, bf16[5,64,64]{2,1,0:T(8,128)(2,1)}, u32[]{:S(2)}, u32[]{:S(2)}) collective-permute-start(bf16[5,64,64]{2,1,0:T(8,128)(2,1)S(1)} %get-tuple-element.31), channel_id=1, source_target_pairs={{16,0},{32,16},{48,32},{64,48},{80,64},{96,80},{112,96},{128,112},... | collective-permute-start | bytes 122888 | tf_op jit(solution)/shard_map/ppermute | solution.py:73
  112.2 1.6 fusion.23
  113.8 7.2 %all-to-all-start.1 = ((bf16[8,144,128]{2,1,0:T(8,128)(2,1)}), bf16[8,144,128]{2,1,0:T(8,128)(2,1)S(1)}, u32[]{:S(2)}, u32[]{:S(2)}) async-start(bf16[8,144,128]{2,1,0:T(8,128)(2,1)} %fusion.23), calls=%async_computation.1 | async-start | bytes 589824 | tf_op jit(solution)/shard_map/all_to_all | solution.py:88
  121.0 2.0 %pad_add_fusion.1.at_ref = s32[3]{0:T(128)S(1)} fusion(s32[1]{0:T(128)} %bitcast.5, s32[1]{0:T(128)} %bitcast.4, s32[1]{0:T(128)} %bitcast.3), kind=kLoop, calls=%fused_computation.120 | loop fusion | flops 6 | bytes 24 | tf_op jit(solution)/shard_map/stack | solution.py:326
  122.9 1.0 fusion.61
  124.0 2.7 %all-to-all-done.1.got_ref = bf16[8,144,128]{2,1,0:T(8,128)(2,1)S(1)} async-done(((bf16[8,144,128]{2,1,0:T(8,128)(2,1)}), bf16[8,144,128]{2,1,0:T(8,128)(2,1)S(1)}, u32[]{:S(2)}, u32[]{:S(2)}) %all-to-all-start.1) | async-done | bytes 294944 | tf_op jit(solution)/shard_map/all_to_all | solution.py:88
  126.8 0.1 all_gather_reshape.3
  126.9 13.3 %all_gather.11.got_ref = bf16[8,3,64,128]{3,2,1,0:T(8,128)(2,1)S(1)} all-gather(bf16[1,3,64,128]{3,2,1,0:T(8,128)(2,1)S(1)} %all_gather_reshape.3), channel_id=1, replica_groups=mesh['row'=16,'col'=8,'depth'=2] {'col'}, dimensions={0}, use_global_device_ids=true | all-gather | bytes 442368 | tf_op jit(solution)/shard_map/all_gather | solution.py:324
  140.2 1.6 copy-done.2
  141.8 1.9 %lift_planes.1 = (bf16[12,128,128]{2,1,0:T(8,128)(2,1)S(1)}, bf16[3,128,128]{2,1,0:T(8,128)(2,1)S(1)}, bf16[3,128,128]{2,1,0:T(8,128)(2,1)S(1)}) custom-call(s32[3]{0:T(128)S(1)} %pad_add_fusion.1.at_ref, bf16[8,3,64,128]{3,2,1,0:T(8,128)(2,1)S(1)} %all_gather.11.got_ref, bf16[8,512,256]{2,1,0:T(8,128)(2,1)S(1)} %copy-done.2), custom_call_target="tpu_custom_call" | custom-call | tf_op jit(solution)/shard_map/lift_planes/pallas_call | solution.py:264
  143.7 7.9 %collective-permute-start.17 = (bf16[3,128,128]{2,1,0:T(8,128)(2,1)S(1)}, bf16[3,128,128]{2,1,0:T(8,128)(2,1)S(1)}, u32[]{:S(2)}, u32[]{:S(2)}) collective-permute-start(bf16[3,128,128]{2,1,0:T(8,128)(2,1)S(1)} %get-tuple-element.35), channel_id=1, source_target_pairs={{0,16},{16,32},{32,48},{48,64},{64,80},{80,96},{96,112},{112,128},... | collective-permute-start | bytes 294920 | tf_op jit(solution)/shard_map/ppermute | solution.py:72
  151.6 1.9 %collective-permute-start.18 = (bf16[3,128,128]{2,1,0:T(8,128)(2,1)S(1)}, bf16[3,128,128]{2,1,0:T(8,128)(2,1)S(1)}, u32[]{:S(2)}, u32[]{:S(2)}) collective-permute-start(bf16[3,128,128]{2,1,0:T(8,128)(2,1)S(1)} %get-tuple-element.36), channel_id=1, source_target_pairs={{16,0},{32,16},{48,32},{64,48},{80,64},{96,80},{112,96},{128,112},... | collective-permute-start | bytes 294920 | tf_op jit(solution)/shard_map/ppermute | solution.py:73
  153.5 2.1 %shard_map.92.part_ref = f32[1024,512]{1,0:T(8,128)S(1)} custom-call(s32[3]{0:T(128)S(1)} %pad_add_fusion.at_ref, bf16[8,144,128]{2,1,0:T(8,128)(2,1)S(1)} %all-to-all-done.1.got_ref, bf16[27,32,256]{2,1,0:T(8,128)(2,1)S(1)} %collective-permute-done.12.wa_ref, bf16[27,32,256]{2,1,0:T(8,128)(2,1)S(1)} %collective-permute-done.13.wb_ref), custom_call_target="tpu_custom_call" | custom-call | tf_op jit(solution)/shard_map/pallas_call | solution.py:177
  155.6 6.5 %collective-permute-done.18.hi_ref = bf16[3,128,128]{2,1,0:T(8,128)(2,1)S(1)} collective-permute-done((bf16[3,128,128]{2,1,0:T(8,128)(2,1)S(1)}, bf16[3,128,128]{2,1,0:T(8,128)(2,1)S(1)}, u32[]{:S(2)}, u32[]{:S(2)}) %collective-permute-start.18) | collective-permute-done | bytes 98336 | tf_op jit(solution)/shard_map/ppermute | solution.py:73
  162.1 2.4 %shard_map.93 = (f32[4,8,16,512]{3,2,1,0:T(8,128)S(1)}, f32[4,8,16,512]{3,2,1,0:T(8,128)S(1)}) custom-call(s32[3]{0:T(128)S(1)} %pad_add_fusion.at_ref, bf16[12,128,128]{2,1,0:T(8,128)(2,1)S(1)} %get-tuple-element.34.lift_ref, bf16[3,128,128]{2,1,0:T(8,128)(2,1)S(1)} %collective-permute-done.17.lo_ref, ...), custom_call_target="tpu_custom_call" | custom-call | tf_op jit(solution)/shard_map/pallas_call | solution.py:177
  164.6 1.1 collective-permute-start.19
  165.7 2.3 %collective-permute-done.19 = f32[4,8,16,512]{3,2,1,0:T(8,128)S(1)} collective-permute-done((f32[4,8,16,512]{3,2,1,0:T(8,128)S(1)}, f32[4,8,16,512]{3,2,1,0:T(8,128)S(1)}, u32[]{:S(2)}, u32[]{:S(2)}) %collective-permute-start.19) | collective-permute-done | bytes 1048608 | tf_op jit(solution)/shard_map/ppermute | solution.py:277
  168.0 0.2 add.158
  168.2 0.3 fusion.88
  168.5 1.3 collective-permute-start.20
  169.8 2.4 %collective-permute-start.22 = (bf16[8,16,512]{2,1,0:T(8,128)(2,1)S(1)}, bf16[8,16,512]{2,1,0:T(8,128)(2,1)S(1)}, u32[]{:S(2)}, u32[]{:S(2)}) collective-permute-start(bf16[8,16,512]{2,1,0:T(8,128)(2,1)S(1)} %get-tuple-element.47), channel_id=1, source_target_pairs={{0,8},{2,10},{4,12},{6,14},{8,0},{10,2},{12,4},{14,6},{1,9},{3,11}... | collective-permute-start | bytes 393224 | tf_op jit(solution)/shard_map/ppermute | solution.py:282
  172.2 0.3 collective-permute-start.21
  172.5 1.5 collective-permute-done.20
  173.9 1.8 collective-permute-done.22
  175.7 3.6 %collective-permute-done.21 = bf16[8,16,512]{2,1,0:T(8,128)(2,1)S(1)} collective-permute-done((bf16[8,16,512]{2,1,0:T(8,128)(2,1)S(1)}, bf16[8,16,512]{2,1,0:T(8,128)(2,1)S(1)}, u32[]{:S(2)}, u32[]{:S(2)}) %collective-permute-start.21) | collective-permute-done | bytes 131104 | tf_op jit(solution)/shard_map/ppermute | solution.py:282
  179.4 0.1 fusion.47
  179.5 0.7 copy.60
  (56 shorter events, 1.0 us)
Async XLA Ops:
  0.0 68.5 %copy-start = (bf16[8,256,512]{2,1,0:T(8,128)(2,1)S(1)}, bf16[8,256,512]{2,1,0:T(8,128)(2,1)}, u32[]{:S(2)}) copy-start(bf16[8,256,512]{2,1,0:T(8,128)(2,1)} %param.13) | copy-start | bytes 6291460
  0.0 29.0 %collective-permute-start.4 = (bf16[27,16,256]{2,1,0:T(8,128)(2,1)}, bf16[27,16,256]{2,1,0:T(8,128)(2,1)S(1)}, u32[]{:S(2)}, u32[]{:S(2)}) collective-permute-start(bf16[27,16,256]{2,1,0:T(8,128)(2,1)} %param.12), channel_id=1, source_target_pairs={{129,0},{128,1},{194,2},{195,3},{181,4},{180,5},{246,6},{247,7},{1... | collective-permute-start | bytes 663560 | tf_op jit(solution)/shard_map/ppermute | solution.py:290
  4.1 24.9 %collective-permute-start.3 = (bf16[27,16,256]{2,1,0:T(8,128)(2,1)}, bf16[27,16,256]{2,1,0:T(8,128)(2,1)S(1)}, u32[]{:S(2)}, u32[]{:S(2)}) collective-permute-start(bf16[27,16,256]{2,1,0:T(8,128)(2,1)} %param.12), channel_id=1, source_target_pairs={{0,0},{1,1},{66,2},{67,3},{20,4},{21,5},{86,6},{87,7},{40,8},{41,9... | collective-permute-start | bytes 663560 | tf_op jit(solution)/shard_map/ppermute | solution.py:290
  7.0 5.3 %collective-permute-start = (bf16[2,16,256]{2,1,0:T(8,128)(2,1)S(1)}, bf16[2,16,256]{2,1,0:T(8,128)(2,1)S(1)}, u32[]{:S(2)}, u32[]{:S(2)}) collective-permute-start(bf16[2,16,256]{2,1,0:T(8,128)(2,1)S(1)} %fusion.83), channel_id=1, source_target_pairs={{0,1},{1,0},{2,3},{3,2},{4,5},{5,4},{6,7},{7,6},{8,9},{9,8},{10,11... | collective-permute-start | bytes 49160 | tf_op jit(solution)/shard_map/ppermute | solution.py:68
  12.3 8.6 %collective-permute-start.1 = (bf16[9,16,256]{2,1,0:T(8,128)(2,1)S(1)}, bf16[9,16,256]{2,1,0:T(8,128)(2,1)S(1)}, u32[]{:S(2)}, u32[]{:S(2)}) collective-permute-start(bf16[9,16,256]{2,1,0:T(8,128)(2,1)S(1)} %get-tuple-element.56), channel_id=1, source_target_pairs={{0,16},{16,32},{32,48},{48,64},{64,80},{80,96},{96,112},{112,128},... | collective-permute-start | bytes 221192 | tf_op jit(solution)/shard_map/ppermute | solution.py:72
  18.8 10.1 %collective-permute-start.2 = (bf16[9,16,256]{2,1,0:T(8,128)(2,1)S(1)}, bf16[9,16,256]{2,1,0:T(8,128)(2,1)S(1)}, u32[]{:S(2)}, u32[]{:S(2)}) collective-permute-start(bf16[9,16,256]{2,1,0:T(8,128)(2,1)S(1)} %get-tuple-element.57), channel_id=1, source_target_pairs={{16,0},{32,16},{48,32},{64,48},{80,64},{96,80},{112,96},{128,112},... | collective-permute-start | bytes 221192 | tf_op jit(solution)/shard_map/ppermute | solution.py:73
  29.0 1.7 copy-start.3
  29.0 1.6 copy-start.5
  30.7 10.1 %all-to-all-start = ((bf16[8,144,128]{2,1,0:T(8,128)(2,1)}), bf16[8,144,128]{2,1,0:T(8,128)(2,1)S(1)}, u32[]{:S(2)}, u32[]{:S(2)}) async-start(bf16[8,144,128]{2,1,0:T(8,128)(2,1)} %fusion.20), calls=%async_computation | async-start | bytes 589824 | tf_op jit(solution)/shard_map/all_to_all | solution.py:88
  40.8 0.9 copy-start.4
  41.7 0.9 copy-start.6
  45.8 3.7 %collective-permute-start.5 = (f32[4,8,16,512]{3,2,1,0:T(8,128)}, f32[4,8,16,512]{3,2,1,0:T(8,128)}, u32[]{:S(2)}, u32[]{:S(2)}) collective-permute-start(f32[4,8,16,512]{3,2,1,0:T(8,128)} %get-tuple-element.28), channel_id=1, source_target_pairs={{0,2},{2,0},{4,6},{6,4},{8,10},{10,8},{12,14},{14,12},{1,3},{3,1},... | collective-permute-start | bytes 3145736 | tf_op jit(solution)/shard_map/ppermute | solution.py:277
  52.8 14.5 %collective-permute-start.6 = (bf16[8,16,512]{2,1,0:T(8,128)(2,1)}, bf16[8,16,512]{2,1,0:T(8,128)(2,1)S(1)}, u32[]{:S(2)}, u32[]{:S(2)}) collective-permute-start(bf16[8,16,512]{2,1,0:T(8,128)(2,1)} %get-tuple-element.49), channel_id=1, source_target_pairs={{0,4},{2,6},{4,8},{6,10},{8,12},{10,14},{12,0},{14,2},{1,5},{3,7},... | collective-permute-start | bytes 393224 | tf_op jit(solution)/shard_map/ppermute | solution.py:282
  52.8 14.5 %collective-permute-start.8 = (bf16[8,16,512]{2,1,0:T(8,128)(2,1)S(1)}, bf16[8,16,512]{2,1,0:T(8,128)(2,1)S(1)}, u32[]{:S(2)}, u32[]{:S(2)}) collective-permute-start(bf16[8,16,512]{2,1,0:T(8,128)(2,1)S(1)} %get-tuple-element.50), channel_id=1, source_target_pairs={{0,8},{2,10},{4,12},{6,14},{8,0},{10,2},{12,4},{14,6},{1,9},{3,11}... | collective-permute-start | bytes 393224 | tf_op jit(solution)/shard_map/ppermute | solution.py:282
  55.8 11.5 %collective-permute-start.7 = (bf16[8,16,512]{2,1,0:T(8,128)(2,1)S(1)}, bf16[8,16,512]{2,1,0:T(8,128)(2,1)}, u32[]{:S(2)}, u32[]{:S(2)}) collective-permute-start(bf16[8,16,512]{2,1,0:T(8,128)(2,1)S(1)} %get-tuple-element.51), channel_id=1, source_target_pairs={{0,12},{2,14},{4,0},{6,2},{8,4},{10,6},{12,8},{14,10},{1,13},{3,15... | collective-permute-start | bytes 393224 | tf_op jit(solution)/shard_map/ppermute | solution.py:282
  62.1 61.8 %collective-permute-start.13 = (bf16[27,32,256]{2,1,0:T(8,128)(2,1)}, bf16[27,32,256]{2,1,0:T(8,128)(2,1)S(1)}, u32[]{:S(2)}, u32[]{:S(2)}) collective-permute-start(bf16[27,32,256]{2,1,0:T(8,128)(2,1)} %param.16), channel_id=1, source_target_pairs={{129,0},{128,1},{194,2},{195,3},{181,4},{180,5},{246,6},{247,7},{1... | collective-permute-start | bytes 1327112 | tf_op jit(solution)/shard_map/ppermute | solution.py:296
  62.1 61.8 %collective-permute-start.12 = (bf16[27,32,256]{2,1,0:T(8,128)(2,1)}, bf16[27,32,256]{2,1,0:T(8,128)(2,1)S(1)}, u32[]{:S(2)}, u32[]{:S(2)}) collective-permute-start(bf16[27,32,256]{2,1,0:T(8,128)(2,1)} %param.16), channel_id=1, source_target_pairs={{0,0},{1,1},{66,2},{67,3},{20,4},{21,5},{86,6},{87,7},{40,8},{41,9... | collective-permute-start | bytes 1327112 | tf_op jit(solution)/shard_map/ppermute | solution.py:295
  69.0 9.4 %collective-permute-start.9 = (bf16[2,8,512]{2,1,0:T(8,128)(2,1)S(1)}, bf16[2,8,512]{2,1,0:T(8,128)(2,1)S(1)}, u32[]{:S(2)}, u32[]{:S(2)}) collective-permute-start(bf16[2,8,512]{2,1,0:T(8,128)(2,1)S(1)} %slice_select_fusion.1), channel_id=1, source_target_pairs={{0,1},{1,0},{2,3},{3,2},{4,5},{5,4},{6,7},{7,6},{8,9},{9,8},{10,11... | collective-permute-start | bytes 49160 | tf_op jit(solution)/shard_map/ppermute | solution.py:306
  71.2 20.1 %collective-permute-start.14 = (bf16[2,16,256]{2,1,0:T(8,128)(2,1)S(1)}, bf16[2,16,256]{2,1,0:T(8,128)(2,1)S(1)}, u32[]{:S(2)}, u32[]{:S(2)}) collective-permute-start(bf16[2,16,256]{2,1,0:T(8,128)(2,1)S(1)} %fusion.82), channel_id=1, source_target_pairs={{0,1},{1,0},{2,3},{3,2},{4,5},{5,4},{6,7},{7,6},{8,9},{9,8},{10,11... | collective-permute-start | bytes 49160 | tf_op jit(solution)/shard_map/ppermute | solution.py:68
  78.4 20.6 %copy-start.1 = (bf16[27,512,64]{2,1,0:T(8,128)(2,1)S(1)}, bf16[27,512,64]{2,1,0:T(8,128)(2,1)}, u32[]{:S(2)}) copy-start(bf16[27,512,64]{2,1,0:T(8,128)(2,1)} %copy.36.w_hbm) | copy-start | bytes 5308420
  91.4 18.9 %collective-permute-start.15 = (bf16[9,16,256]{2,1,0:T(8,128)(2,1)S(1)}, bf16[9,16,256]{2,1,0:T(8,128)(2,1)S(1)}, u32[]{:S(2)}, u32[]{:S(2)}) collective-permute-start(bf16[9,16,256]{2,1,0:T(8,128)(2,1)S(1)} %get-tuple-element.54), channel_id=1, source_target_pairs={{0,16},{16,32},{32,48},{48,64},{64,80},{80,96},{96,112},{112,128},... | collective-permute-start | bytes 221192 | tf_op jit(solution)/shard_map/ppermute | solution.py:72
  96.8 15.4 %collective-permute-start.16 = (bf16[9,16,256]{2,1,0:T(8,128)(2,1)S(1)}, bf16[9,16,256]{2,1,0:T(8,128)(2,1)S(1)}, u32[]{:S(2)}, u32[]{:S(2)}) collective-permute-start(bf16[9,16,256]{2,1,0:T(8,128)(2,1)S(1)} %get-tuple-element.55), channel_id=1, source_target_pairs={{16,0},{32,16},{48,32},{64,48},{80,64},{96,80},{112,96},{128,112},... | collective-permute-start | bytes 221192 | tf_op jit(solution)/shard_map/ppermute | solution.py:73
  102.6 20.3 %collective-permute-start.10 = (bf16[5,64,64]{2,1,0:T(8,128)(2,1)}, bf16[5,64,64]{2,1,0:T(8,128)(2,1)}, u32[]{:S(2)}, u32[]{:S(2)}) collective-permute-start(bf16[5,64,64]{2,1,0:T(8,128)(2,1)} %get-tuple-element.30), channel_id=1, source_target_pairs={{0,16},{16,32},{32,48},{48,64},{64,80},{80,96},{96,112},{112,128},... | collective-permute-start | bytes 122888 | tf_op jit(solution)/shard_map/ppermute | solution.py:72
  110.2 12.7 %collective-permute-start.11 = (bf16[5,64,64]{2,1,0:T(8,128)(2,1)S(1)}, bf16[5,64,64]{2,1,0:T(8,128)(2,1)}, u32[]{:S(2)}, u32[]{:S(2)}) collective-permute-start(bf16[5,64,64]{2,1,0:T(8,128)(2,1)S(1)} %get-tuple-element.31), channel_id=1, source_target_pairs={{16,0},{32,16},{48,32},{64,48},{80,64},{96,80},{112,96},{128,112},... | collective-permute-start | bytes 122888 | tf_op jit(solution)/shard_map/ppermute | solution.py:73
  113.8 12.9 %all-to-all-start.1 = ((bf16[8,144,128]{2,1,0:T(8,128)(2,1)}), bf16[8,144,128]{2,1,0:T(8,128)(2,1)S(1)}, u32[]{:S(2)}, u32[]{:S(2)}) async-start(bf16[8,144,128]{2,1,0:T(8,128)(2,1)} %fusion.23), calls=%async_computation.1 | async-start | bytes 589824 | tf_op jit(solution)/shard_map/all_to_all | solution.py:88
  140.2 1.6 copy-start.2
  143.7 11.9 %collective-permute-start.17 = (bf16[3,128,128]{2,1,0:T(8,128)(2,1)S(1)}, bf16[3,128,128]{2,1,0:T(8,128)(2,1)S(1)}, u32[]{:S(2)}, u32[]{:S(2)}) collective-permute-start(bf16[3,128,128]{2,1,0:T(8,128)(2,1)S(1)} %get-tuple-element.35), channel_id=1, source_target_pairs={{0,16},{16,32},{32,48},{48,64},{64,80},{80,96},{96,112},{112,128},... | collective-permute-start | bytes 294920 | tf_op jit(solution)/shard_map/ppermute | solution.py:72
  151.6 10.5 %collective-permute-start.18 = (bf16[3,128,128]{2,1,0:T(8,128)(2,1)S(1)}, bf16[3,128,128]{2,1,0:T(8,128)(2,1)S(1)}, u32[]{:S(2)}, u32[]{:S(2)}) collective-permute-start(bf16[3,128,128]{2,1,0:T(8,128)(2,1)S(1)} %get-tuple-element.36), channel_id=1, source_target_pairs={{16,0},{32,16},{48,32},{64,48},{80,64},{96,80},{112,96},{128,112},... | collective-permute-start | bytes 294920 | tf_op jit(solution)/shard_map/ppermute | solution.py:73
  164.6 3.4 %collective-permute-start.19 = (f32[4,8,16,512]{3,2,1,0:T(8,128)S(1)}, f32[4,8,16,512]{3,2,1,0:T(8,128)S(1)}, u32[]{:S(2)}, u32[]{:S(2)}) collective-permute-start(f32[4,8,16,512]{3,2,1,0:T(8,128)S(1)} %get-tuple-element.41), channel_id=1, source_target_pairs={{0,2},{2,0},{4,6},{6,4},{8,10},{10,8},{12,14},{14,12},{1,3},{3,1},... | collective-permute-start | bytes 3145736 | tf_op jit(solution)/shard_map/ppermute | solution.py:277
  168.5 5.4 %collective-permute-start.20 = (bf16[8,16,512]{2,1,0:T(8,128)(2,1)S(1)}, bf16[8,16,512]{2,1,0:T(8,128)(2,1)S(1)}, u32[]{:S(2)}, u32[]{:S(2)}) collective-permute-start(bf16[8,16,512]{2,1,0:T(8,128)(2,1)S(1)} %get-tuple-element.46), channel_id=1, source_target_pairs={{0,4},{2,6},{4,8},{6,10},{8,12},{10,14},{12,0},{14,2},{1,5},{3,7},... | collective-permute-start | bytes 393224 | tf_op jit(solution)/shard_map/ppermute | solution.py:282
  169.8 5.9 %collective-permute-start.22 = (bf16[8,16,512]{2,1,0:T(8,128)(2,1)S(1)}, bf16[8,16,512]{2,1,0:T(8,128)(2,1)S(1)}, u32[]{:S(2)}, u32[]{:S(2)}) collective-permute-start(bf16[8,16,512]{2,1,0:T(8,128)(2,1)S(1)} %get-tuple-element.47), channel_id=1, source_target_pairs={{0,8},{2,10},{4,12},{6,14},{8,0},{10,2},{12,4},{14,6},{1,9},{3,11}... | collective-permute-start | bytes 393224 | tf_op jit(solution)/shard_map/ppermute | solution.py:282
  172.2 7.1 %collective-permute-start.21 = (bf16[8,16,512]{2,1,0:T(8,128)(2,1)S(1)}, bf16[8,16,512]{2,1,0:T(8,128)(2,1)S(1)}, u32[]{:S(2)}, u32[]{:S(2)}) collective-permute-start(bf16[8,16,512]{2,1,0:T(8,128)(2,1)S(1)} %get-tuple-element.48), channel_id=1, source_target_pairs={{0,12},{2,14},{4,0},{6,2},{8,4},{10,6},{12,8},{14,10},{1,13},{3,15... | collective-permute-start | bytes 393224 | tf_op jit(solution)/shard_map/ppermute | solution.py:282

commit v5 on v4

--- a/solution.py
+++ b/solution.py
@@ -287,11 +287,12 @@
     r, j, d = (lax.axis_index(a) for a in ALL)
     p1, p2 = shard_perms()
     first_table, skip_table = (jnp.asarray(t) for t in tables())
-    wa, wb = (lax.ppermute(first_kernel, ALL, p) for p in (p1, p2))
+    wa = lax.ppermute(first_kernel, ALL, p1)
+    wb = lax.ppermute(first_kernel, ALL, p2)
     in_low = (r // 4 + j % 2) % 4 < 2
 
     tile = volume.transpose(0, 2, 1, 3)
-    t4, wa, wb, last_kernel = lax.optimization_barrier((fine_halo(tile, d), wa, wb, last_kernel))
+    t4, last_kernel = lax.optimization_barrier((fine_halo(tile, d), last_kernel))
     la = lax.ppermute(last_kernel, ALL, p1)
     lb = lax.ppermute(last_kernel, ALL, p2)
     at = jnp.stack([d, j % 2, in_low.astype(jnp.int32)])
@@ -316,7 +317,7 @@
 
     slab_skip = to_slab(fine_halo(skip.transpose(2, 0, 1, 3), d), pick(skip_table[r]))
 
-    middle, la, lb, slab_skip = lax.optimization_barrier((middle, la, lb, slab_skip))
+    middle, la, lb = lax.optimization_barrier((middle, la, lb))
     part = slab_call(skip_body, at, slab_skip, la, lb, split=False)
 
     packed = jnp.concatenate([middle, jnp.zeros((1, 64, 64), BF)], 0)

time: 182 us -> 187 us (1.027)
  local copies, waits for them, and re-layouts: 13.3 us -> 15.6 us
    all_to_all x2, waiting for transfers between devices: 8.37 us -> 0.01 us  [to_slab(): got = lax.all_to_all(mixed, 'col', 0, 0, tiled=True)]
    ppermute x4, starting transfers between devices: 27.3 us -> 19.6 us  [row_halo(): lo = lax.ppermute(for_next, 'row', [(i, i + 1) for i in range(15)])]
    ppermute x4, waiting for transfers between devices: 14.5 us -> 21.8 us  [row_halo(): hi = lax.ppermute(for_prev, 'row', [(i + 1, i) for i in range(15)])]
    ppermute x2, waiting for transfers between devices: 0.01 us -> 7.19 us  [the longest x1 3.87 us: body(): wa = lax.ppermute(first_kernel, ALL, p1)]
    all_to_all x2, starting transfers between devices: 11.6 us -> 16.1 us  [to_slab(): got = lax.all_to_all(mixed, 'col', 0, 0, tiled=True)]
    ppermute x2, waiting for transfers between devices: 3.36 us -> 0.05 us  [edge_swap(): return lax.ppermute(send, 'depth', [(0, 1), (1, 0)])]
    ppermute x6, starting transfers between devices: 7.19 us -> 9.93 us  [reduce_tiles(): total = total + lax.ppermute(pair[o].astype(BF), 'col', perm).astype(F32)]
    unnamed x16 -> x22, local copies, waits for them, and re-layouts: 8.94 us -> 11.3 us
  transfers between devices with their start and end apart: 25 -> 25, of which waited for: 12 -> 12; matrix products, arithmetic and copies ran while one was open for 8% -> 6% of each run, Pallas kernels for 3% -> 4%
where the time goes in v5:
time: 187 us; the launch traced here: 185 us
  starting transfers between devices  69.2 us (37%)
  waiting for transfers between devices  47 us (25%)
  blocking collectives  27.4 us (15%)
  local copies, waits for them, and re-layouts  15.6 us (8%)
  Pallas kernels  13.8 us (7%)
  other arithmetic  6.84 us (4%)
  matrix products  4.62 us (2%)
    ppermute x4, waiting for transfers between devices, row_halo(): hi = lax.ppermute(for_prev, 'row', [(i + 1, i) for i in range(15)])  21.8 us
    ppermute x4, starting transfers between devices, row_halo(): lo = lax.ppermute(for_next, 'row', [(i, i + 1) for i in range(15)])  19.6 us
    all_to_all x2, starting transfers between devices, to_slab(): got = lax.all_to_all(mixed, 'col', 0, 0, tiled=True)  16.1 us
    all_gather x1, blocking collectives, body(): got = lax.all_gather(packed, 'col', axis=0)  13.7 us
    all_gather x1, blocking collectives, body(): got = lax.all_gather(jnp.concatenate([coarse, recv], 0), 'col', axis=0)  13.7 us
    unnamed x22, local copies, waits for them, and re-layouts  11.3 us
    ppermute x6, starting transfers between devices, reduce_tiles(): total = total + lax.ppermute(pair[o].astype(BF), 'col', perm).astype(F32)  9.93 us
    ppermute x4, starting transfers between devices, row_halo(): hi = lax.ppermute(for_prev, 'row', [(i + 1, i) for i in range(15)])  9.12 us
  transfers between devices with their start and end apart: 25, of which 12 were waited for; matrix products, arithmetic and copies ran while one was open for 6% of the time, Pallas kernels for 4%

profile of v5, /device:TPU:79, one launch (start us, length us, event | category | flops | bytes accessed | tf_op | source)
XLA Modules:
  0.0 184.9 jit_solution(2476984117377078256)
XLA Ops:
  0.0 1.1 copy.61
  1.1 1.7 collective-permute-start
  2.8 0.7 fusion.84
  4.0 6.0 %collective-permute-start.1 = (bf16[9,16,256]{2,1,0:T(8,128)(2,1)S(1)}, bf16[9,16,256]{2,1,0:T(8,128)(2,1)S(1)}, u32[]{:S(2)}, u32[]{:S(2)}) collective-permute-start(bf16[9,16,256]{2,1,0:T(8,128)(2,1)S(1)} %get-tuple-element.50), channel_id=1, source_target_pairs={{0,16},{16,32},{32,48},{48,64},{64,80},{80,96},{96,112},{112,128},... | collective-permute-start | bytes 221192 | tf_op jit(solution)/shard_map/ppermute | solution.py:72
  10.0 1.9 %collective-permute-start.2 = (bf16[9,16,256]{2,1,0:T(8,128)(2,1)S(1)}, bf16[9,16,256]{2,1,0:T(8,128)(2,1)S(1)}, u32[]{:S(2)}, u32[]{:S(2)}) collective-permute-start(bf16[9,16,256]{2,1,0:T(8,128)(2,1)S(1)} %get-tuple-element.51), channel_id=1, source_target_pairs={{16,0},{32,16},{48,32},{64,48},{80,64},{96,80},{112,96},{128,112},... | collective-permute-start | bytes 221192 | tf_op jit(solution)/shard_map/ppermute | solution.py:73
  11.9 8.2 %collective-permute-done.2 = bf16[9,16,256]{2,1,0:T(8,128)(2,1)S(1)} collective-permute-done((bf16[9,16,256]{2,1,0:T(8,128)(2,1)S(1)}, bf16[9,16,256]{2,1,0:T(8,128)(2,1)S(1)}, u32[]{:S(2)}, u32[]{:S(2)}) %collective-permute-start.2) | collective-permute-done | bytes 73760 | tf_op jit(solution)/shard_map/ppermute | solution.py:73
  20.1 1.6 fusion.20
  21.8 7.8 %all-to-all-start = ((bf16[8,144,128]{2,1,0:T(8,128)(2,1)}), bf16[8,144,128]{2,1,0:T(8,128)(2,1)S(1)}, u32[]{:S(2)}, u32[]{:S(2)}) async-start(bf16[8,144,128]{2,1,0:T(8,128)(2,1)} %fusion.20), calls=%async_computation | async-start | bytes 589824 | tf_op jit(solution)/shard_map/all_to_all | solution.py:88
  29.5 5.2 %collective-permute-start.3 = (bf16[27,16,256]{2,1,0:T(8,128)(2,1)S(1)}, bf16[27,16,256]{2,1,0:T(8,128)(2,1)S(1)}, u32[]{:S(2)}, u32[]{:S(2)}) collective-permute-start(bf16[27,16,256]{2,1,0:T(8,128)(2,1)S(1)} %copy-done.9), channel_id=1, source_target_pairs={{0,0},{1,1},{66,2},{67,3},{20,4},{21,5},{86,6},{87,7},{40,8},{41,9... | collective-permute-start | bytes 663560 | tf_op jit(solution)/shard_map/ppermute | solution.py:290
  34.8 3.3 %collective-permute-done.4.wb_ref = bf16[27,16,256]{2,1,0:T(8,128)(2,1)S(1)} collective-permute-done((bf16[27,16,256]{2,1,0:T(8,128)(2,1)S(1)}, bf16[27,16,256]{2,1,0:T(8,128)(2,1)S(1)}, u32[]{:S(2)}, u32[]{:S(2)}) %collective-permute-start.4) | collective-permute-done | bytes 221216 | tf_op jit(solution)/shard_map/ppermute | solution.py:291
  38.1 0.7 copy-done.5
  38.8 3.9 %collective-permute-done.3.wa_ref = bf16[27,16,256]{2,1,0:T(8,128)(2,1)S(1)} collective-permute-done((bf16[27,16,256]{2,1,0:T(8,128)(2,1)S(1)}, bf16[27,16,256]{2,1,0:T(8,128)(2,1)S(1)}, u32[]{:S(2)}, u32[]{:S(2)}) %collective-permute-start.3) | collective-permute-done | bytes 221216 | tf_op jit(solution)/shard_map/ppermute | solution.py:290
  42.7 0.7 copy-done.7
  43.4 0.9 copy-done.6
  44.4 0.9 copy-done.8
  45.3 3.1 %shard_map.91 = (f32[4,8,16,512]{3,2,1,0:T(8,128)S(1)}, f32[4,8,16,512]{3,2,1,0:T(8,128)}) custom-call(s32[3]{0:T(128)S(1)} %pad_add_fusion.at_ref, bf16[8,144,128]{2,1,0:T(8,128)(2,1)S(1)} %all-to-all-done.got_ref, bf16[27,16,256]{2,1,0:T(8,128)(2,1)S(1)} %copy-done.8, bf16[27,16,256]{2,1,0:T(8,128)(2,1)S(1)} %copy-done.6), custom_call_target="tpu_custom_call" | custom-call | tf_op jit(solution)/shard_map/pallas_call | solution.py:177
  48.4 3.0 %collective-permute-done.5 = f32[4,8,16,512]{3,2,1,0:T(8,128)} collective-permute-done((f32[4,8,16,512]{3,2,1,0:T(8,128)}, f32[4,8,16,512]{3,2,1,0:T(8,128)}, u32[]{:S(2)}, u32[]{:S(2)}) %collective-permute-start.5) | collective-permute-done | bytes 1048608 | tf_op jit(solution)/shard_map/ppermute | solution.py:277
  51.4 1.4 add.143
  52.8 1.3 fusion.90
  54.1 0.7 slice_bitcast_fusion.9
  54.7 4.2 %collective-permute-start.6 = (bf16[8,16,512]{2,1,0:T(8,128)(2,1)}, bf16[8,16,512]{2,1,0:T(8,128)(2,1)S(1)}, u32[]{:S(2)}, u32[]{:S(2)}) collective-permute-start(bf16[8,16,512]{2,1,0:T(8,128)(2,1)} %get-tuple-element.43), channel_id=1, source_target_pairs={{0,4},{2,6},{4,8},{6,10},{8,12},{10,14},{12,0},{14,2},{1,5},{3,7},... | collective-permute-start | bytes 393224 | tf_op jit(solution)/shard_map/ppermute | solution.py:282
  59.0 1.8 collective-permute-start.7
  60.7 4.6 %copy.36.w_hbm = bf16[27,512,64]{2,1,0:T(8,128)(2,1)} copy(bf16[27,512,64]{1,2,0:T(8,128)(2,1)} %param.14) | data formatting | bytes 3538944 | tf_op args[3]
  65.4 1.4 fusion.92
  66.8 2.0 %pad_add_fusion.1.at_ref = s32[3]{0:T(128)S(1)} fusion(s32[1]{0:T(128)} %bitcast.5, s32[1]{0:T(128)} %bitcast.4, s32[1]{0:T(128)} %bitcast.3), kind=kLoop, calls=%fused_computation.120 | loop fusion | flops 6 | bytes 24 | tf_op jit(solution)/shard_map/stack | solution.py:327
  68.8 5.1 %collective-permute-start.12 = (bf16[27,32,256]{2,1,0:T(8,128)(2,1)}, bf16[27,32,256]{2,1,0:T(8,128)(2,1)S(1)}, u32[]{:S(2)}, u32[]{:S(2)}) collective-permute-start(bf16[27,32,256]{2,1,0:T(8,128)(2,1)} %param.16), channel_id=1, source_target_pairs={{0,0},{1,1},{66,2},{67,3},{20,4},{21,5},{86,6},{87,7},{40,8},{41,9... | collective-permute-start | bytes 1327112 | tf_op jit(solution)/shard_map/ppermute | solution.py:296
  74.0 1.1 fusion.39
  75.2 0.5 fusion.79
  75.7 1.8 collective-permute-start.9
  77.4 0.1 collective-permute-start.16
  77.5 6.3 %collective-permute-done.9 = bf16[2,8,512]{2,1,0:T(8,128)(2,1)S(1)} collective-permute-done((bf16[2,8,512]{2,1,0:T(8,128)(2,1)S(1)}, bf16[2,8,512]{2,1,0:T(8,128)(2,1)S(1)}, u32[]{:S(2)}, u32[]{:S(2)}) %collective-permute-start.9) | collective-permute-done | bytes 16416 | tf_op jit(solution)/shard_map/ppermute | solution.py:307
  83.8 13.7 %all-gather = bf16[48,8,512]{2,1,0:T(8,128)(2,1)S(1)} all-gather(bf16[6,8,512]{2,1,0:T(8,128)(2,1)S(1)} %pad_maximum_fusion.3), channel_id=2, replica_groups=mesh['row'=16,'col'=8,'depth'=2] {'col'}, dimensions={0}, use_global_device_ids=true | all-gather | bytes 442368 | tf_op jit(solution)/shard_map/all_gather | solution.py:308
  97.6 0.1 maximum_select_fusion.slab_ref
  97.7 3.6 %mid_taps.1 = (bf16[5,64,64]{2,1,0:T(8,128)(2,1)S(1)}, f32[5,64,64]{2,1,0:T(8,128)S(1)}, bf16[5,64,64]{2,1,0:T(8,128)(2,1)S(1)}) custom-call(bf16[7,64,512]{2,1,0:T(8,128)(2,1)S(1)} %maximum_select_fusion.slab_ref, bf16[27,512,64]{2,1,0:T(8,128)(2,1)S(1)} %copy-done.1), custom_call_target="tpu_custom_call" | custom-call | tf_op jit(solution)/shard_map/mid_taps/pallas_call | solution.py:212
  101.3 4.1 %collective-permute-start.10 = (bf16[5,64,64]{2,1,0:T(8,128)(2,1)S(1)}, bf16[5,64,64]{2,1,0:T(8,128)(2,1)S(1)}, u32[]{:S(2)}, u32[]{:S(2)}) collective-permute-start(bf16[5,64,64]{2,1,0:T(8,128)(2,1)S(1)} %get-tuple-element.25), channel_id=1, source_target_pairs={{0,16},{16,32},{32,48},{48,64},{64,80},{80,96},{96,112},{112,128},... | collective-permute-start | bytes 122888 | tf_op jit(solution)/shard_map/ppermute | solution.py:72
  105.4 1.9 %collective-permute-start.11 = (bf16[5,64,64]{2,1,0:T(8,128)(2,1)S(1)}, bf16[5,64,64]{2,1,0:T(8,128)(2,1)S(1)}, u32[]{:S(2)}, u32[]{:S(2)}) collective-permute-start(bf16[5,64,64]{2,1,0:T(8,128)(2,1)S(1)} %get-tuple-element.26), channel_id=1, source_target_pairs={{16,0},{32,16},{48,32},{64,48},{80,64},{96,80},{112,96},{128,112},... | collective-permute-start | bytes 122888 | tf_op jit(solution)/shard_map/ppermute | solution.py:73
  107.4 7.6 %collective-permute-start.17 = (bf16[9,16,256]{2,1,0:T(8,128)(2,1)S(1)}, bf16[9,16,256]{2,1,0:T(8,128)(2,1)}, u32[]{:S(2)}, u32[]{:S(2)}) collective-permute-start(bf16[9,16,256]{2,1,0:T(8,128)(2,1)S(1)} %get-tuple-element.48), channel_id=1, source_target_pairs={{0,16},{16,32},{32,48},{48,64},{64,80},{80,96},{96,112},{112,128},... | collective-permute-start | bytes 221192 | tf_op jit(solution)/shard_map/ppermute | solution.py:72
  115.0 1.9 %collective-permute-start.18 = (bf16[9,16,256]{2,1,0:T(8,128)(2,1)S(1)}, bf16[9,16,256]{2,1,0:T(8,128)(2,1)}, u32[]{:S(2)}, u32[]{:S(2)}) collective-permute-start(bf16[9,16,256]{2,1,0:T(8,128)(2,1)S(1)} %get-tuple-element.49), channel_id=1, source_target_pairs={{16,0},{32,16},{48,32},{64,48},{80,64},{96,80},{112,96},{128,112},... | collective-permute-start | bytes 221192 | tf_op jit(solution)/shard_map/ppermute | solution.py:73
  117.1 0.1 copy.37
  117.2 0.1 all_gather_reshape.3
  117.4 7.2 %collective-permute-done.18 = bf16[9,16,256]{2,1,0:T(8,128)(2,1)} collective-permute-done((bf16[9,16,256]{2,1,0:T(8,128)(2,1)S(1)}, bf16[9,16,256]{2,1,0:T(8,128)(2,1)}, u32[]{:S(2)}, u32[]{:S(2)}) %collective-permute-start.18) | collective-permute-done | bytes 73760 | tf_op jit(solution)/shard_map/ppermute | solution.py:73
  124.5 2.5 %fusion.23 = bf16[8,144,128]{2,1,0:T(8,128)(2,1)} fusion(s32[8,128]{1,0:T(8,128)S(1)} %get-tuple-element.55, s32[4,256]{1,0:T(4,128)S(1)} %multiply_add_fusion, bf16[1,144,256]{2,1,0:T(8,128)(2,1)} %bitcast.41, bf16[2,144,256]{2,1,0:T(8,128)(2,1)S(1)} %bitcast.144, bf16[1,144,256]{2,1,0:T(8,128)(2,1)} %bitcast.38), kind=kOutput, calls=%fused_computation.17 | convolution fusion | flops 303480832 | bytes 598016 | tf_op jit(solution)/shard_map/prc,pcjk->jrk/dot_general | solution.py:87
  127.1 8.3 %all-to-all-start.1 = ((bf16[8,144,128]{2,1,0:T(8,128)(2,1)}), bf16[8,144,128]{2,1,0:T(8,128)(2,1)S(1)}, u32[]{:S(2)}, u32[]{:S(2)}) async-start(bf16[8,144,128]{2,1,0:T(8,128)(2,1)} %fusion.23), calls=%async_computation.1 | async-start | bytes 589824 | tf_op jit(solution)/shard_map/all_to_all | solution.py:88
  135.4 13.7 %all_gather.11.got_ref = bf16[8,3,64,128]{3,2,1,0:T(8,128)(2,1)S(1)} all-gather(bf16[1,3,64,128]{3,2,1,0:T(8,128)(2,1)S(1)} %all_gather_reshape.3), channel_id=1, replica_groups=mesh['row'=16,'col'=8,'depth'=2] {'col'}, dimensions={0}, use_global_device_ids=true | all-gather | bytes 442368 | tf_op jit(solution)/shard_map/all_gather | solution.py:325
  149.1 1.6 copy-done.2
  150.7 2.6 %lift_planes.1 = (bf16[12,128,128]{2,1,0:T(8,128)(2,1)S(1)}, bf16[3,128,128]{2,1,0:T(8,128)(2,1)}, bf16[3,128,128]{2,1,0:T(8,128)(2,1)}) custom-call(s32[3]{0:T(128)S(1)} %pad_add_fusion.1.at_ref, bf16[8,3,64,128]{3,2,1,0:T(8,128)(2,1)S(1)} %all_gather.11.got_ref, bf16[8,512,256]{2,1,0:T(8,128)(2,1)S(1)} %copy-done.2), custom_call_target="tpu_custom_call" | custom-call | tf_op jit(solution)/shard_map/lift_planes/pallas_call | solution.py:264
  153.3 0.7 copy-done.3
  154.1 1.9 %collective-permute-start.14 = (bf16[3,128,128]{2,1,0:T(8,128)(2,1)}, bf16[3,128,128]{2,1,0:T(8,128)(2,1)S(1)}, u32[]{:S(2)}, u32[]{:S(2)}) collective-permute-start(bf16[3,128,128]{2,1,0:T(8,128)(2,1)} %get-tuple-element.30), channel_id=1, source_target_pairs={{0,16},{16,32},{32,48},{48,64},{64,80},{80,96},{96,112},{112,128},... | collective-permute-start | bytes 294920 | tf_op jit(solution)/shard_map/ppermute | solution.py:72
  156.0 3.4 %collective-permute-start.15 = (bf16[3,128,128]{2,1,0:T(8,128)(2,1)}, bf16[3,128,128]{2,1,0:T(8,128)(2,1)S(1)}, u32[]{:S(2)}, u32[]{:S(2)}) collective-permute-start(bf16[3,128,128]{2,1,0:T(8,128)(2,1)} %get-tuple-element.31), channel_id=1, source_target_pairs={{16,0},{32,16},{48,32},{64,48},{80,64},{96,80},{112,96},{128,112},... | collective-permute-start | bytes 294920 | tf_op jit(solution)/shard_map/ppermute | solution.py:73
  159.4 2.1 %shard_map.92.part_ref = f32[1024,512]{1,0:T(8,128)S(1)} custom-call(s32[3]{0:T(128)S(1)} %pad_add_fusion.at_ref, bf16[8,144,128]{2,1,0:T(8,128)(2,1)S(1)} %all-to-all-done.1.got_ref, bf16[27,32,256]{2,1,0:T(8,128)(2,1)S(1)} %collective-permute-done.12.wa_ref, bf16[27,32,256]{2,1,0:T(8,128)(2,1)S(1)} %collective-permute-done.13.wb_ref), custom_call_target="tpu_custom_call" | custom-call | tf_op jit(solution)/shard_map/pallas_call | solution.py:177
  161.5 6.4 %collective-permute-done.15.hi_ref = bf16[3,128,128]{2,1,0:T(8,128)(2,1)S(1)} collective-permute-done((bf16[3,128,128]{2,1,0:T(8,128)(2,1)}, bf16[3,128,128]{2,1,0:T(8,128)(2,1)S(1)}, u32[]{:S(2)}, u32[]{:S(2)}) %collective-permute-start.15) | collective-permute-done | bytes 98336 | tf_op jit(solution)/shard_map/ppermute | solution.py:73
  167.9 2.4 %shard_map.93 = (f32[4,8,16,512]{3,2,1,0:T(8,128)S(1)}, f32[4,8,16,512]{3,2,1,0:T(8,128)S(1)}) custom-call(s32[3]{0:T(128)S(1)} %pad_add_fusion.at_ref, bf16[12,128,128]{2,1,0:T(8,128)(2,1)S(1)} %copy-done.4, bf16[3,128,128]{2,1,0:T(8,128)(2,1)S(1)} %collective-permute-done.14.lo_ref, bf16[3,128,128]{2,1,0:T(8,128)(2,1)S(1)} %collective-permute-done.15.hi_ref, ...), custom_call_target="tpu_custom_call" | custom-call | tf_op jit(solution)/shard_map/pallas_call | solution.py:177
  170.4 0.5 collective-permute-start.19
  170.9 2.3 %collective-permute-done.19 = f32[4,8,16,512]{3,2,1,0:T(8,128)S(1)} collective-permute-done((f32[4,8,16,512]{3,2,1,0:T(8,128)S(1)}, f32[4,8,16,512]{3,2,1,0:T(8,128)S(1)}, u32[]{:S(2)}, u32[]{:S(2)}) %collective-permute-start.19) | collective-permute-done | bytes 1048608 | tf_op jit(solution)/shard_map/ppermute | solution.py:277
  173.2 0.2 add.158
  173.4 0.3 fusion.88
  173.7 0.7 collective-permute-start.20
  174.5 2.4 %collective-permute-start.22 = (bf16[8,16,512]{2,1,0:T(8,128)(2,1)S(1)}, bf16[8,16,512]{2,1,0:T(8,128)(2,1)S(1)}, u32[]{:S(2)}, u32[]{:S(2)}) collective-permute-start(bf16[8,16,512]{2,1,0:T(8,128)(2,1)S(1)} %get-tuple-element.41), channel_id=1, source_target_pairs={{0,8},{2,10},{4,12},{6,14},{8,0},{10,2},{12,4},{14,6},{1,9},{3,11}... | collective-permute-start | bytes 393224 | tf_op jit(solution)/shard_map/ppermute | solution.py:282
  176.9 0.8 collective-permute-start.21
  177.7 0.8 collective-permute-done.20
  178.5 1.9 %collective-permute-done.22 = bf16[8,16,512]{2,1,0:T(8,128)(2,1)S(1)} collective-permute-done((bf16[8,16,512]{2,1,0:T(8,128)(2,1)S(1)}, bf16[8,16,512]{2,1,0:T(8,128)(2,1)S(1)}, u32[]{:S(2)}, u32[]{:S(2)}) %collective-permute-start.22) | collective-permute-done | bytes 131104 | tf_op jit(solution)/shard_map/ppermute | solution.py:282
  180.4 3.6 %collective-permute-done.21 = bf16[8,16,512]{2,1,0:T(8,128)(2,1)S(1)} collective-permute-done((bf16[8,16,512]{2,1,0:T(8,128)(2,1)S(1)}, bf16[8,16,512]{2,1,0:T(8,128)(2,1)S(1)}, u32[]{:S(2)}, u32[]{:S(2)}) %collective-permute-start.21) | collective-permute-done | bytes 131104 | tf_op jit(solution)/shard_map/ppermute | solution.py:282
  184.0 0.1 fusion.47
  184.2 0.7 copy.60
  (62 shorter events, 1.1 us)
Async XLA Ops:
  0.0 75.2 %copy-start = (bf16[8,256,512]{2,1,0:T(8,128)(2,1)S(1)}, bf16[8,256,512]{2,1,0:T(8,128)(2,1)}, u32[]{:S(2)}) copy-start(bf16[8,256,512]{2,1,0:T(8,128)(2,1)} %param.13) | copy-start | bytes 6291460
  1.1 2.9 %collective-permute-start = (bf16[2,16,256]{2,1,0:T(8,128)(2,1)S(1)}, bf16[2,16,256]{2,1,0:T(8,128)(2,1)S(1)}, u32[]{:S(2)}, u32[]{:S(2)}) collective-permute-start(bf16[2,16,256]{2,1,0:T(8,128)(2,1)S(1)} %fusion.83), channel_id=1, source_target_pairs={{0,1},{1,0},{2,3},{3,2},{4,5},{5,4},{6,7},{7,6},{8,9},{9,8},{10,11... | collective-permute-start | bytes 49160 | tf_op jit(solution)/shard_map/ppermute | solution.py:68
  4.0 25.6 %copy-start.9 = (bf16[27,16,256]{2,1,0:T(8,128)(2,1)S(1)}, bf16[27,16,256]{2,1,0:T(8,128)(2,1)}, u32[]{:S(2)}) copy-start(bf16[27,16,256]{2,1,0:T(8,128)(2,1)} %param.12) | copy-start | bytes 663556
  4.0 7.9 %collective-permute-start.1 = (bf16[9,16,256]{2,1,0:T(8,128)(2,1)S(1)}, bf16[9,16,256]{2,1,0:T(8,128)(2,1)S(1)}, u32[]{:S(2)}, u32[]{:S(2)}) collective-permute-start(bf16[9,16,256]{2,1,0:T(8,128)(2,1)S(1)} %get-tuple-element.50), channel_id=1, source_target_pairs={{0,16},{16,32},{32,48},{48,64},{64,80},{80,96},{96,112},{112,128},... | collective-permute-start | bytes 221192 | tf_op jit(solution)/shard_map/ppermute | solution.py:72
  10.0 10.1 %collective-permute-start.2 = (bf16[9,16,256]{2,1,0:T(8,128)(2,1)S(1)}, bf16[9,16,256]{2,1,0:T(8,128)(2,1)S(1)}, u32[]{:S(2)}, u32[]{:S(2)}) collective-permute-start(bf16[9,16,256]{2,1,0:T(8,128)(2,1)S(1)} %get-tuple-element.51), channel_id=1, source_target_pairs={{16,0},{32,16},{48,32},{64,48},{80,64},{96,80},{112,96},{128,112},... | collective-permute-start | bytes 221192 | tf_op jit(solution)/shard_map/ppermute | solution.py:73
  21.8 21.7 %all-to-all-start = ((bf16[8,144,128]{2,1,0:T(8,128)(2,1)}), bf16[8,144,128]{2,1,0:T(8,128)(2,1)S(1)}, u32[]{:S(2)}, u32[]{:S(2)}) async-start(bf16[8,144,128]{2,1,0:T(8,128)(2,1)} %fusion.20), calls=%async_computation | async-start | bytes 589824 | tf_op jit(solution)/shard_map/all_to_all | solution.py:88
  29.5 8.6 %collective-permute-start.4 = (bf16[27,16,256]{2,1,0:T(8,128)(2,1)S(1)}, bf16[27,16,256]{2,1,0:T(8,128)(2,1)S(1)}, u32[]{:S(2)}, u32[]{:S(2)}) collective-permute-start(bf16[27,16,256]{2,1,0:T(8,128)(2,1)S(1)} %copy-done.9), channel_id=1, source_target_pairs={{129,0},{128,1},{194,2},{195,3},{181,4},{180,5},{246,6},{247,7},{1... | collective-permute-start | bytes 663560 | tf_op jit(solution)/shard_map/ppermute | solution.py:291
  29.5 13.2 %collective-permute-start.3 = (bf16[27,16,256]{2,1,0:T(8,128)(2,1)S(1)}, bf16[27,16,256]{2,1,0:T(8,128)(2,1)S(1)}, u32[]{:S(2)}, u32[]{:S(2)}) collective-permute-start(bf16[27,16,256]{2,1,0:T(8,128)(2,1)S(1)} %copy-done.9), channel_id=1, source_target_pairs={{0,0},{1,1},{66,2},{67,3},{20,4},{21,5},{86,6},{87,7},{40,8},{41,9... | collective-permute-start | bytes 663560 | tf_op jit(solution)/shard_map/ppermute | solution.py:290
  38.1 0.7 copy-start.5
  42.7 0.7 copy-start.7
  43.4 0.9 copy-start.6
  44.4 0.9 copy-start.8
  48.4 3.0 %collective-permute-start.5 = (f32[4,8,16,512]{3,2,1,0:T(8,128)}, f32[4,8,16,512]{3,2,1,0:T(8,128)}, u32[]{:S(2)}, u32[]{:S(2)}) collective-permute-start(f32[4,8,16,512]{3,2,1,0:T(8,128)} %get-tuple-element.23), channel_id=1, source_target_pairs={{0,2},{2,0},{4,6},{6,4},{8,10},{10,8},{12,14},{14,12},{1,3},{3,1},... | collective-permute-start | bytes 3145736 | tf_op jit(solution)/shard_map/ppermute | solution.py:277
  54.7 19.2 %collective-permute-start.6 = (bf16[8,16,512]{2,1,0:T(8,128)(2,1)}, bf16[8,16,512]{2,1,0:T(8,128)(2,1)S(1)}, u32[]{:S(2)}, u32[]{:S(2)}) collective-permute-start(bf16[8,16,512]{2,1,0:T(8,128)(2,1)} %get-tuple-element.43), channel_id=1, source_target_pairs={{0,4},{2,6},{4,8},{6,10},{8,12},{10,14},{12,0},{14,2},{1,5},{3,7},... | collective-permute-start | bytes 393224 | tf_op jit(solution)/shard_map/ppermute | solution.py:282
  59.0 15.0 %collective-permute-start.8 = (bf16[8,16,512]{2,1,0:T(8,128)(2,1)S(1)}, bf16[8,16,512]{2,1,0:T(8,128)(2,1)S(1)}, u32[]{:S(2)}, u32[]{:S(2)}) collective-permute-start(bf16[8,16,512]{2,1,0:T(8,128)(2,1)S(1)} %get-tuple-element.44), channel_id=1, source_target_pairs={{0,8},{2,10},{4,12},{6,14},{8,0},{10,2},{12,4},{14,6},{1,9},{3,11}... | collective-permute-start | bytes 393224 | tf_op jit(solution)/shard_map/ppermute | solution.py:282
  59.0 15.0 %collective-permute-start.7 = (bf16[8,16,512]{2,1,0:T(8,128)(2,1)S(1)}, bf16[8,16,512]{2,1,0:T(8,128)(2,1)}, u32[]{:S(2)}, u32[]{:S(2)}) collective-permute-start(bf16[8,16,512]{2,1,0:T(8,128)(2,1)S(1)} %get-tuple-element.45), channel_id=1, source_target_pairs={{0,12},{2,14},{4,0},{6,2},{8,4},{10,6},{12,8},{14,10},{1,13},{3,15... | collective-permute-start | bytes 393224 | tf_op jit(solution)/shard_map/ppermute | solution.py:282
  68.8 48.3 %collective-permute-start.13 = (bf16[27,32,256]{2,1,0:T(8,128)(2,1)}, bf16[27,32,256]{2,1,0:T(8,128)(2,1)S(1)}, u32[]{:S(2)}, u32[]{:S(2)}) collective-permute-start(bf16[27,32,256]{2,1,0:T(8,128)(2,1)} %param.16), channel_id=1, source_target_pairs={{129,0},{128,1},{194,2},{195,3},{181,4},{180,5},{246,6},{247,7},{1... | collective-permute-start | bytes 1327112 | tf_op jit(solution)/shard_map/ppermute | solution.py:297
  68.8 48.3 %collective-permute-start.12 = (bf16[27,32,256]{2,1,0:T(8,128)(2,1)}, bf16[27,32,256]{2,1,0:T(8,128)(2,1)S(1)}, u32[]{:S(2)}, u32[]{:S(2)}) collective-permute-start(bf16[27,32,256]{2,1,0:T(8,128)(2,1)} %param.16), channel_id=1, source_target_pairs={{0,0},{1,1},{66,2},{67,3},{20,4},{21,5},{86,6},{87,7},{40,8},{41,9... | collective-permute-start | bytes 1327112 | tf_op jit(solution)/shard_map/ppermute | solution.py:296
  75.2 22.6 %copy-start.1 = (bf16[27,512,64]{2,1,0:T(8,128)(2,1)S(1)}, bf16[27,512,64]{2,1,0:T(8,128)(2,1)}, u32[]{:S(2)}) copy-start(bf16[27,512,64]{2,1,0:T(8,128)(2,1)} %copy.36.w_hbm) | copy-start | bytes 5308420
  75.7 8.2 %collective-permute-start.9 = (bf16[2,8,512]{2,1,0:T(8,128)(2,1)S(1)}, bf16[2,8,512]{2,1,0:T(8,128)(2,1)S(1)}, u32[]{:S(2)}, u32[]{:S(2)}) collective-permute-start(bf16[2,8,512]{2,1,0:T(8,128)(2,1)S(1)} %slice_select_fusion.1), channel_id=1, source_target_pairs={{0,1},{1,0},{2,3},{3,2},{4,5},{5,4},{6,7},{7,6},{8,9},{9,8},{10,11... | collective-permute-start | bytes 49160 | tf_op jit(solution)/shard_map/ppermute | solution.py:307
  77.4 29.9 %collective-permute-start.16 = (bf16[2,16,256]{2,1,0:T(8,128)(2,1)S(1)}, bf16[2,16,256]{2,1,0:T(8,128)(2,1)S(1)}, u32[]{:S(2)}, u32[]{:S(2)}) collective-permute-start(bf16[2,16,256]{2,1,0:T(8,128)(2,1)S(1)} %fusion.82), channel_id=1, source_target_pairs={{0,1},{1,0},{2,3},{3,2},{4,5},{5,4},{6,7},{7,6},{8,9},{9,8},{10,11... | collective-permute-start | bytes 49160 | tf_op jit(solution)/shard_map/ppermute | solution.py:68
  101.3 13.7 %collective-permute-start.10 = (bf16[5,64,64]{2,1,0:T(8,128)(2,1)S(1)}, bf16[5,64,64]{2,1,0:T(8,128)(2,1)S(1)}, u32[]{:S(2)}, u32[]{:S(2)}) collective-permute-start(bf16[5,64,64]{2,1,0:T(8,128)(2,1)S(1)} %get-tuple-element.25), channel_id=1, source_target_pairs={{0,16},{16,32},{32,48},{48,64},{64,80},{80,96},{96,112},{112,128},... | collective-permute-start | bytes 122888 | tf_op jit(solution)/shard_map/ppermute | solution.py:72
  105.4 11.5 %collective-permute-start.11 = (bf16[5,64,64]{2,1,0:T(8,128)(2,1)S(1)}, bf16[5,64,64]{2,1,0:T(8,128)(2,1)S(1)}, u32[]{:S(2)}, u32[]{:S(2)}) collective-permute-start(bf16[5,64,64]{2,1,0:T(8,128)(2,1)S(1)} %get-tuple-element.26), channel_id=1, source_target_pairs={{16,0},{32,16},{48,32},{64,48},{80,64},{96,80},{112,96},{128,112},... | collective-permute-start | bytes 122888 | tf_op jit(solution)/shard_map/ppermute | solution.py:73
  107.4 9.9 %collective-permute-start.17 = (bf16[9,16,256]{2,1,0:T(8,128)(2,1)S(1)}, bf16[9,16,256]{2,1,0:T(8,128)(2,1)}, u32[]{:S(2)}, u32[]{:S(2)}) collective-permute-start(bf16[9,16,256]{2,1,0:T(8,128)(2,1)S(1)} %get-tuple-element.48), channel_id=1, source_target_pairs={{0,16},{16,32},{32,48},{48,64},{64,80},{80,96},{96,112},{112,128},... | collective-permute-start | bytes 221192 | tf_op jit(solution)/shard_map/ppermute | solution.py:72
  115.0 9.5 %collective-permute-start.18 = (bf16[9,16,256]{2,1,0:T(8,128)(2,1)S(1)}, bf16[9,16,256]{2,1,0:T(8,128)(2,1)}, u32[]{:S(2)}, u32[]{:S(2)}) collective-permute-start(bf16[9,16,256]{2,1,0:T(8,128)(2,1)S(1)} %get-tuple-element.49), channel_id=1, source_target_pairs={{16,0},{32,16},{48,32},{64,48},{80,64},{96,80},{112,96},{128,112},... | collective-permute-start | bytes 221192 | tf_op jit(solution)/shard_map/ppermute | solution.py:73
  127.1 32.3 %all-to-all-start.1 = ((bf16[8,144,128]{2,1,0:T(8,128)(2,1)}), bf16[8,144,128]{2,1,0:T(8,128)(2,1)S(1)}, u32[]{:S(2)}, u32[]{:S(2)}) async-start(bf16[8,144,128]{2,1,0:T(8,128)(2,1)} %fusion.23), calls=%async_computation.1 | async-start | bytes 589824 | tf_op jit(solution)/shard_map/all_to_all | solution.py:88
  149.1 1.6 copy-start.2
  153.3 0.7 copy-start.3
  154.1 7.4 %collective-permute-start.14 = (bf16[3,128,128]{2,1,0:T(8,128)(2,1)}, bf16[3,128,128]{2,1,0:T(8,128)(2,1)S(1)}, u32[]{:S(2)}, u32[]{:S(2)}) collective-permute-start(bf16[3,128,128]{2,1,0:T(8,128)(2,1)} %get-tuple-element.30), channel_id=1, source_target_pairs={{0,16},{16,32},{32,48},{48,64},{64,80},{80,96},{96,112},{112,128},... | collective-permute-start | bytes 294920 | tf_op jit(solution)/shard_map/ppermute | solution.py:72
  156.0 11.9 %collective-permute-start.15 = (bf16[3,128,128]{2,1,0:T(8,128)(2,1)}, bf16[3,128,128]{2,1,0:T(8,128)(2,1)S(1)}, u32[]{:S(2)}, u32[]{:S(2)}) collective-permute-start(bf16[3,128,128]{2,1,0:T(8,128)(2,1)} %get-tuple-element.31), channel_id=1, source_target_pairs={{16,0},{32,16},{48,32},{64,48},{80,64},{96,80},{112,96},{128,112},... | collective-permute-start | bytes 294920 | tf_op jit(solution)/shard_map/ppermute | solution.py:73
  159.4 8.6 %copy-start.4 = (bf16[12,128,128]{2,1,0:T(8,128)(2,1)S(1)}, bf16[12,128,128]{2,1,0:T(8,128)(2,1)}, u32[]{:S(2)}) copy-start(bf16[12,128,128]{2,1,0:T(8,128)(2,1)} %copy-done.3) | copy-start | bytes 1179652
  170.4 2.8 %collective-permute-start.19 = (f32[4,8,16,512]{3,2,1,0:T(8,128)S(1)}, f32[4,8,16,512]{3,2,1,0:T(8,128)S(1)}, u32[]{:S(2)}, u32[]{:S(2)}) collective-permute-start(f32[4,8,16,512]{3,2,1,0:T(8,128)S(1)} %get-tuple-element.35), channel_id=1, source_target_pairs={{0,2},{2,0},{4,6},{6,4},{8,10},{10,8},{12,14},{14,12},{1,3},{3,1},... | collective-permute-start | bytes 3145736 | tf_op jit(solution)/shard_map/ppermute | solution.py:277
  173.7 4.8 %collective-permute-start.20 = (bf16[8,16,512]{2,1,0:T(8,128)(2,1)S(1)}, bf16[8,16,512]{2,1,0:T(8,128)(2,1)S(1)}, u32[]{:S(2)}, u32[]{:S(2)}) collective-permute-start(bf16[8,16,512]{2,1,0:T(8,128)(2,1)S(1)} %get-tuple-element.40), channel_id=1, source_target_pairs={{0,4},{2,6},{4,8},{6,10},{8,12},{10,14},{12,0},{14,2},{1,5},{3,7},... | collective-permute-start | bytes 393224 | tf_op jit(solution)/shard_map/ppermute | solution.py:282
  174.5 5.9 %collective-permute-start.22 = (bf16[8,16,512]{2,1,0:T(8,128)(2,1)S(1)}, bf16[8,16,512]{2,1,0:T(8,128)(2,1)S(1)}, u32[]{:S(2)}, u32[]{:S(2)}) collective-permute-start(bf16[8,16,512]{2,1,0:T(8,128)(2,1)S(1)} %get-tuple-element.41), channel_id=1, source_target_pairs={{0,8},{2,10},{4,12},{6,14},{8,0},{10,2},{12,4},{14,6},{1,9},{3,11}... | collective-permute-start | bytes 393224 | tf_op jit(solution)/shard_map/ppermute | solution.py:282
  176.9 7.1 %collective-permute-start.21 = (bf16[8,16,512]{2,1,0:T(8,128)(2,1)S(1)}, bf16[8,16,512]{2,1,0:T(8,128)(2,1)S(1)}, u32[]{:S(2)}, u32[]{:S(2)}) collective-permute-start(bf16[8,16,512]{2,1,0:T(8,128)(2,1)S(1)} %get-tuple-element.42), channel_id=1, source_target_pairs={{0,12},{2,14},{4,0},{6,2},{8,4},{10,6},{12,8},{14,10},{1,13},{3,15... | collective-permute-start | bytes 393224 | tf_op jit(solution)/shard_map/ppermute | solution.py:282
